TPU v7x, 128 devices: a whole 4x4x4 slice. The times are simulated.
128 devices in a mesh: clus: 32 (over x, y, core), lab: 4 (over z).
Axes of the slice: x: 4, y: 4, z: 4, core: 2. Of those that a mesh axis runs over, the one named last changes fastest.
Arguments:
- queries: bfloat16 [16384, 768], P(('clus', 'lab')), may hold values from -6 to 6
- visits: int32 [16384, 4], P(('clus', 'lab')), may hold values from 0 to 63, all different within a row; in each aligned block of 128 rows (0 to 127, 128 to 255, ...) at most 16 rows name the same one
- positives: int32 [16384, 4], P(('clus', 'lab')), may hold values from 0 to 4095
- weights: bfloat16 [64, 4096, 768], P('clus', 'lab'), may hold values from -0.21875 to 0.21875
- momentum: float32 [64, 4096, 768], P('clus', 'lab'), may hold values from -24 to 24
Outputs:
- query_grad: float32 [16384, 768], P(('clus', 'lab'))
- weights_new: bfloat16 [64, 4096, 768], P('clus', 'lab')
- momentum_new: float32 [64, 4096, 768], P('clus', 'lab')
Inputs may be any that keep to these rules, and one draw needn't show every extreme that they name: `visits`: each query names 4 different clusters; among the 128 queries of one device at most 16 visit any one cluster.
All inputs are finite; a program needn't handle non-finite values.
Results may differ from a plain program's by a relative error of at most 0.006.
Values may be sent and summed in bfloat16 or wider, within the bound.
No kernel may reach another device: no remote copies, remote signals or barrier semaphores. Data moves between devices by JAX's collectives and lax.ppermute only.
A program may use at most 128 MiB of HBM per device.

v0:
```python
import jax
import jax.numpy as jnp
from jax import lax
from jax.sharding import PartitionSpec as P

momentum_decay = 0.9
step_rate = 0.002


def in_blocks(x, dim, peers):
    before, after = (x.shape[:dim], x.shape[dim + 1 :])
    return jnp.moveaxis(x.reshape(*before, peers, -1, *after), dim, 0)


def piece_ends(length, count):
    unit = 8 if length >= 8 * count else 1
    return [length // unit * k // count * unit for k in range(1, count)]


def joined_along(pieces, dim):
    pieces = jnp.moveaxis(pieces, 0, dim)
    dims = pieces.shape
    return pieces.reshape(*dims[:dim], dims[dim] * dims[dim + 1], *dims[dim + 2 :])


def exchange_in_pieces(x, axis, pieces, split_dim, concat_dim):
    blocks = in_blocks(x, split_dim, lax.axis_size(axis))
    cut = max(range(1, max(2, blocks.ndim - 1)), key=lambda d: blocks.shape[d])
    done = []
    for share in jnp.split(blocks, piece_ends(blocks.shape[cut], pieces), axis=cut):
        if share.size:
            done.append(lax.all_to_all(share, axis, split_axis=0, concat_axis=0, tiled=True))
    return joined_along(jnp.concatenate(done, axis=cut), concat_dim)


def shards(queries, visits, positives, weights, momentum):
    n_clus = lax.axis_size("clus")
    n_lab = lax.axis_size("lab")
    q_count, width = queries.shape
    visit_count = visits.shape[1]
    clus_local, block_size, _ = weights.shape
    all_clusters = clus_local * n_clus
    capacity = 2 * q_count * visit_count // all_clusters
    flat_visits = visits.reshape(-1)
    one_hot = (flat_visits[:, None] == jnp.arange(all_clusters, dtype=jnp.int32)[None, :]).astype(
        jnp.int32
    )
    before = jnp.cumsum(one_hot, axis=0) - one_hot
    ranks = jnp.sum(before * one_hot, axis=1)
    slots = flat_visits * capacity + ranks
    repeated = jnp.repeat(queries, visit_count, axis=0)
    outbox = jnp.zeros((all_clusters * capacity, width), jnp.bfloat16).at[slots].set(repeated)
    outbox = outbox.reshape(all_clusters, capacity, width)
    out_tags = (
        jnp.full((all_clusters * capacity,), -1, jnp.int32).at[slots].set(positives.reshape(-1))
    )
    out_tags = out_tags.reshape(all_clusters, capacity)
    wide_box = jnp.broadcast_to(
        outbox.reshape(n_clus, 1, clus_local, capacity, width),
        (n_clus, n_lab, clus_local, capacity, width),
    )
    wide_box = wide_box.reshape(n_clus * n_lab * clus_local, capacity, width)
    wide_tags = jnp.broadcast_to(
        out_tags.reshape(n_clus, 1, clus_local, capacity), (n_clus, n_lab, clus_local, capacity)
    )
    wide_tags = wide_tags.reshape(n_clus * n_lab * clus_local, capacity)
    arrived, label_tag = (
        lax.all_to_all(wide_box, ("clus", "lab"), split_axis=0, concat_axis=1, tiled=True),
        lax.all_to_all(wide_tags, ("clus", "lab"), split_axis=0, concat_axis=1, tiled=True),
    )
    offsets = lax.axis_index("lab") * block_size + jnp.arange(block_size, dtype=jnp.int32)
    logits = jnp.einsum("crd,cbd->crb", arrived, weights, preferred_element_type=jnp.float32)
    target = (label_tag[:, :, None] == offsets[None, None, :]).astype(jnp.float32)
    live = label_tag >= 0
    grad = jnp.where(live[:, :, None], jax.nn.sigmoid(logits) - target, 0.0).astype(jnp.bfloat16)
    partial_grad = jnp.einsum("crb,cbd->crd", grad, weights, preferred_element_type=jnp.float32)
    label_grad = jnp.einsum("crb,crd->cbd", grad, arrived, preferred_element_type=jnp.float32)
    homed = exchange_in_pieces(partial_grad.astype(jnp.bfloat16), ("clus", "lab"), 2, 1, 0).astype(
        partial_grad.dtype
    )
    homed = jnp.sum(homed.reshape(n_clus, n_lab, clus_local, capacity, width), axis=1)
    homed = homed.reshape(all_clusters * capacity, width)
    query_grad = jnp.sum(homed[slots].reshape(q_count, visit_count, width), axis=1)
    momentum_new = momentum_decay * momentum + label_grad
    weights_new = (weights.astype(jnp.float32) - step_rate * momentum_new).astype(jnp.bfloat16)
    return (query_grad, weights_new, momentum_new)


def solution(mesh):
    in_specs = (
        P(("clus", "lab"), None),
        P(("clus", "lab"), None),
        P(("clus", "lab"), None),
        P("clus", "lab", None),
        P("clus", "lab", None),
    )
    out_specs = (P(("clus", "lab"), None), P("clus", "lab", None), P("clus", "lab", None))
    return jax.shard_map(shards, mesh=mesh, in_specs=in_specs, out_specs=out_specs, check_vma=False)
```

profile of v0, /device:TPU:1, one launch (start us, length us, event | category | flops | bytes accessed | tf_op | source)
XLA Modules:
  0.0 249.9 jit_solution(1994159719770943331)
XLA Ops:
  0.6 0.7 broadcast_multiply_fusion
  1.3 0.8 copy.18
  2.3 0.1 copy.17
  2.5 0.8 copy.21
  3.5 1.2 reduce-window.6
  4.7 0.2 slice_reduce_fusion
  4.9 0.1 fusion.4
  5.1 2.4 scatter_custom_fusion
  7.6 0.7 broadcast_in_dim.44
  8.3 11.5 %all-to-all-start = ((s32[128,2,16]{2,1,0:T(2,128)}), s32[128,2,16]{2,1,0:T(2,128)S(1)}, u32[]{:S(2)}, u32[]{:S(2)}) async-start(s32[128,2,16]{2,1,0:T(2,128)} %bitcast.3), calls=%async_computation | async-start | bytes 262144 | tf_op jit(solution)/shard_map/all_to_all | solution.py:69
  19.8 1.1 broadcast_in_dim.47
  21.0 0.2 reshape.121
  21.1 3.0 %scatter_custom_fusion.1 = bf16[1024,768]{1,0:T(8,128)(2,1)S(1)} fusion(s32[512]{0:T(512)S(1)} %bitcast.55, bf16[512,768]{1,0:T(8,128)(2,1)S(1)} %reshape.121, bf16[]{:T(256)} %constant.4.clone.1), kind=kCustom, calls=%fused_computation.10 | custom fusion | bytes 1572866 | tf_op jit(solution)/shard_map/scatter | solution.py:52
  24.1 5.6 %all-to-all-done = s32[128,2,16]{2,1,0:T(2,128)S(1)} async-done(((s32[128,2,16]{2,1,0:T(2,128)}), s32[128,2,16]{2,1,0:T(2,128)S(1)}, u32[]{:S(2)}, u32[]{:S(2)}) %all-to-all-start) | async-done | bytes 16416 | tf_op jit(solution)/shard_map/all_to_all | solution.py:69
  29.7 3.5 %broadcast_in_dim.49 = bf16[32,4,2,16,768]{4,3,2,1,0:T(8,128)(2,1)} broadcast(bf16[32,2,16,768]{3,2,1,0:T(8,128)(2,1)S(1)} %bitcast.51), dimensions={0,2,3,4} | broadcast | bytes 7864320 | tf_op jit(solution)/shard_map/broadcast_in_dim | solution.py:58
  33.2 5.0 %all-to-all-start.1 = ((bf16[256,16,768]{2,1,0:T(8,128)(2,1)}), bf16[256,16,768]{2,1,0:T(8,128)(2,1)}, u32[]{:S(2)}, u32[]{:S(2)}) async-start(bf16[256,16,768]{2,1,0:T(8,128)(2,1)} %bitcast.47), calls=%async_computation.1 | async-start | bytes 12582912 | tf_op jit(solution)/shard_map/all_to_all | solution.py:68
  38.2 0.1 all_to_all.36
  38.3 76.4 %all-to-all-done.1 = bf16[256,16,768]{2,1,0:T(8,128)(2,1)} async-done(((bf16[256,16,768]{2,1,0:T(8,128)(2,1)}), bf16[256,16,768]{2,1,0:T(8,128)(2,1)}, u32[]{:S(2)}, u32[]{:S(2)}) %all-to-all-start.1) | async-done | bytes 6291488 | tf_op jit(solution)/shard_map/all_to_all | solution.py:68
  114.7 3.4 %copy.23 = bf16[2,128,16,768]{3,2,1,0:T(8,128)(2,1)S(1)} copy(bf16[2,128,16,768]{3,2,0,1:T(8,128)(2,1)} %bitcast.8) | data formatting | bytes 12582912 | tf_op jit(solution)/shard_map/all_to_all | solution.py:68
  118.2 0.3 copy-done.1
  118.4 10.6 %select_convert_fusion = bf16[2,2048,1024]{2,1,0:T(8,128)(2,1)S(1)} fusion(s32[1024]{0:T(1024)S(1)} %iota_add_fusion, s32[2,2048]{1,0:T(2,128)S(1)} %all_to_all.36, pred[2,2048]{1,0:T(4,128)(4,1)S(1)} %broadcast_compare_fusion, bf16[2,2048,768]{2,1,0:T(8,128)(2,1)S(1)} %bitcast.48, bf16[2,1024,768]{2,1,0:T(8,128)(2,1)S(1)} %copy-done.1), kind=kOutput, calls=%fused_computation.3 | convolution fusion | flops 6476005376 | bytes 17850368 | tf_op jit(solution)/shard_map/crd,cbd->crb/dot_general | solution.py:72
  129.1 7.7 %convolution_convert_fusion = bf16[2,2048,768]{2,1,0:T(8,128)(2,1)S(1)} fusion(bf16[2,2048,1024]{2,1,0:T(8,128)(2,1)S(1)} %select_convert_fusion, bf16[2,1024,768]{2,1,0:T(8,128)(2,1)S(1)} %copy-done.1), kind=kOutput, calls=%fused_computation.9 | convolution fusion | flops 6445596672 | bytes 17825792 | tf_op jit(solution)/shard_map/crb,cbd->crd/dot_general | solution.py:76
  136.9 1.0 copy.33
  137.8 2.1 fusion.8
  139.9 52.2 %all_to_all.47 = bf16[128,2,8,768]{3,2,1,0:T(8,128)(2,1)} all-to-all(bf16[128,2,8,768]{3,2,1,0:T(8,128)(2,1)S(1)} %get-tuple-element.3), channel_id=1, replica_groups=mesh['clus'=32,'lab'=4] {'clus','lab'}, dimensions={0} | all-to-all | bytes 6291456 | tf_op jit(solution)/shard_map/all_to_all | solution.py:32
  192.2 4.8 %all-to-all-start.3 = ((bf16[128,2,8,768]{3,2,1,0:T(8,128)(2,1)}), bf16[128,2,8,768]{3,2,1,0:T(8,128)(2,1)}, u32[]{:S(2)}, u32[]{:S(2)}) async-start(bf16[128,2,8,768]{3,2,1,0:T(8,128)(2,1)} %get-tuple-element.4), calls=%async_computation.3 | async-start | bytes 6291456 | tf_op jit(solution)/shard_map/all_to_all | solution.py:32
  197.0 15.4 %subtract_convert_fusion = (bf16[2,1024,768]{2,1,0:T(8,128)(2,1)}, f32[2,1024,768]{2,1,0:T(8,128)}) fusion(bf16[2,1024,768]{2,1,0:T(8,128)(2,1)} %param.8, bf16[2,2048,1024]{2,1,0:T(8,128)(2,1)} %copy-done.2, bf16[2,2048,768]{2,1,0:T(8,128)(2,1)} %bitcast.49, f32[2,1024,768]{2,1,0:T(8,128)} %param.9), kind=kOutput, calls=%fused_computation.7 | convolution fusion | flops 6451888128 | bytes 33554432 | tf_op jit(solution)/shard_map/crb,crd->cbd/dot_general | solution.py:77
  212.4 26.4 %all-to-all-done.3 = bf16[128,2,8,768]{3,2,1,0:T(8,128)(2,1)} async-done(((bf16[128,2,8,768]{3,2,1,0:T(8,128)(2,1)}), bf16[128,2,8,768]{3,2,1,0:T(8,128)(2,1)}, u32[]{:S(2)}, u32[]{:S(2)}) %all-to-all-start.3) | async-done | bytes 3145760 | tf_op jit(solution)/shard_map/all_to_all | solution.py:32
  238.8 4.9 %convert_reduce_fusion = f32[32,2,16,768]{3,2,1,0:T(8,128)S(1)} fusion(bf16[128,2,8,768]{3,2,1,0:T(8,128)(2,1)} %all-to-all-done.3, bf16[128,2,8,768]{3,2,1,0:T(8,128)(2,1)} %all_to_all.47), kind=kLoop, calls=%fused_computation.4 | loop fusion | flops 18087936 | bytes 9437184 | tf_op jit(solution)/shard_map/reduce_sum | solution.py:81
  243.7 2.6 %gather_fusion = f32[512,768]{1,0:T(8,128)} fusion(f32[1024,768]{1,0:T(8,128)S(1)} %bitcast.45, s32[1024]{0:T(1024)S(1)} %pad_clamp_fusion), kind=kCustom, calls=%fused_computation | custom fusion | bytes 3147776 | tf_op jit(solution)/shard_map/gather | solution.py:83
  246.3 1.8 reshape.99
  248.1 1.8 reduce_sum.32
  (18 shorter events, 0.6 us)
Async XLA Ops:
  8.3 21.4 %all-to-all-start = ((s32[128,2,16]{2,1,0:T(2,128)}), s32[128,2,16]{2,1,0:T(2,128)S(1)}, u32[]{:S(2)}, u32[]{:S(2)}) async-start(s32[128,2,16]{2,1,0:T(2,128)} %bitcast.3), calls=%async_computation | async-start | bytes 262144 | tf_op jit(solution)/shard_map/all_to_all | solution.py:69
  33.2 81.5 %all-to-all-start.1 = ((bf16[256,16,768]{2,1,0:T(8,128)(2,1)}), bf16[256,16,768]{2,1,0:T(8,128)(2,1)}, u32[]{:S(2)}, u32[]{:S(2)}) async-start(bf16[256,16,768]{2,1,0:T(8,128)(2,1)} %bitcast.47), calls=%async_computation.1 | async-start | bytes 12582912 | tf_op jit(solution)/shard_map/all_to_all | solution.py:68
  114.7 3.7 %copy-start.1 = (bf16[2,1024,768]{2,1,0:T(8,128)(2,1)S(1)}, bf16[2,1024,768]{2,1,0:T(8,128)(2,1)}, u32[]{:S(2)}) copy-start(bf16[2,1024,768]{2,1,0:T(8,128)(2,1)} %param.8) | copy-start | bytes 9437188
  118.2 10.9 %copy-start = (bf16[2,128,16,768]{3,2,1,0:T(8,128)(2,1)}, bf16[2,128,16,768]{3,2,1,0:T(8,128)(2,1)S(1)}, u32[]{:S(2)}) copy-start(bf16[2,128,16,768]{3,2,1,0:T(8,128)(2,1)S(1)} %copy.23) | copy-start | bytes 18874372
  129.1 7.8 %copy-start.2 = (bf16[2,2048,1024]{2,1,0:T(8,128)(2,1)}, bf16[2,2048,1024]{2,1,0:T(8,128)(2,1)S(1)}, u32[]{:S(2)}) copy-start(bf16[2,2048,1024]{2,1,0:T(8,128)(2,1)S(1)} %select_convert_fusion) | copy-start | bytes 25165828
  192.2 46.7 %all-to-all-start.3 = ((bf16[128,2,8,768]{3,2,1,0:T(8,128)(2,1)}), bf16[128,2,8,768]{3,2,1,0:T(8,128)(2,1)}, u32[]{:S(2)}, u32[]{:S(2)}) async-start(bf16[128,2,8,768]{3,2,1,0:T(8,128)(2,1)} %get-tuple-element.4), calls=%async_computation.3 | async-start | bytes 6291456 | tf_op jit(solution)/shard_map/all_to_all | solution.py:32
where the time goes:
time: 250 us
  waiting for transfers between devices  108 us (43%)
  blocking collectives  52.2 us (21%)
  matrix products  33.8 us (14%)
  local copies, waits for them, and re-layouts  24.6 us (10%)
  starting transfers between devices  21.2 us (8%)
  other arithmetic  8.75 us (4%)
    all_to_all x1, waiting for transfers between devices, shards(): lax.all_to_all(wide_box, ('clus', 'lab'), split_axis=0, concat_axis=1, ti...  76.4 us
    all_to_all x1, blocking collectives, exchange_in_pieces(): lax.all_to_all(share, axis, split_axis=0, concat_axis=0, tiled=True)  52.2 us
    all_to_all x1, waiting for transfers between devices, exchange_in_pieces(): lax.all_to_all(share, axis, split_axis=0, concat_axis=0, tiled=True)  26.4 us
    dot_general x1, matrix products, shards(): jnp.einsum('crb,crd->cbd', grad, arrived, preferred_element_type=jnp.floa...  15.4 us
    all_to_all x1, starting transfers between devices, shards(): lax.all_to_all(wide_tags, ('clus', 'lab'), split_axis=0, concat_axis=1, t...  11.5 us
    dot_general x1, matrix products, shards(): jnp.einsum('crd,cbd->crb', arrived, weights, preferred_element_type=jnp.f...  10.6 us
    dot_general x1, matrix products, shards(): jnp.einsum('crb,cbd->crd', grad, weights, preferred_element_type=jnp.floa...  7.74 us
    all_to_all x1, waiting for transfers between devices, shards(): lax.all_to_all(wide_tags, ('clus', 'lab'), split_axis=0, concat_axis=1, t...  5.55 us
  transfers between devices with their start and end apart: 3, of which 3 were waited for; matrix products, arithmetic and copies ran while one was open for 8% of the time, Pallas kernels for 0%

commit v1 on v0

v1 whole, which is shorter than its diff:
```python
import jax
import jax.numpy as jnp
from jax import lax
from jax.experimental import pallas as pl
from jax.experimental.pallas import tpu as pltpu
from jax.sharding import PartitionSpec as P

momentum_decay = 0.9
step_rate = 0.002

CLUS = 32
LAB = 4
CAP = 16
NQ = 128
VISITS = 4
D = 768
EXTRA = 8
TAGS = 128
LABELS = 1024
BAND = 256
ROWS = CLUS * CAP


def ring(shift):
    return [(i, (i + shift) % LAB) for i in range(LAB)]


def picks(visits_t, parity):
    dest = lax.broadcasted_iota(jnp.int32, (CLUS, NQ), 0) * 2 + parity
    hit = visits_t[0:1, :] == dest
    for k in range(1, VISITS):
        hit = hit | (visits_t[k : k + 1, :] == dest)
    before = lax.broadcasted_iota(jnp.int32, (NQ, NQ), 0) < lax.broadcasted_iota(
        jnp.int32, (NQ, NQ), 1
    )
    rank = jnp.dot(
        hit.astype(jnp.float32).astype(jnp.bfloat16),
        before.astype(jnp.float32).astype(jnp.bfloat16),
        preferred_element_type=jnp.float32,
    )
    place = jnp.where(hit, rank, -1.0).astype(jnp.int32)
    slot = lax.broadcasted_iota(jnp.int32, (CLUS, CAP, NQ), 1)
    return (place[:, None, :] == slot).reshape(ROWS, NQ)


def as_bf16(flags):
    return flags.astype(jnp.float32).astype(jnp.bfloat16)


def labels_of(visits_t, positives_t, parity):
    dest = lax.broadcasted_iota(jnp.int32, (CLUS, NQ), 0) * 2 + parity
    label = jnp.zeros((CLUS, NQ), jnp.int32)
    for k in range(VISITS):
        label = label + jnp.where(visits_t[k : k + 1, :] == dest, positives_t[k : k + 1, :] + 1, 0)
    return label


def slot_labels(chosen, label):
    wide = jnp.broadcast_to(label[:, None, :], (CLUS, CAP, NQ)).reshape(ROWS, NQ)
    return jnp.sum(jnp.where(chosen, wide, 0), axis=1, keepdims=True) - 1


def own_kernel(visits_ref, positives_ref, queries_ref, box_ref, raw_ref):
    bf = jnp.bfloat16
    visits_t, positives_t = visits_ref[...], positives_ref[...]
    lane = lax.broadcasted_iota(jnp.int32, (ROWS, TAGS), 1)
    notes = jnp.zeros((ROWS, TAGS), jnp.float32)
    for parity in range(2):
        chosen = picks(visits_t, parity)
        label = slot_labels(chosen, labels_of(visits_t, positives_t, parity))
        high = label >> 6
        low = label & 63
        notes = jnp.where(lane == 2 * parity, high.astype(jnp.float32), notes)
        notes = jnp.where(lane == 2 * parity + 1, low.astype(jnp.float32), notes)
        if parity == 0:
            filled = jnp.dot(as_bf16(chosen), queries_ref[...], preferred_element_type=jnp.float32)
            box_ref[:, :D] = filled.astype(bf)
    box_ref[:, D:] = notes.astype(bf)
    raw_ref[:NQ] = queries_ref[...]
    values = visits_t.astype(jnp.float32)
    parts = [values[k : k + 1, :] for k in range(VISITS)]
    row = jnp.concatenate(parts + [jnp.zeros((1, D - VISITS * NQ), jnp.float32)], axis=1)
    raw_ref[NQ:] = jnp.concatenate([row, jnp.zeros((EXTRA - 1, D), jnp.float32)], axis=0).astype(bf)


def all_kernel(order_ref, raw_ref, box_ref):
    for k in range(LAB):
        s = order_ref[k]
        extra = raw_ref[s, NQ:].astype(jnp.float32)
        parts = [extra[0:1, j * NQ : (j + 1) * NQ] for j in range(VISITS)]
        visits_t = jnp.concatenate(parts, axis=0).astype(jnp.int32)
        filled = jnp.dot(
            as_bf16(picks(visits_t, 1)), raw_ref[s, :NQ], preferred_element_type=jnp.float32
        )
        box_ref[:, k] = filled.astype(jnp.bfloat16).reshape(CLUS, CAP, D)


def home_kernel(visits_ref, first_ref, second_ref, out_ref):
    total = jnp.zeros((NQ, D), jnp.float32)
    for parity, ref in ((0, first_ref), (1, second_ref)):
        chosen = as_bf16(picks(visits_ref[...], parity))
        total = total + lax.dot_general(
            chosen, ref[...], (((0,), (0,)), ((), ())), preferred_element_type=jnp.float32
        )
    out_ref[...] = total


def update_kernel(ga_ref, gb_ref, ra_ref, rb_ref, w_ref, m_ref, wo_ref, mo_ref):
    def apply(grad_ref, rows_ref):
        label_grad = lax.dot_general(
            grad_ref[...], rows_ref[...], (((0,), (0,)), ((), ())), preferred_element_type=jnp.float32
        )
        fresh = momentum_decay * m_ref[0] + label_grad
        mo_ref[0] = fresh
        wo_ref[0] = (w_ref[0].astype(jnp.float32) - step_rate * fresh).astype(jnp.bfloat16)

    @pl.when(pl.program_id(0) == 0)
    def _():
        apply(ga_ref, ra_ref)

    @pl.when(pl.program_id(0) == 1)
    def _():
        apply(gb_ref, rb_ref)


def update(grad_a, grad_b, rows_a, rows_b, weights, momentum):
    bands = LABELS // BAND
    n = LAB * ROWS
    whole = pl.BlockSpec((n, D), lambda c, b: (0, 0))
    band = pl.BlockSpec((1, BAND, D), lambda c, b: (c, b, 0))
    return pl.pallas_call(
        update_kernel,
        grid=(2, bands),
        in_specs=[
            pl.BlockSpec((n, BAND), lambda c, b: (0, b * (1 - c) + (bands - 1) * c)),
            pl.BlockSpec((n, BAND), lambda c, b: (0, b * c)),
            whole,
            whole,
            band,
            band,
        ],
        out_specs=(band, band),
        out_shape=(
            jax.ShapeDtypeStruct(weights.shape, weights.dtype),
            jax.ShapeDtypeStruct(momentum.shape, momentum.dtype),
        ),
        compiler_params=pltpu.CompilerParams(
            dimension_semantics=("arbitrary", "arbitrary"), vmem_limit_bytes=40 << 20
        ),
        cost_estimate=pl.CostEstimate(
            flops=2 * 2 * n * LABELS * D, bytes_accessed=36 << 20, transcendentals=0
        ),
        name="update",
    )(grad_a, grad_b, rows_a, rows_b, weights, momentum)


def grads(rows, tag, weights, offsets):
    logits = jnp.einsum("rd,bd->rb", rows, weights, preferred_element_type=jnp.float32)
    target = (tag == offsets[None, :]).astype(jnp.float32)
    grad = (jax.nn.sigmoid(logits) - target).astype(jnp.bfloat16)
    part = jnp.einsum("rb,bd->rd", grad, weights, preferred_element_type=jnp.float32)
    return grad, part.astype(jnp.bfloat16)


def swap(x):
    return lax.all_to_all(x, "clus", split_axis=0, concat_axis=0, tiled=True)


def add(*terms):
    total = terms[0].astype(jnp.float32)
    for term in terms[1:]:
        total = total + term.astype(jnp.float32)
    return total.astype(jnp.bfloat16)


def scatter_sum(own, low, high, far):
    half = own.shape[0] // 2
    up = lax.ppermute(far[:half], "lab", ring(1))
    down = lax.ppermute(far[half:], "lab", ring(-1))
    up = jnp.concatenate([add(high[:half], up), high[half:]])
    down = jnp.concatenate([low[:half], add(low[half:], down)])
    up = lax.ppermute(up, "lab", ring(1))
    down = lax.ppermute(down, "lab", ring(-1))
    return add(own, up, down)


def shards(queries, visits, positives, weights, momentum):
    vt, pt = visits.T, positives.T
    bf = jnp.bfloat16
    me = lax.axis_index("lab")
    order = (me + jnp.array([0, 3, 1, 2], jnp.int32)) & 3

    box_a, raw = pl.pallas_call(
        own_kernel,
        out_shape=(
            jax.ShapeDtypeStruct((ROWS, D + TAGS), bf),
            jax.ShapeDtypeStruct((NQ + EXTRA, D), bf),
        ),
        name="own_box",
    )(vt, pt, queries)
    got_a = swap(box_a.reshape(CLUS, CAP, D + TAGS)).reshape(ROWS, D + TAGS)
    peers = lax.all_gather(raw, "lab", axis=0, tiled=False)
    box_b = pl.pallas_call(
        all_kernel,
        in_specs=[pl.BlockSpec(memory_space=pltpu.SMEM), pl.BlockSpec(memory_space=pltpu.VMEM)],
        out_shape=jax.ShapeDtypeStruct((CLUS, LAB, CAP, D), bf),
        name="all_box",
    )(order, peers)
    got_a, box_b = lax.optimization_barrier((got_a, box_b))
    got_b = swap(box_b.reshape(CLUS, LAB * CAP, D)).reshape(LAB * ROWS, D)

    half = ROWS // 2
    from_low = lax.ppermute(got_a, "lab", ring(1))
    from_high = lax.ppermute(got_a, "lab", ring(-1))
    far_low = lax.ppermute(from_low[:half], "lab", ring(1))
    far_high = lax.ppermute(from_high[half:], "lab", ring(-1))
    pieces = (got_a, from_low, from_high, far_low, far_high)
    rows_a = jnp.concatenate([p[:, :D] for p in pieces])
    notes = jnp.concatenate([p[:, D : D + 4] for p in pieces]).astype(jnp.int32)
    tag_a = notes[:, 0:1] * 64 + notes[:, 1:2]
    tag_b = notes[:, 2:3] * 64 + notes[:, 3:4]
    tag_b = jnp.moveaxis(tag_b.reshape(LAB, CLUS, CAP), 0, 1).reshape(LAB * ROWS, 1)

    offsets = me * LABELS + jnp.arange(LABELS, dtype=jnp.int32)
    grad_a, part_a = grads(rows_a, tag_a, weights[0], offsets)
    part_a = part_a.reshape(LAB, ROWS, D)
    home_a = scatter_sum(part_a[0], part_a[1], part_a[2], part_a[3])
    grad_b, part_b = grads(got_b, tag_b, weights[1], offsets)
    part_b = part_b.reshape(CLUS, LAB, CAP, D)
    home_b = scatter_sum(*[part_b[:, k].reshape(ROWS, D) for k in range(LAB)])
    home_a = swap(home_a.reshape(CLUS, CAP, D)).reshape(ROWS, D)
    home_b = swap(home_b.reshape(CLUS, CAP, D)).reshape(ROWS, D)
    weights_new, momentum_new = update(grad_a, grad_b, rows_a, got_b, weights, momentum)
    query_grad = pl.pallas_call(
        home_kernel, out_shape=jax.ShapeDtypeStruct((NQ, D), jnp.float32), name="home_sum"
    )(vt, home_a, home_b)
    return (query_grad, weights_new, momentum_new)


def solution(mesh):
    in_specs = (
        P(("clus", "lab"), None),
        P(("clus", "lab"), None),
        P(("clus", "lab"), None),
        P("clus", "lab", None),
        P("clus", "lab", None),
    )
    out_specs = (P(("clus", "lab"), None), P("clus", "lab", None), P("clus", "lab", None))
    return jax.shard_map(shards, mesh=mesh, in_specs=in_specs, out_specs=out_specs, check_vma=False)
```

time: 250 us -> 188 us (0.75)
  waiting for transfers between devices: 108 us -> 32.5 us
  blocking collectives: 52.2 us -> 15.5 us
  starting transfers between devices: 21.2 us -> 56.3 us
  Pallas kernels: 0 us -> 23.1 us
  matrix products: 33.8 us -> 20.1 us
  local copies, waits for them, and re-layouts: 24.6 us -> 29.7 us
    all_to_all x3 -> x4, waiting for transfers between devices: 108 us -> 10.5 us  [swap(): return lax.all_to_all(x, 'clus', split_axis=0, concat_axis=0, tiled=True)]
    all_to_all x1 -> x0, blocking collectives: 52.2 us -> none  [exchange_in_pieces(): lax.all_to_all(share, axis, split_axis=0, concat_axis=0, tiled=True)]
    pallas_call x0 -> x4, Pallas kernels: none -> 23.1 us  [the longest x1 13.7 us: update(): pl.pallas_call(update_kernel, grid=(2, bands), in_specs=[pl.BlockSpec((n,...]
    ppermute x0 -> x12, waiting for transfers between devices: none -> 22 us  [the longest x2 8.54 us: scatter_sum(): up = lax.ppermute(up, 'lab', ring(1))]
    all_to_all x3 -> x4, starting transfers between devices: 21.2 us -> 40.6 us  [swap(): return lax.all_to_all(x, 'clus', split_axis=0, concat_axis=0, tiled=True)]
    unnamed x8 -> x32, local copies, waits for them, and re-layouts: 1.85 us -> 18.1 us
    ppermute x0 -> x12, starting transfers between devices: none -> 15.7 us  [the longest x2 6.08 us: scatter_sum(): down = lax.ppermute(far[half:], 'lab', ring(-1))]
    all_gather x0 -> x1, blocking collectives: none -> 15.5 us  [shards(): peers = lax.all_gather(raw, 'lab', axis=0, tiled=False)]
  transfers between devices with their start and end apart: 3 -> 16, of which waited for: 3 -> 8; matrix products, arithmetic and copies ran while one was open for 8% -> 26% of each run, Pallas kernels for 0% -> 10%
where the time goes in v1:
time: 188 us; the launch traced here: 187 us
  starting transfers between devices  56.3 us (30%)
  waiting for transfers between devices  32.5 us (17%)
  local copies, waits for them, and re-layouts  29.7 us (16%)
  Pallas kernels  23.1 us (12%)
  matrix products  20.1 us (11%)
  blocking collectives  15.5 us (8%)
  other arithmetic  8.45 us (4%)
    all_to_all x4, starting transfers between devices, swap(): return lax.all_to_all(x, 'clus', split_axis=0, concat_axis=0, tiled=True)  40.6 us
    unnamed x32, local copies, waits for them, and re-layouts  18.1 us
    all_gather x1, blocking collectives, shards(): peers = lax.all_gather(raw, 'lab', axis=0, tiled=False)  15.5 us
    pallas_call x1, Pallas kernels, update(): pl.pallas_call(update_kernel, grid=(2, bands), in_specs=[pl.BlockSpec((n,...  13.7 us
    dot_general x2, matrix products, grads(): jnp.einsum('rd,bd->rb', rows, weights, preferred_element_type=jnp.float32)  12.8 us
    all_to_all x4, waiting for transfers between devices, swap(): return lax.all_to_all(x, 'clus', split_axis=0, concat_axis=0, tiled=True)  10.5 us
    ppermute x2, waiting for transfers between devices, scatter_sum(): up = lax.ppermute(up, 'lab', ring(1))  8.54 us
    dot_general x2, matrix products, grads(): jnp.einsum('rb,bd->rd', grad, weights, preferred_element_type=jnp.float32)  7.23 us
  transfers between devices with their start and end apart: 16, of which 8 were waited for; matrix products, arithmetic and copies ran while one was open for 26% of the time, Pallas kernels for 10%

profile of v1, /device:TPU:1, one launch (start us, length us, event | category | flops | bytes accessed | tf_op | source)
XLA Modules:
  0.0 186.7 jit_solution(10476009809165139364)
XLA Ops:
  0.6 2.6 %own_box.1 = (bf16[512,896]{1,0:T(8,128)(2,1)}, bf16[136,768]{1,0:T(8,128)(2,1)}) custom-call(s32[4,128]{1,0:T(4,128)} %bitcast.55, s32[4,128]{1,0:T(4,128)} %bitcast.58, bf16[128,768]{1,0:T(8,128)(2,1)} %queries_ref.1), custom_call_target="tpu_custom_call" | custom-call | tf_op jit(solution)/shard_map/own_box/pallas_call | solution.py:193
  3.2 8.6 %all-to-all-start = ((bf16[32,16,896]{2,1,0:T(8,128)(2,1)}), bf16[32,16,896]{2,1,0:T(8,128)(2,1)}, u32[]{:S(2)}, u32[]{:S(2)}) async-start(bf16[32,16,896]{2,1,0:T(8,128)(2,1)} %bitcast.51), calls=%async_computation | async-start | bytes 1835008 | tf_op jit(solution)/shard_map/all_to_all | solution.py:166
  13.0 15.5 %all-gather = bf16[544,768]{1,0:T(8,128)(2,1)} all-gather(bf16[136,768]{1,0:T(8,128)(2,1)} %get-tuple-element.10), channel_id=2, replica_groups=mesh['clus'=32,'lab'=4] {'lab'}, dimensions={0}, use_global_device_ids=true | all-gather | bytes 1044480 | tf_op jit(solution)/shard_map/all_gather | solution.py:202
  28.6 4.1 %all_box.1 = bf16[32,4,16,768]{3,2,1,0:T(8,128)(2,1)} custom-call(s32[4]{0:T(128)} %add_and_fusion.order_ref, bf16[4,136,768]{2,1,0:T(8,128)(2,1)} %bitcast.44), custom_call_target="tpu_custom_call" | custom-call | tf_op jit(solution)/shard_map/all_box/pallas_call | solution.py:203
  32.7 2.7 %collective-permute-start.1 = (bf16[512,896]{1,0:T(8,128)(2,1)}, bf16[512,896]{1,0:T(8,128)(2,1)}, u32[]{:S(2)}, u32[]{:S(2)}) collective-permute-start(bf16[512,896]{1,0:T(8,128)(2,1)} %bitcast.3), channel_id=1, source_target_pairs={{0,3},{1,0},{2,1},{3,2},{4,7},{5,4},{6,5},{7,6},{8,11},{9,8},{10,9... | collective-permute-start | bytes 2752520 | tf_op jit(solution)/shard_map/ppermute | solution.py:214
  36.4 10.0 %all-to-all-start.2 = ((bf16[32,64,768]{2,1,0:T(8,128)(2,1)}), bf16[32,64,768]{2,1,0:T(8,128)(2,1)S(1)}, u32[]{:S(2)}, u32[]{:S(2)}) async-start(bf16[32,64,768]{2,1,0:T(8,128)(2,1)} %bitcast.43), calls=%async_computation.2 | async-start | bytes 6291456 | tf_op jit(solution)/shard_map/all_to_all | solution.py:166
  46.4 2.1 %slice_dynamic-update-slice_fusion.2 = bf16[2048,768]{1,0:T(8,128)(2,1)} fusion(bf16[512,896]{1,0:T(8,128)(2,1)} %bitcast.3), kind=kLoop, calls=%fused_computation.28 | loop fusion | bytes 1572864
  48.5 5.5 %collective-permute-done = bf16[512,896]{1,0:T(8,128)(2,1)} collective-permute-done((bf16[512,896]{1,0:T(8,128)(2,1)}, bf16[512,896]{1,0:T(8,128)(2,1)}, u32[]{:S(2)}, u32[]{:S(2)}) %collective-permute-start) | collective-permute-done | bytes 917536 | tf_op jit(solution)/shard_map/ppermute | solution.py:213
  57.2 1.8 slice.175
  59.0 2.7 %collective-permute-start.3 = (bf16[256,896]{1,0:T(8,128)(2,1)}, bf16[256,896]{1,0:T(8,128)(2,1)}, u32[]{:S(2)}, u32[]{:S(2)}) collective-permute-start(bf16[256,896]{1,0:T(8,128)(2,1)} %slice.175), channel_id=1, source_target_pairs={{0,3},{1,0},{2,1},{3,2},{4,7},{5,4},{6,5},{7,6},{8,11},{9,8},{10,9... | collective-permute-start | bytes 1376264 | tf_op jit(solution)/shard_map/ppermute | solution.py:216
  61.7 2.1 %slice_dynamic-update-slice_fusion.1 = bf16[2048,768]{1,0:T(8,128)(2,1)} fusion(bf16[2048,768]{1,0:T(8,128)(2,1)} %slice_dynamic-update-slice_fusion.2, bf16[512,896]{1,0:T(8,128)(2,1)} %collective-permute-done), kind=kLoop, calls=%fused_computation.17 | loop fusion | bytes 1572864
  63.8 2.1 %slice_dynamic-update-slice_fusion = bf16[2048,768]{1,0:T(8,128)(2,1)} fusion(bf16[2048,768]{1,0:T(8,128)(2,1)} %slice_dynamic-update-slice_fusion.1, bf16[512,896]{1,0:T(8,128)(2,1)} %collective-permute-done.1), kind=kLoop, calls=%fused_computation.16 | loop fusion | bytes 1572864
  73.4 6.7 %subtract_convert_fusion.1.ga_ref = bf16[2048,1024]{1,0:T(8,128)(2,1)S(1)} fusion(bf16[2048,768]{1,0:T(8,128)(2,1)} %slice_dynamic-update-slice_fusion.3.ra_ref, s32[1024]{0:T(1024)S(1)} %iota_add_fusion, s32[2048]{0:T(1024)S(1)} %bitcast.57, bf16[2,1024,768]{2,1,0:T(8,128)(2,1)} %w_ref.1), kind=kOutput, calls=%fused_computation.1 | convolution fusion | flops 3235905536 | bytes 8925184 | tf_op jit(solution)/shard_map/rd,bd->rb/dot_general | solution.py:158
  80.1 3.6 %convolution_convert_fusion.1 = bf16[2048,768]{1,0:T(8,128)(2,1)S(1)} fusion(bf16[2048,1024]{1,0:T(8,128)(2,1)S(1)} %subtract_convert_fusion.1.ga_ref, bf16[2,1024,768]{2,1,0:T(8,128)(2,1)S(1)} %copy-done.3), kind=kOutput, calls=%fused_computation.3 | convolution fusion | flops 3222798336 | bytes 8912896 | tf_op jit(solution)/shard_map/rb,bd->rd/dot_general | solution.py:161
  85.9 3.4 %collective-permute-start.6 = (bf16[256,768]{1,0:T(8,128)(2,1)}, bf16[256,768]{1,0:T(8,128)(2,1)}, u32[]{:S(2)}, u32[]{:S(2)}) collective-permute-start(bf16[256,768]{1,0:T(8,128)(2,1)} %get-tuple-element.24), channel_id=1, source_target_pairs={{0,3},{1,0},{2,1},{3,2},{4,7},{5,4},{6,5},{7,6},{8,11},{9,8},{10,9... | collective-permute-start | bytes 1179656 | tf_op jit(solution)/shard_map/ppermute | solution.py:179
  89.3 6.1 %subtract_convert_fusion.gb_ref = bf16[2048,1024]{1,0:T(8,128)(2,1)S(1)} fusion(bf16[2048,768]{1,0:T(8,128)(2,1)S(1)} %bitcast.41, s32[1024]{0:T(1024)S(1)} %iota_add_fusion, s32[2048]{0:T(1024)S(1)} %eq.32, bf16[2,1024,768]{2,1,0:T(8,128)(2,1)} %w_ref.1), kind=kOutput, calls=%fused_computation | convolution fusion | flops 3235905536 | bytes 8925184 | tf_op jit(solution)/shard_map/rd,bd->rb/dot_general | solution.py:158
  95.4 3.6 %convolution_convert_fusion = bf16[2048,768]{1,0:T(8,128)(2,1)S(1)} fusion(bf16[2048,1024]{1,0:T(8,128)(2,1)S(1)} %subtract_convert_fusion.gb_ref, bf16[2,1024,768]{2,1,0:T(8,128)(2,1)S(1)} %copy-done.4), kind=kOutput, calls=%fused_computation.2 | convolution fusion | flops 3222798336 | bytes 8912896 | tf_op jit(solution)/shard_map/rb,bd->rd/dot_general | solution.py:161
  99.4 2.7 %copy-done.9 = bf16[2048,768]{1,0:T(8,128)(2,1)S(1)} copy-done((bf16[2048,768]{1,0:T(8,128)(2,1)S(1)}, bf16[2048,768]{1,0:T(8,128)(2,1)}, u32[]{:S(2)}) %copy-start.9) | copy-done | bytes 3145752
  103.6 2.7 %collective-permute-start.10 = (bf16[256,768]{1,0:T(8,128)(2,1)S(1)}, bf16[256,768]{1,0:T(8,128)(2,1)S(1)}, u32[]{:S(2)}, u32[]{:S(2)}) collective-permute-start(bf16[256,768]{1,0:T(8,128)(2,1)S(1)} %bitcast.52), channel_id=1, source_target_pairs={{0,3},{1,0},{2,1},{3,2},{4,7},{5,4},{6,5},{7,6},{8,11},{9,8},{10,9... | collective-permute-start | bytes 1179656 | tf_op jit(solution)/shard_map/ppermute | solution.py:179
  108.9 2.1 %collective-permute-done.10 = bf16[256,768]{1,0:T(8,128)(2,1)S(1)} collective-permute-done((bf16[256,768]{1,0:T(8,128)(2,1)S(1)}, bf16[256,768]{1,0:T(8,128)(2,1)S(1)}, u32[]{:S(2)}, u32[]{:S(2)}) %collective-permute-start.10) | collective-permute-done | bytes 393248 | tf_op jit(solution)/shard_map/ppermute | solution.py:179
  112.0 3.1 %collective-permute-start.11 = (bf16[512,768]{1,0:T(8,128)(2,1)}, bf16[512,768]{1,0:T(8,128)(2,1)}, u32[]{:S(2)}, u32[]{:S(2)}) collective-permute-start(bf16[512,768]{1,0:T(8,128)(2,1)} %pad_maximum_fusion.3), channel_id=1, source_target_pairs={{0,3},{1,0},{2,1},{3,2},{4,7},{5,4},{6,5},{7,6},{8,11},{9,8},{10,9... | collective-permute-start | bytes 2359304 | tf_op jit(solution)/shard_map/ppermute | solution.py:183
  115.1 8.5 %collective-permute-done.5 = bf16[512,768]{1,0:T(8,128)(2,1)S(1)} collective-permute-done((bf16[512,768]{1,0:T(8,128)(2,1)S(1)}, bf16[512,768]{1,0:T(8,128)(2,1)S(1)}, u32[]{:S(2)}, u32[]{:S(2)}) %collective-permute-start.5) | collective-permute-done | bytes 786464 | tf_op jit(solution)/shard_map/ppermute | solution.py:182
  123.7 3.1 %collective-permute-done.7 = bf16[512,768]{1,0:T(8,128)(2,1)S(1)} collective-permute-done((bf16[512,768]{1,0:T(8,128)(2,1)S(1)}, bf16[512,768]{1,0:T(8,128)(2,1)S(1)}, u32[]{:S(2)}, u32[]{:S(2)}) %collective-permute-start.7) | collective-permute-done | bytes 786464 | tf_op jit(solution)/shard_map/ppermute | solution.py:183
  128.0 17.6 %all-to-all-start.1 = ((bf16[32,16,768]{2,1,0:T(8,128)(2,1)}), bf16[32,16,768]{2,1,0:T(8,128)(2,1)}, u32[]{:S(2)}, u32[]{:S(2)}) async-start(bf16[32,16,768]{2,1,0:T(8,128)(2,1)} %bitcast.47), calls=%async_computation.1 | async-start | bytes 1572864 | tf_op jit(solution)/shard_map/all_to_all | solution.py:166
  146.8 2.5 %fusion.1 = bf16[512,768]{1,0:T(8,128)(2,1)} fusion(bf16[512,768]{1,0:T(8,128)(2,1)} %collective-permute-done.11, bf16[512,768]{1,0:T(8,128)(2,1)} %collective-permute-done.9, bf16[32,1,16,768]{3,2,1,0:T(8,128)(2,1)S(1)} %slice.192), kind=kLoop, calls=%fused_computation.6 | loop fusion | flops 2359296 | bytes 3145728 | tf_op jit(solution)/shard_map/convert_element_type | solution.py:173
  149.4 10.5 %all-to-all-done.1 = bf16[32,16,768]{2,1,0:T(8,128)(2,1)} async-done(((bf16[32,16,768]{2,1,0:T(8,128)(2,1)}), bf16[32,16,768]{2,1,0:T(8,128)(2,1)}, u32[]{:S(2)}, u32[]{:S(2)}) %all-to-all-start.1) | async-done | bytes 786464 | tf_op jit(solution)/shard_map/all_to_all | solution.py:166
  159.9 4.4 %all-to-all-start.3 = ((bf16[32,16,768]{2,1,0:T(8,128)(2,1)}), bf16[32,16,768]{2,1,0:T(8,128)(2,1)}, u32[]{:S(2)}, u32[]{:S(2)}) async-start(bf16[32,16,768]{2,1,0:T(8,128)(2,1)} %bitcast.48), calls=%async_computation.3 | async-start | bytes 1572864 | tf_op jit(solution)/shard_map/all_to_all | solution.py:166
  164.3 1.9 %copy-done = bf16[2048,768]{1,0:T(8,128)(2,1)S(1)} copy-done((bf16[2048,768]{1,0:T(8,128)(2,1)S(1)}, bf16[2048,768]{1,0:T(8,128)(2,1)}, u32[]{:S(2)}) %copy-start) | copy-done | bytes 3145752
  166.2 2.2 %copy-done.2 = bf16[2048,1024]{1,0:T(8,128)(2,1)S(1)} copy-done((bf16[2048,1024]{1,0:T(8,128)(2,1)S(1)}, bf16[2048,1024]{1,0:T(8,128)(2,1)}, u32[]{:S(2)}) %copy-start.2) | copy-done | bytes 4194328
  168.4 1.9 %copy-done.5 = bf16[2,1024,768]{2,1,0:T(8,128)(2,1)S(1)} copy-done((bf16[2,1024,768]{2,1,0:T(8,128)(2,1)S(1)}, bf16[2,1024,768]{2,1,0:T(8,128)(2,1)}, u32[]{:S(2)}) %copy-start.5) | copy-done | bytes 3145752
  170.3 13.7 %update.1 = (bf16[2,1024,768]{2,1,0:T(8,128)(2,1)}, f32[2,1024,768]{2,1,0:T(8,128)}) custom-call(bf16[2048,1024]{1,0:T(8,128)(2,1)S(1)} %copy-done.2, bf16[2048,1024]{1,0:T(8,128)(2,1)} %copy-done.6, bf16[2048,768]{1,0:T(8,128)(2,1)S(1)} %copy-done, bf16[2048,768]{1,0:T(8,128)(2,1)S(1)} %bitcast.42, bf16[2,1024,768]{2,1,0:T(8,128)(2,1)S(1)} %copy-done.5, ...), custom_call_target="tpu_custom_call" | custom-call | flops 6442450944 | bytes 37748736 | tf_op jit(solution)/shard_map/update/pallas_call | solution.py:131
  184.0 2.7 %home_sum.1 = f32[128,768]{1,0:T(8,128)} custom-call(s32[4,128]{1,0:T(4,128)} %bitcast.56, bf16[512,768]{1,0:T(8,128)(2,1)} %bitcast.8.first_ref, bf16[512,768]{1,0:T(8,128)(2,1)} %bitcast.22.second_ref), custom_call_target="tpu_custom_call" | custom-call | tf_op jit(solution)/shard_map/home_sum/pallas_call | solution.py:234
  (74 shorter events, 22.9 us)
Async XLA Ops:
  3.2 29.5 %all-to-all-start = ((bf16[32,16,896]{2,1,0:T(8,128)(2,1)}), bf16[32,16,896]{2,1,0:T(8,128)(2,1)}, u32[]{:S(2)}, u32[]{:S(2)}) async-start(bf16[32,16,896]{2,1,0:T(8,128)(2,1)} %bitcast.51), calls=%async_computation | async-start | bytes 1835008 | tf_op jit(solution)/shard_map/all_to_all | solution.py:166
  32.7 21.3 %collective-permute-start = (bf16[512,896]{1,0:T(8,128)(2,1)}, bf16[512,896]{1,0:T(8,128)(2,1)}, u32[]{:S(2)}, u32[]{:S(2)}) collective-permute-start(bf16[512,896]{1,0:T(8,128)(2,1)} %bitcast.3), channel_id=1, source_target_pairs={{0,1},{1,2},{2,3},{3,0},{4,5},{5,6},{6,7},{7,4},{8,9},{9,10},{10,1... | collective-permute-start | bytes 2752520 | tf_op jit(solution)/shard_map/ppermute | solution.py:213
  32.7 22.3 %collective-permute-start.1 = (bf16[512,896]{1,0:T(8,128)(2,1)}, bf16[512,896]{1,0:T(8,128)(2,1)}, u32[]{:S(2)}, u32[]{:S(2)}) collective-permute-start(bf16[512,896]{1,0:T(8,128)(2,1)} %bitcast.3), channel_id=1, source_target_pairs={{0,3},{1,0},{2,1},{3,2},{4,7},{5,4},{6,5},{7,6},{8,11},{9,8},{10,9... | collective-permute-start | bytes 2752520 | tf_op jit(solution)/shard_map/ppermute | solution.py:214
  36.4 52.8 %all-to-all-start.2 = ((bf16[32,64,768]{2,1,0:T(8,128)(2,1)}), bf16[32,64,768]{2,1,0:T(8,128)(2,1)S(1)}, u32[]{:S(2)}, u32[]{:S(2)}) async-start(bf16[32,64,768]{2,1,0:T(8,128)(2,1)} %bitcast.43), calls=%async_computation.2 | async-start | bytes 6291456 | tf_op jit(solution)/shard_map/all_to_all | solution.py:166
  57.1 10.3 %collective-permute-start.2 = (bf16[256,896]{1,0:T(8,128)(2,1)S(1)}, bf16[256,896]{1,0:T(8,128)(2,1)S(1)}, u32[]{:S(2)}, u32[]{:S(2)}) collective-permute-start(bf16[256,896]{1,0:T(8,128)(2,1)S(1)} %slice.173), channel_id=1, source_target_pairs={{0,1},{1,2},{2,3},{3,0},{4,5},{5,6},{6,7},{7,4},{8,9},{9,10},{10,1... | collective-permute-start | bytes 1376264 | tf_op jit(solution)/shard_map/ppermute | solution.py:215
  59.0 9.5 %collective-permute-start.3 = (bf16[256,896]{1,0:T(8,128)(2,1)}, bf16[256,896]{1,0:T(8,128)(2,1)}, u32[]{:S(2)}, u32[]{:S(2)}) collective-permute-start(bf16[256,896]{1,0:T(8,128)(2,1)} %slice.175), channel_id=1, source_target_pairs={{0,3},{1,0},{2,1},{3,2},{4,7},{5,4},{6,5},{7,6},{8,11},{9,8},{10,9... | collective-permute-start | bytes 1376264 | tf_op jit(solution)/shard_map/ppermute | solution.py:216
  67.4 0.8 copy-start.11
  73.4 6.7 %copy-start.3 = (bf16[2,1024,768]{2,1,0:T(8,128)(2,1)S(1)}, bf16[2,1024,768]{2,1,0:T(8,128)(2,1)}, u32[]{:S(2)}) copy-start(bf16[2,1024,768]{2,1,0:T(8,128)(2,1)} %w_ref.1) | copy-start | bytes 9437188
  80.1 3.6 %copy-start.1 = (bf16[2048,1024]{1,0:T(8,128)(2,1)}, bf16[2048,1024]{1,0:T(8,128)(2,1)S(1)}, u32[]{:S(2)}) copy-start(bf16[2048,1024]{1,0:T(8,128)(2,1)S(1)} %subtract_convert_fusion.1.ga_ref) | copy-start | bytes 12582916
  83.8 2.1 %copy-start.8 = (bf16[2048,768]{1,0:T(8,128)(2,1)}, bf16[2048,768]{1,0:T(8,128)(2,1)S(1)}, u32[]{:S(2)}) copy-start(bf16[2048,768]{1,0:T(8,128)(2,1)S(1)} %convolution_convert_fusion.1) | copy-start | bytes 9437188
  84.9 14.5 %collective-permute-start.4 = (bf16[256,768]{1,0:T(8,128)(2,1)}, bf16[256,768]{1,0:T(8,128)(2,1)}, u32[]{:S(2)}, u32[]{:S(2)}) collective-permute-start(bf16[256,768]{1,0:T(8,128)(2,1)} %get-tuple-element.23), channel_id=1, source_target_pairs={{0,1},{1,2},{2,3},{3,0},{4,5},{5,6},{6,7},{7,4},{8,9},{9,10},{10,1... | collective-permute-start | bytes 1179656 | tf_op jit(solution)/shard_map/ppermute | solution.py:178
  85.9 13.6 %collective-permute-start.6 = (bf16[256,768]{1,0:T(8,128)(2,1)}, bf16[256,768]{1,0:T(8,128)(2,1)}, u32[]{:S(2)}, u32[]{:S(2)}) collective-permute-start(bf16[256,768]{1,0:T(8,128)(2,1)} %get-tuple-element.24), channel_id=1, source_target_pairs={{0,3},{1,0},{2,1},{3,2},{4,7},{5,4},{6,5},{7,6},{8,11},{9,8},{10,9... | collective-permute-start | bytes 1179656 | tf_op jit(solution)/shard_map/ppermute | solution.py:179
  89.3 6.1 %copy-start.4 = (bf16[2,1024,768]{2,1,0:T(8,128)(2,1)S(1)}, bf16[2,1024,768]{2,1,0:T(8,128)(2,1)}, u32[]{:S(2)}) copy-start(bf16[2,1024,768]{2,1,0:T(8,128)(2,1)} %w_ref.1) | copy-start | bytes 9437188
  95.4 3.6 %copy-start.6 = (bf16[2048,1024]{1,0:T(8,128)(2,1)}, bf16[2048,1024]{1,0:T(8,128)(2,1)S(1)}, u32[]{:S(2)}) copy-start(bf16[2048,1024]{1,0:T(8,128)(2,1)S(1)} %subtract_convert_fusion.gb_ref) | copy-start | bytes 12582916
  99.1 4.3 %copy-start.7 = (bf16[2048,768]{1,0:T(8,128)(2,1)}, bf16[2048,768]{1,0:T(8,128)(2,1)S(1)}, u32[]{:S(2)}) copy-start(bf16[2048,768]{1,0:T(8,128)(2,1)S(1)} %convolution_convert_fusion) | copy-start | bytes 9437188
  99.1 3.0 %copy-start.9 = (bf16[2048,768]{1,0:T(8,128)(2,1)S(1)}, bf16[2048,768]{1,0:T(8,128)(2,1)}, u32[]{:S(2)}) copy-start(bf16[2048,768]{1,0:T(8,128)(2,1)} %copy-done.8) | copy-start | bytes 9437188
  99.1 4.3 %copy-start.10 = (bf16[256,768]{1,0:T(8,128)(2,1)S(1)}, bf16[256,768]{1,0:T(8,128)(2,1)}, u32[]{:S(2)}) copy-start(bf16[256,768]{1,0:T(8,128)(2,1)} %get-tuple-element.26) | copy-start | bytes 1179652
  99.3 7.9 %collective-permute-start.8 = (bf16[256,768]{1,0:T(8,128)(2,1)S(1)}, bf16[256,768]{1,0:T(8,128)(2,1)S(1)}, u32[]{:S(2)}, u32[]{:S(2)}) collective-permute-start(bf16[256,768]{1,0:T(8,128)(2,1)S(1)} %bitcast.53), channel_id=1, source_target_pairs={{0,1},{1,2},{2,3},{3,0},{4,5},{5,6},{6,7},{7,4},{8,9},{9,10},{10,1... | collective-permute-start | bytes 1179656 | tf_op jit(solution)/shard_map/ppermute | solution.py:178
  103.5 20.2 %collective-permute-start.5 = (bf16[512,768]{1,0:T(8,128)(2,1)S(1)}, bf16[512,768]{1,0:T(8,128)(2,1)S(1)}, u32[]{:S(2)}, u32[]{:S(2)}) collective-permute-start(bf16[512,768]{1,0:T(8,128)(2,1)S(1)} %pad_maximum_fusion), channel_id=1, source_target_pairs={{0,1},{1,2},{2,3},{3,0},{4,5},{5,6},{6,7},{7,4},{8,9},{9,10},{10,1... | collective-permute-start | bytes 2359304 | tf_op jit(solution)/shard_map/ppermute | solution.py:182
  103.6 7.4 %collective-permute-start.10 = (bf16[256,768]{1,0:T(8,128)(2,1)S(1)}, bf16[256,768]{1,0:T(8,128)(2,1)S(1)}, u32[]{:S(2)}, u32[]{:S(2)}) collective-permute-start(bf16[256,768]{1,0:T(8,128)(2,1)S(1)} %bitcast.52), channel_id=1, source_target_pairs={{0,3},{1,0},{2,1},{3,2},{4,7},{5,4},{6,5},{7,6},{8,11},{9,8},{10,9... | collective-permute-start | bytes 1179656 | tf_op jit(solution)/shard_map/ppermute | solution.py:179
  106.3 20.5 %collective-permute-start.7 = (bf16[512,768]{1,0:T(8,128)(2,1)S(1)}, bf16[512,768]{1,0:T(8,128)(2,1)S(1)}, u32[]{:S(2)}, u32[]{:S(2)}) collective-permute-start(bf16[512,768]{1,0:T(8,128)(2,1)S(1)} %pad_maximum_fusion.1), channel_id=1, source_target_pairs={{0,3},{1,0},{2,1},{3,2},{4,7},{5,4},{6,5},{7,6},{8,11},{9,8},{10,9... | collective-permute-start | bytes 2359304 | tf_op jit(solution)/shard_map/ppermute | solution.py:183
  108.3 38.5 %collective-permute-start.9 = (bf16[512,768]{1,0:T(8,128)(2,1)}, bf16[512,768]{1,0:T(8,128)(2,1)}, u32[]{:S(2)}, u32[]{:S(2)}) collective-permute-start(bf16[512,768]{1,0:T(8,128)(2,1)} %pad_maximum_fusion.2), channel_id=1, source_target_pairs={{0,1},{1,2},{2,3},{3,0},{4,5},{5,6},{6,7},{7,4},{8,9},{9,10},{10,1... | collective-permute-start | bytes 2359304 | tf_op jit(solution)/shard_map/ppermute | solution.py:182
  112.0 34.8 %collective-permute-start.11 = (bf16[512,768]{1,0:T(8,128)(2,1)}, bf16[512,768]{1,0:T(8,128)(2,1)}, u32[]{:S(2)}, u32[]{:S(2)}) collective-permute-start(bf16[512,768]{1,0:T(8,128)(2,1)} %pad_maximum_fusion.3), channel_id=1, source_target_pairs={{0,3},{1,0},{2,1},{3,2},{4,7},{5,4},{6,5},{7,6},{8,11},{9,8},{10,9... | collective-permute-start | bytes 2359304 | tf_op jit(solution)/shard_map/ppermute | solution.py:183
  128.0 31.9 %all-to-all-start.1 = ((bf16[32,16,768]{2,1,0:T(8,128)(2,1)}), bf16[32,16,768]{2,1,0:T(8,128)(2,1)}, u32[]{:S(2)}, u32[]{:S(2)}) async-start(bf16[32,16,768]{2,1,0:T(8,128)(2,1)} %bitcast.47), calls=%async_computation.1 | async-start | bytes 1572864 | tf_op jit(solution)/shard_map/all_to_all | solution.py:166
  159.9 24.1 %all-to-all-start.3 = ((bf16[32,16,768]{2,1,0:T(8,128)(2,1)}), bf16[32,16,768]{2,1,0:T(8,128)(2,1)}, u32[]{:S(2)}, u32[]{:S(2)}) async-start(bf16[32,16,768]{2,1,0:T(8,128)(2,1)} %bitcast.48), calls=%async_computation.3 | async-start | bytes 1572864 | tf_op jit(solution)/shard_map/all_to_all | solution.py:166
  164.3 1.9 %copy-start = (bf16[2048,768]{1,0:T(8,128)(2,1)S(1)}, bf16[2048,768]{1,0:T(8,128)(2,1)}, u32[]{:S(2)}) copy-start(bf16[2048,768]{1,0:T(8,128)(2,1)} %slice_dynamic-update-slice_fusion.3.ra_ref) | copy-start | bytes 9437188
  166.2 2.2 %copy-start.2 = (bf16[2048,1024]{1,0:T(8,128)(2,1)S(1)}, bf16[2048,1024]{1,0:T(8,128)(2,1)}, u32[]{:S(2)}) copy-start(bf16[2048,1024]{1,0:T(8,128)(2,1)} %copy-done.1) | copy-start | bytes 12582916
  168.4 1.9 %copy-start.5 = (bf16[2,1024,768]{2,1,0:T(8,128)(2,1)S(1)}, bf16[2,1024,768]{2,1,0:T(8,128)(2,1)}, u32[]{:S(2)}) copy-start(bf16[2,1024,768]{2,1,0:T(8,128)(2,1)} %w_ref.1) | copy-start | bytes 9437188

commit v2 on v1

v2 whole, which is shorter than its diff:
```python
import jax
import jax.numpy as jnp
from jax import lax
from jax.experimental import pallas as pl
from jax.experimental.pallas import tpu as pltpu
from jax.sharding import PartitionSpec as P

momentum_decay = 0.9
step_rate = 0.002

CLUS = 32
LAB = 4
CAP = 16
NQ = 128
VISITS = 4
D = 768
EXTRA = 8
TAGS = 128
TILE = 256
SRC = TILE // (LAB * CAP)
STEPS = CLUS // SRC
LABELS = 1024
BAND = 256
ROWS = CLUS * CAP


def ring(shift):
    return [(i, (i + shift) % LAB) for i in range(LAB)]


def picks(visits_t, parity):
    dest = lax.broadcasted_iota(jnp.int32, (CLUS, NQ), 0) * 2 + parity
    hit = visits_t[0:1, :] == dest
    for k in range(1, VISITS):
        hit = hit | (visits_t[k : k + 1, :] == dest)
    before = lax.broadcasted_iota(jnp.int32, (NQ, NQ), 0) < lax.broadcasted_iota(
        jnp.int32, (NQ, NQ), 1
    )
    rank = jnp.dot(
        hit.astype(jnp.float32).astype(jnp.bfloat16),
        before.astype(jnp.float32).astype(jnp.bfloat16),
        preferred_element_type=jnp.float32,
    )
    place = jnp.where(hit, rank, -1.0).astype(jnp.int32)
    slot = lax.broadcasted_iota(jnp.int32, (CLUS, CAP, NQ), 1)
    return (place[:, None, :] == slot).reshape(ROWS, NQ)


def as_bf16(flags):
    return flags.astype(jnp.float32).astype(jnp.bfloat16)


def labels_of(visits_t, positives_t, parity):
    dest = lax.broadcasted_iota(jnp.int32, (CLUS, NQ), 0) * 2 + parity
    label = jnp.zeros((CLUS, NQ), jnp.int32)
    for k in range(VISITS):
        label = label + jnp.where(visits_t[k : k + 1, :] == dest, positives_t[k : k + 1, :] + 1, 0)
    return label


def slot_labels(chosen, label):
    wide = jnp.broadcast_to(label[:, None, :], (CLUS, CAP, NQ)).reshape(ROWS, NQ)
    return jnp.sum(jnp.where(chosen, wide, 0), axis=1, keepdims=True) - 1


def own_kernel(visits_ref, positives_ref, queries_ref, box_ref, raw_ref):
    bf = jnp.bfloat16
    visits_t, positives_t = visits_ref[...], positives_ref[...]
    lane = lax.broadcasted_iota(jnp.int32, (ROWS, TAGS), 1)
    notes = jnp.zeros((ROWS, TAGS), jnp.float32)
    for parity in range(2):
        chosen = picks(visits_t, parity)
        label = slot_labels(chosen, labels_of(visits_t, positives_t, parity))
        high = label >> 6
        low = label & 63
        notes = jnp.where(lane == 2 * parity, high.astype(jnp.float32), notes)
        notes = jnp.where(lane == 2 * parity + 1, low.astype(jnp.float32), notes)
        if parity == 0:
            filled = jnp.dot(as_bf16(chosen), queries_ref[...], preferred_element_type=jnp.float32)
            box_ref[:, :D] = filled.astype(bf)
    box_ref[:, D:] = notes.astype(bf)
    raw_ref[:NQ] = queries_ref[...]
    values = visits_t.astype(jnp.float32)
    parts = [values[k : k + 1, :] for k in range(VISITS)]
    row = jnp.concatenate(parts + [jnp.zeros((1, D - VISITS * NQ), jnp.float32)], axis=1)
    raw_ref[NQ:] = jnp.concatenate([row, jnp.zeros((EXTRA - 1, D), jnp.float32)], axis=0).astype(bf)


def all_kernel(*refs):
    box_ref = refs[LAB]
    for k in range(LAB):
        extra = refs[k][NQ:].astype(jnp.float32)
        parts = [extra[0:1, j * NQ : (j + 1) * NQ] for j in range(VISITS)]
        visits_t = jnp.concatenate(parts, axis=0).astype(jnp.int32)
        filled = jnp.dot(
            as_bf16(picks(visits_t, 1)), refs[k][:NQ], preferred_element_type=jnp.float32
        )
        box_ref[:, k] = filled.astype(jnp.bfloat16).reshape(CLUS, CAP, D)


def home_kernel(parity, visits_ref, homed_ref, before_ref, out_ref):
    chosen = as_bf16(picks(visits_ref[...], parity))
    out_ref[...] = before_ref[...] + lax.dot_general(
        chosen, homed_ref[...], (((0,), (0,)), ((), ())), preferred_element_type=jnp.float32
    )


def tile_grads(rows, high, low, first, w_ref):
    tag = (high * 64.0 + low).astype(jnp.int32) - first
    cols = []
    for c in range(0, LABELS, BAND):
        logits = lax.dot_general(
            rows,
            w_ref[0, c : c + BAND],
            (((1,), (1,)), ((), ())),
            preferred_element_type=jnp.float32,
        )
        place = lax.broadcasted_iota(jnp.int32, logits.shape, 1) + c
        target = jnp.where(tag == place, 1.0, 0.0)
        cols.append((jax.nn.sigmoid(logits) - target).astype(jnp.bfloat16))
    grad = jnp.concatenate(cols, axis=1)
    part = jnp.dot(grad, w_ref[0], preferred_element_type=jnp.float32)
    return grad, part.astype(jnp.bfloat16)


def first_kernel(lab_ref, rows_ref, w_ref, grad_ref, part_ref):
    for t in range(0, rows_ref.shape[0], TILE):
        notes = rows_ref[t : t + TILE, D:].astype(jnp.float32)
        grad, part = tile_grads(
            rows_ref[t : t + TILE, :D], notes[:, 0:1], notes[:, 1:2], lab_ref[0] * LABELS, w_ref
        )
        grad_ref[t : t + TILE] = grad
        part_ref[t : t + TILE] = part


def first_grads(lab, rows, weights):
    n = rows.shape[0]
    vmem = pltpu.VMEM
    return pl.pallas_call(
        first_kernel,
        grid=(1,),
        in_specs=[
            pl.BlockSpec(memory_space=pltpu.SMEM),
            pl.BlockSpec((n, D + TAGS), lambda i: (0, 0), memory_space=vmem),
            pl.BlockSpec((1, LABELS, D), lambda i: (0, 0, 0), memory_space=vmem),
        ],
        out_specs=(
            pl.BlockSpec((n, LABELS), lambda i: (0, 0), memory_space=vmem),
            pl.BlockSpec((n, D), lambda i: (0, 0), memory_space=vmem),
        ),
        out_shape=(
            jax.ShapeDtypeStruct((n, LABELS), jnp.bfloat16),
            jax.ShapeDtypeStruct((n, D), jnp.bfloat16),
        ),
        cost_estimate=pl.CostEstimate(
            flops=4 * n * LABELS * D, bytes_accessed=2 * n * 3000, transcendentals=n * LABELS
        ),
        name="first_grads",
    )(lab, rows, weights)


def second_kernel(lab_ref, rows_ref, own, low, high, far_a, far_b, w_ref, grad_ref, *parts):
    step = pl.program_id(0)
    early = step < STEPS // 2
    f32 = jnp.float32
    far = jnp.where(early, far_a[...].astype(f32), far_b[...].astype(f32))
    notes = [own[...].astype(f32), low[...].astype(f32), high[...].astype(f32), far]
    notes = jnp.stack([x.reshape(SRC, CAP, TAGS) for x in notes], axis=1).reshape(TILE, TAGS)
    rows = rows_ref[...].reshape(TILE, D)
    grad, part = tile_grads(rows, notes[:, 2:3], notes[:, 3:4], lab_ref[0] * LABELS, w_ref)
    grad_ref[...] = grad
    part = part.reshape(SRC, LAB, CAP, D)
    for k in range(3):
        parts[k][...] = part[:, k].reshape(SRC * CAP, D)

    @pl.when(early)
    def _():
        parts[3][...] = part[:, 3].reshape(SRC * CAP, D)

    @pl.when(jnp.logical_not(early))
    def _():
        parts[4][...] = part[:, 3].reshape(SRC * CAP, D)


def second_grads(lab, rows, pieces, weights):
    n = LAB * ROWS
    bf = jnp.bfloat16
    last = STEPS // 2 - 1
    here = SRC * CAP
    whole = lambda i: (i, D // TAGS)
    early = lambda i: (jnp.minimum(i, last), D // TAGS)
    late = lambda i: (jnp.maximum(i - last - 1, 0), D // TAGS)
    note = lambda at: pl.BlockSpec((here, TAGS), at)
    return pl.pallas_call(
        second_kernel,
        grid=(STEPS,),
        in_specs=[
            pl.BlockSpec(memory_space=pltpu.SMEM),
            pl.BlockSpec((SRC, LAB * CAP, D), lambda i: (i, 0, 0)),
            note(whole),
            note(whole),
            note(whole),
            note(early),
            note(late),
            pl.BlockSpec((1, LABELS, D), lambda i: (1, 0, 0)),
        ],
        out_specs=(
            pl.BlockSpec((TILE, LABELS), lambda i: (i, 0)),
            pl.BlockSpec((here, D), lambda i: (i, 0)),
            pl.BlockSpec((here, D), lambda i: (i, 0)),
            pl.BlockSpec((here, D), lambda i: (i, 0)),
            pl.BlockSpec((here, D), lambda i: (jnp.minimum(i, last), 0)),
            pl.BlockSpec((here, D), lambda i: (jnp.maximum(i - last - 1, 0), 0)),
        ),
        out_shape=(jax.ShapeDtypeStruct((n, LABELS), bf),)
        + (jax.ShapeDtypeStruct((ROWS, D), bf),) * 3
        + (jax.ShapeDtypeStruct((ROWS // 2, D), bf),) * 2,
        cost_estimate=pl.CostEstimate(
            flops=4 * n * LABELS * D, bytes_accessed=2 * n * 3000, transcendentals=n * LABELS
        ),
        name="second_grads",
    )(lab, rows, *pieces, weights)


def update_kernel(count, *refs):
    grads, rows = refs[:count], refs[count : 2 * count]
    w_ref, m_ref = refs[2 * count : 2 * count + 2]
    wo_ref, mo_ref = refs[-2:]
    fresh = momentum_decay * m_ref[0]
    for grad_ref, rows_ref in zip(grads, rows):
        fresh = fresh + lax.dot_general(
            grad_ref[...],
            rows_ref[:, :D],
            (((0,), (0,)), ((), ())),
            preferred_element_type=jnp.float32,
        )
    mo_ref[0] = fresh
    wo_ref[0] = (w_ref[0].astype(jnp.float32) - step_rate * fresh).astype(jnp.bfloat16)


def update(cluster, grads, rows, weights, momentum, before=()):
    bands = LABELS // BAND
    band = pl.BlockSpec((1, BAND, D), lambda b: (cluster, b, 0))
    n = sum(r.shape[0] for r in rows)
    count = len(grads)
    keep = [pl.BlockSpec(memory_space=pl.ANY) for _ in before]
    return pl.pallas_call(
        lambda *refs: update_kernel(count, *refs),
        grid=(bands,),
        in_specs=[pl.BlockSpec((g.shape[0], BAND), lambda b: (0, b)) for g in grads]
        + [pl.BlockSpec(r.shape, lambda b: (0, 0)) for r in rows]
        + [band, band]
        + keep,
        out_specs=(band, band),
        out_shape=(
            jax.ShapeDtypeStruct(weights.shape, weights.dtype),
            jax.ShapeDtypeStruct(momentum.shape, momentum.dtype),
        ),
        input_output_aliases={2 * count + 2 + k: k for k in range(len(before))},
        cost_estimate=pl.CostEstimate(
            flops=2 * n * LABELS * D, bytes_accessed=18 << 20, transcendentals=0
        ),
        name="update",
    )(*grads, *rows, weights, momentum, *before)


def swap(x):
    return lax.all_to_all(x, "clus", split_axis=0, concat_axis=0, tiled=True)


def add(*terms):
    total = terms[0].astype(jnp.float32)
    for term in terms[1:]:
        total = total + term.astype(jnp.float32)
    return total.astype(jnp.bfloat16)


def scatter_sum(own, low, high, far_a, far_b):
    half = ROWS // 2
    up = lax.ppermute(far_a, "lab", ring(1))
    down = lax.ppermute(far_b, "lab", ring(-1))
    up = jnp.concatenate([add(high[:half], up), high[half:]])
    down = jnp.concatenate([low[:half], add(low[half:], down)])
    up = lax.ppermute(up, "lab", ring(1))
    down = lax.ppermute(down, "lab", ring(-1))
    return own, up, down


def shards(queries, visits, positives, weights, momentum):
    vt, pt = visits.T, positives.T
    bf = jnp.bfloat16
    lab = lax.axis_index("lab").reshape(1).astype(jnp.int32)

    box_a, raw = pl.pallas_call(
        own_kernel,
        out_shape=(
            jax.ShapeDtypeStruct((ROWS, D + TAGS), bf),
            jax.ShapeDtypeStruct((NQ + EXTRA, D), bf),
        ),
        name="own_box",
    )(vt, pt, queries)
    peers = [raw] + [lax.ppermute(raw, "lab", ring(s)) for s in (1, -1, 2)]
    got_a = swap(box_a.reshape(CLUS, CAP, D + TAGS)).reshape(ROWS, D + TAGS)
    box_b = pl.pallas_call(
        all_kernel,
        out_shape=jax.ShapeDtypeStruct((CLUS, LAB, CAP, D), bf),
        name="all_box",
    )(*peers)
    got_a, box_b = lax.optimization_barrier((got_a, box_b))
    got_b = swap(box_b.reshape(CLUS, LAB * CAP, D))

    half = ROWS // 2
    from_low = lax.ppermute(got_a, "lab", ring(1))
    from_high = lax.ppermute(got_a, "lab", ring(-1))
    far_a = lax.ppermute(from_low[:half], "lab", ring(1))
    far_b = lax.ppermute(from_high[half:], "lab", ring(-1))
    pieces = (got_a, from_low, from_high, far_a, far_b)
    grads_a, parts_a = zip(*[first_grads(lab, p, weights) for p in pieces])
    own, up, down = scatter_sum(*parts_a)
    home_a = swap(add(own, up, down).reshape(CLUS, CAP, D)).reshape(ROWS, D)
    grad_b, *parts_b = second_grads(lab, got_b, pieces, weights)
    own, up, down = scatter_sum(*parts_b)
    new = update(0, grads_a, pieces, weights, momentum)
    new = update(1, (grad_b,), (got_b.reshape(LAB * ROWS, D),), weights, momentum, new)
    own, up, down, new = lax.optimization_barrier((own, up, down, new))
    home_b = swap(add(own, up, down).reshape(CLUS, CAP, D)).reshape(ROWS, D)

    total = jnp.zeros((NQ, D), jnp.float32)
    for parity, homed in ((0, home_a), (1, home_b)):
        total = pl.pallas_call(
            lambda *refs, parity=parity: home_kernel(parity, *refs),
            out_shape=jax.ShapeDtypeStruct((NQ, D), jnp.float32),
            name=f"home_{parity}",
        )(vt, homed, total)
    return (total, *new)


def solution(mesh):
    in_specs = (
        P(("clus", "lab"), None),
        P(("clus", "lab"), None),
        P(("clus", "lab"), None),
        P("clus", "lab", None),
        P("clus", "lab", None),
    )
    out_specs = (P(("clus", "lab"), None), P("clus", "lab", None), P("clus", "lab", None))
    return jax.shard_map(shards, mesh=mesh, in_specs=in_specs, out_specs=out_specs, check_vma=False)
```

time: 188 us -> 208 us (1.11)
  Pallas kernels: 23.1 us -> 63.9 us
  waiting for transfers between devices: 32.5 us -> 62 us
  matrix products: 20.1 us -> 0 us
  local copies, waits for them, and re-layouts: 29.7 us -> 12 us
  blocking collectives: 15.5 us -> 0 us
    pallas_call x3 -> x11, Pallas kernels: 20.5 us -> 61.3 us  [the longest x5 20.8 us: first_grads(): pl.pallas_call(first_kernel, grid=(1,), in_specs=[pl.BlockSpec(memory_spa...]
    ppermute x6 -> x9, waiting for transfers between devices: 4.83 us -> 31.2 us  [the longest x2 13.4 us: scatter_sum(): up = lax.ppermute(far_a, 'lab', ring(1))]
    dot_general x4 -> x0, matrix products: 20.1 us -> none  [the longest x2 12.8 us: grads(): jnp.einsum('rd,bd->rb', rows, weights, preferred_element_type=jnp.float32)]
    ppermute x1, waiting for transfers between devices: 0.01 us -> 19.8 us  [shards(): from_high = lax.ppermute(got_a, 'lab', ring(-1))]
    all_gather x1 -> x0, blocking collectives: 15.5 us -> none  [shards(): peers = lax.all_gather(raw, 'lab', axis=0, tiled=False)]
    unnamed x32 -> x28, local copies, waits for them, and re-layouts: 18.1 us -> 6.74 us
    ppermute x2, waiting for transfers between devices: 8.54 us -> 0.01 us  [scatter_sum(): up = lax.ppermute(up, 'lab', ring(1))]
    slice x14 -> x4, local copies, waits for them, and re-layouts: 9.31 us -> 3.41 us  [the longest x2 1.79 us: scatter_sum(): down = jnp.concatenate([low[:half], add(low[half:], down)])]
  transfers between devices with their start and end apart: 16 -> 19, of which waited for: 8 -> 7; matrix products, arithmetic and copies ran while one was open for 26% -> 8% of each run, Pallas kernels for 10% -> 28%
where the time goes in v2:
time: 208 us; the launch traced here: 207 us
  Pallas kernels  63.9 us (31%)
  waiting for transfers between devices  62 us (30%)
  starting transfers between devices  57.8 us (28%)
  local copies, waits for them, and re-layouts  12 us (6%)
  other arithmetic  10.5 us (5%)
    all_to_all x4, starting transfers between devices, swap(): return lax.all_to_all(x, 'clus', split_axis=0, concat_axis=0, tiled=True)  35.6 us
    pallas_call x5, Pallas kernels, first_grads(): pl.pallas_call(first_kernel, grid=(1,), in_specs=[pl.BlockSpec(memory_spa...  20.8 us
    ppermute x1, waiting for transfers between devices, shards(): from_high = lax.ppermute(got_a, 'lab', ring(-1))  19.8 us
    pallas_call x2, Pallas kernels, update(): pl.pallas_call(lambda *refs: update_kernel(count, *refs), grid=(bands,),...  18.7 us
    ppermute x2, waiting for transfers between devices, scatter_sum(): up = lax.ppermute(far_a, 'lab', ring(1))  13.4 us
    pallas_call x1, Pallas kernels, second_grads(): pl.pallas_call(second_kernel, grid=(STEPS,), in_specs=[pl.BlockSpec(memor...  12.7 us
    all_to_all x4, waiting for transfers between devices, swap(): return lax.all_to_all(x, 'clus', split_axis=0, concat_axis=0, tiled=True)  11 us
    ppermute x3, waiting for transfers between devices, shards(): peers = [raw] + [lax.ppermute(raw, 'lab', ring(s)) for s in (1, -1, 2)]  8.82 us
  transfers between devices with their start and end apart: 19, of which 7 were waited for; matrix products, arithmetic and copies ran while one was open for 8% of the time, Pallas kernels for 28%

profile of v2, /device:TPU:1, one launch (start us, length us, event | category | flops | bytes accessed | tf_op | source)
XLA Modules:
  0.0 207.1 jit_solution(17841221041837360016)
XLA Ops:
  0.6 2.6 %own_box.1 = (bf16[512,896]{1,0:T(8,128)(2,1)}, bf16[136,768]{1,0:T(8,128)(2,1)}) custom-call(s32[4,128]{1,0:T(4,128)} %bitcast.21, s32[4,128]{1,0:T(4,128)} %bitcast.24, bf16[128,768]{1,0:T(8,128)(2,1)} %queries_ref.1), custom_call_target="tpu_custom_call" | custom-call | tf_op jit(solution)/shard_map/own_box/pallas_call | solution.py:294
  3.2 8.7 %all-to-all-start = ((bf16[32,16,896]{2,1,0:T(8,128)(2,1)}), bf16[32,16,896]{2,1,0:T(8,128)(2,1)S(1)}, u32[]{:S(2)}, u32[]{:S(2)}) async-start(bf16[32,16,896]{2,1,0:T(8,128)(2,1)} %bitcast.20), calls=%async_computation | async-start | bytes 1835008 | tf_op jit(solution)/shard_map/all_to_all | solution.py:268
  12.0 3.7 %collective-permute-start.2 = (bf16[136,768]{1,0:T(8,128)(2,1)S(1)}, bf16[136,768]{1,0:T(8,128)(2,1)S(1)}, u32[]{:S(2)}, u32[]{:S(2)}) collective-permute-start(bf16[136,768]{1,0:T(8,128)(2,1)S(1)} %copy-done.10), channel_id=1, source_target_pairs={{0,2},{1,3},{2,0},{3,1},{4,6},{5,7},{6,4},{7,5},{8,10},{9,11},{10,... | collective-permute-start | bytes 626696 | tf_op jit(solution)/shard_map/ppermute | solution.py:302
  17.1 3.8 %collective-permute-done.2.refs_3_ = bf16[136,768]{1,0:T(8,128)(2,1)S(1)} collective-permute-done((bf16[136,768]{1,0:T(8,128)(2,1)S(1)}, bf16[136,768]{1,0:T(8,128)(2,1)S(1)}, u32[]{:S(2)}, u32[]{:S(2)}) %collective-permute-start.2) | collective-permute-done | bytes 208928 | tf_op jit(solution)/shard_map/ppermute | solution.py:302
  21.0 5.0 %collective-permute-done.1.refs_2_ = bf16[136,768]{1,0:T(8,128)(2,1)S(1)} collective-permute-done((bf16[136,768]{1,0:T(8,128)(2,1)S(1)}, bf16[136,768]{1,0:T(8,128)(2,1)S(1)}, u32[]{:S(2)}, u32[]{:S(2)}) %collective-permute-start.1) | collective-permute-done | bytes 208928 | tf_op jit(solution)/shard_map/ppermute | solution.py:302
  27.3 4.2 %all_box.1 = bf16[32,4,16,768]{3,2,1,0:T(8,128)(2,1)} custom-call(bf16[136,768]{1,0:T(8,128)(2,1)} %get-tuple-element.33.refs_0_, bf16[136,768]{1,0:T(8,128)(2,1)} %copy-done.13, bf16[136,768]{1,0:T(8,128)(2,1)} %copy-done.12, bf16[136,768]{1,0:T(8,128)(2,1)} %copy-done.11), custom_call_target="tpu_custom_call" | custom-call | tf_op jit(solution)/shard_map/all_box/pallas_call | solution.py:304
  32.4 8.1 %all-to-all-start.1 = ((bf16[32,64,768]{2,1,0:T(8,128)(2,1)}), bf16[32,64,768]{2,1,0:T(8,128)(2,1)S(1)}, u32[]{:S(2)}, u32[]{:S(2)}) async-start(bf16[32,64,768]{2,1,0:T(8,128)(2,1)} %bitcast.12), calls=%async_computation.1 | async-start | bytes 6291456 | tf_op jit(solution)/shard_map/all_to_all | solution.py:268
  40.5 2.4 %collective-permute-start.4 = (bf16[512,896]{1,0:T(8,128)(2,1)}, bf16[512,896]{1,0:T(8,128)(2,1)S(1)}, u32[]{:S(2)}, u32[]{:S(2)}) collective-permute-start(bf16[512,896]{1,0:T(8,128)(2,1)} %bitcast.13), channel_id=1, source_target_pairs={{0,3},{1,0},{2,1},{3,2},{4,7},{5,4},{6,5},{7,6},{8,11},{9,8},{10,9... | collective-permute-start | bytes 2752520 | tf_op jit(solution)/shard_map/ppermute | solution.py:314
  42.9 19.8 %collective-permute-done.4.high.rows_ref.refs_7_ = bf16[512,896]{1,0:T(8,128)(2,1)S(1)} collective-permute-done((bf16[512,896]{1,0:T(8,128)(2,1)}, bf16[512,896]{1,0:T(8,128)(2,1)S(1)}, u32[]{:S(2)}, u32[]{:S(2)}) %collective-permute-start.4) | collective-permute-done | bytes 917536 | tf_op jit(solution)/shard_map/ppermute | solution.py:314
  64.5 3.3 %collective-permute-start.6 = (bf16[256,896]{1,0:T(8,128)(2,1)}, bf16[256,896]{1,0:T(8,128)(2,1)}, u32[]{:S(2)}, u32[]{:S(2)}) collective-permute-start(bf16[256,896]{1,0:T(8,128)(2,1)} %slice.41), channel_id=1, source_target_pairs={{0,3},{1,0},{2,1},{3,2},{4,7},{5,4},{6,5},{7,6},{8,11},{9,8},{10,9... | collective-permute-start | bytes 1376264 | tf_op jit(solution)/shard_map/ppermute | solution.py:316
  69.6 7.3 %collective-permute-done.6.far_b.rows_ref.refs_9_ = bf16[256,896]{1,0:T(8,128)(2,1)} collective-permute-done((bf16[256,896]{1,0:T(8,128)(2,1)}, bf16[256,896]{1,0:T(8,128)(2,1)}, u32[]{:S(2)}, u32[]{:S(2)}) %collective-permute-start.6) | collective-permute-done | bytes 458784 | tf_op jit(solution)/shard_map/ppermute | solution.py:316
  76.9 3.5 %first_grads.9 = (bf16[256,1024]{1,0:T(8,128)(2,1)}, bf16[256,768]{1,0:T(8,128)(2,1)}) custom-call(s32[1]{0:T(128)} %bitcast.1.lab_ref, bf16[256,896]{1,0:T(8,128)(2,1)} %collective-permute-done.6.far_b.rows_ref.refs_9_, bf16[2,1024,768]{2,1,0:T(8,128)(2,1)} %refs_2_.1), custom_call_target="tpu_custom_call" | custom-call | flops 805306368 | bytes 1536000 | tf_op jit(solution)/shard_map/first_grads/pallas_call | solution.py:139
  80.4 3.4 %collective-permute-start.13 = (bf16[256,768]{1,0:T(8,128)(2,1)}, bf16[256,768]{1,0:T(8,128)(2,1)}, u32[]{:S(2)}, u32[]{:S(2)}) collective-permute-start(bf16[256,768]{1,0:T(8,128)(2,1)} %get-tuple-element.58), channel_id=1, source_target_pairs={{0,3},{1,0},{2,1},{3,2},{4,7},{5,4},{6,5},{7,6},{8,11},{9,8},{10,9... | collective-permute-start | bytes 1179656 | tf_op jit(solution)/shard_map/ppermute | solution.py:281
  83.8 4.6 %first_grads.6 = (bf16[512,1024]{1,0:T(8,128)(2,1)}, bf16[512,768]{1,0:T(8,128)(2,1)}) custom-call(s32[1]{0:T(128)} %bitcast.1.lab_ref, bf16[512,896]{1,0:T(8,128)(2,1)} %copy-done.5, bf16[2,1024,768]{2,1,0:T(8,128)(2,1)} %refs_2_.1), custom_call_target="tpu_custom_call" | custom-call | flops 1610612736 | bytes 3072000 | tf_op jit(solution)/shard_map/first_grads/pallas_call | solution.py:139
  88.3 1.8 slice.38
  90.1 4.6 %first_grads.7 = (bf16[512,1024]{1,0:T(8,128)(2,1)}, bf16[512,768]{1,0:T(8,128)(2,1)}) custom-call(s32[1]{0:T(128)} %bitcast.1.lab_ref, bf16[512,896]{1,0:T(8,128)(2,1)} %copy-done.4, bf16[2,1024,768]{2,1,0:T(8,128)(2,1)} %refs_2_.1), custom_call_target="tpu_custom_call" | custom-call | flops 1610612736 | bytes 3072000 | tf_op jit(solution)/shard_map/first_grads/pallas_call | solution.py:139
  95.7 3.5 %first_grads.8 = (bf16[256,1024]{1,0:T(8,128)(2,1)}, bf16[256,768]{1,0:T(8,128)(2,1)}) custom-call(s32[1]{0:T(128)} %bitcast.1.lab_ref, bf16[256,896]{1,0:T(8,128)(2,1)} %collective-permute-done.5.far_a.rows_ref.refs_8_, bf16[2,1024,768]{2,1,0:T(8,128)(2,1)} %refs_2_.1), custom_call_target="tpu_custom_call" | custom-call | flops 805306368 | bytes 1536000 | tf_op jit(solution)/shard_map/first_grads/pallas_call | solution.py:139
  100.4 1.9 pad_maximum_fusion.3
  102.4 2.7 %collective-permute-start.14 = (bf16[512,768]{1,0:T(8,128)(2,1)}, bf16[512,768]{1,0:T(8,128)(2,1)}, u32[]{:S(2)}, u32[]{:S(2)}) collective-permute-start(bf16[512,768]{1,0:T(8,128)(2,1)} %pad_maximum_fusion.3), channel_id=1, source_target_pairs={{0,3},{1,0},{2,1},{3,2},{4,7},{5,4},{6,5},{7,6},{8,11},{9,8},{10,9... | collective-permute-start | bytes 2359304 | tf_op jit(solution)/shard_map/ppermute | solution.py:285
  106.7 12.7 %second_grads.1 = (bf16[2048,1024]{1,0:T(8,128)(2,1)}, bf16[512,768]{1,0:T(8,128)(2,1)}, bf16[512,768]{1,0:T(8,128)(2,1)}, bf16[512,768]{1,0:T(8,128)(2,1)}, bf1...) custom-call(s32[1]{0:T(128)} %bitcast.1.lab_ref, bf16[32,64,768]{2,1,0:T(8,128)(2,1)} %copy-done, ...), custom_call_target="tpu_custom_call" | custom-call | flops 6442450944 | bytes 12288000 | tf_op jit(solution)/shard_map/second_grads/pallas_call | solution.py:194
  122.4 4.7 %first_grads.5 = (bf16[512,1024]{1,0:T(8,128)(2,1)}, bf16[512,768]{1,0:T(8,128)(2,1)}) custom-call(s32[1]{0:T(128)} %bitcast.1.lab_ref, bf16[512,896]{1,0:T(8,128)(2,1)} %bitcast.16, bf16[2,1024,768]{2,1,0:T(8,128)(2,1)} %refs_2_.1), custom_call_target="tpu_custom_call" | custom-call | flops 1610612736 | bytes 3072000 | tf_op jit(solution)/shard_map/first_grads/pallas_call | solution.py:139
  129.9 3.5 %collective-permute-start.10 = (bf16[512,768]{1,0:T(8,128)(2,1)S(1)}, bf16[512,768]{1,0:T(8,128)(2,1)}, u32[]{:S(2)}, u32[]{:S(2)}) collective-permute-start(bf16[512,768]{1,0:T(8,128)(2,1)S(1)} %pad_maximum_fusion.1), channel_id=1, source_target_pairs={{0,3},{1,0},{2,1},{3,2},{4,7},{5,4},{6,5},{7,6},{8,11},{9,8},{10,9... | collective-permute-start | bytes 2359304 | tf_op jit(solution)/shard_map/ppermute | solution.py:285
  133.4 13.4 %collective-permute-done.7 = bf16[256,768]{1,0:T(8,128)(2,1)S(1)} collective-permute-done((bf16[256,768]{1,0:T(8,128)(2,1)}, bf16[256,768]{1,0:T(8,128)(2,1)S(1)}, u32[]{:S(2)}, u32[]{:S(2)}) %collective-permute-start.7) | collective-permute-done | bytes 393248 | tf_op jit(solution)/shard_map/ppermute | solution.py:280
  147.1 2.3 %add_convert_fusion = bf16[512,768]{1,0:T(8,128)(2,1)} fusion(bf16[512,768]{1,0:T(8,128)(2,1)} %collective-permute-done.14, bf16[512,768]{1,0:T(8,128)(2,1)S(1)} %collective-permute-done.12, bf16[512,768]{1,0:T(8,128)(2,1)S(1)} %copy-done.9), kind=kLoop, calls=%fused_computation | loop fusion | flops 2359296 | bytes 3145728 | tf_op jit(solution)/shard_map/convert_element_type | solution.py:275
  149.4 11.4 %all-to-all-start.3 = ((bf16[32,16,768]{2,1,0:T(8,128)(2,1)}), bf16[32,16,768]{2,1,0:T(8,128)(2,1)S(1)}, u32[]{:S(2)}, u32[]{:S(2)}) async-start(bf16[32,16,768]{2,1,0:T(8,128)(2,1)} %bitcast.9), calls=%async_computation.3 | async-start | bytes 1572864 | tf_op jit(solution)/shard_map/all_to_all | solution.py:268
  160.8 9.4 %update.2 = (bf16[2,1024,768]{2,1,0:T(8,128)(2,1)}, f32[2,1024,768]{2,1,0:T(8,128)}) custom-call(bf16[512,1024]{1,0:T(8,128)(2,1)} %get-tuple-element.42.refs_0_, bf16[512,1024]{1,0:T(8,128)(2,1)} %get-tuple-element.43.refs_1_, bf16[512,1024]{1,0:T(8,128)(2,1)} %get-tuple-element.44.refs_2_, bf16[256,1024]{1,0:T(8,128)(2,1)} %get-tuple-element.45.refs_3_, ...), custom_call_target="tpu_custom_call" | custom-call | flops 3221225472 | bytes 18874368 | tf_op jit(solution)/shard_map/update/pallas_call | solution.py:247
  170.3 9.2 %update.3 = (bf16[2,1024,768]{2,1,0:T(8,128)(2,1)}, f32[2,1024,768]{2,1,0:T(8,128)}) custom-call(bf16[2048,1024]{1,0:T(8,128)(2,1)} %get-tuple-element.41.refs_0_, bf16[2048,768]{1,0:T(8,128)(2,1)} %bitcast.11, bf16[2,1024,768]{2,1,0:T(8,128)(2,1)} %refs_2_.1, f32[2,1024,768]{2,1,0:T(8,128)} %refs_3_.1, ...), custom_call_target="tpu_custom_call", output_to_operand_aliasing={{0}: (4, {}), {1}: (5, {})} | custom-call | flops 3221225472 | bytes 18874368 | tf_op jit(solution)/shard_map/update/pallas_call | solution.py:247
  179.6 2.5 %add_convert_fusion.1 = bf16[512,768]{1,0:T(8,128)(2,1)} fusion(bf16[512,768]{1,0:T(8,128)(2,1)} %collective-permute-done.10, bf16[512,768]{1,0:T(8,128)(2,1)} %collective-permute-done.8, bf16[512,768]{1,0:T(8,128)(2,1)S(1)} %copy-done.8), kind=kLoop, calls=%fused_computation.1 | loop fusion | flops 2359296 | bytes 3145728 | tf_op jit(solution)/shard_map/convert_element_type | solution.py:275
  182.1 7.4 %all-to-all-start.2 = ((bf16[32,16,768]{2,1,0:T(8,128)(2,1)}), bf16[32,16,768]{2,1,0:T(8,128)(2,1)S(1)}, u32[]{:S(2)}, u32[]{:S(2)}) async-start(bf16[32,16,768]{2,1,0:T(8,128)(2,1)} %bitcast.7), calls=%async_computation.2 | async-start | bytes 1572864 | tf_op jit(solution)/shard_map/all_to_all | solution.py:268
  190.3 2.4 %home_0.1.refs_2_ = f32[128,768]{1,0:T(8,128)} custom-call(s32[4,128]{1,0:T(4,128)} %bitcast.22, bf16[512,768]{1,0:T(8,128)(2,1)} %bitcast.18, f32[128,768]{1,0:T(8,128)} %broadcast_in_dim.3.refs_2_), custom_call_target="tpu_custom_call" | custom-call | tf_op jit(solution)/shard_map/home_0/pallas_call | solution.py:330
  192.7 11.0 %all-to-all-done.2 = bf16[32,16,768]{2,1,0:T(8,128)(2,1)S(1)} async-done(((bf16[32,16,768]{2,1,0:T(8,128)(2,1)}), bf16[32,16,768]{2,1,0:T(8,128)(2,1)S(1)}, u32[]{:S(2)}, u32[]{:S(2)}) %all-to-all-start.2) | async-done | bytes 786464 | tf_op jit(solution)/shard_map/all_to_all | solution.py:268
  204.6 2.4 %home_1.1 = f32[128,768]{1,0:T(8,128)} custom-call(s32[4,128]{1,0:T(4,128)} %bitcast.23, bf16[512,768]{1,0:T(8,128)(2,1)} %bitcast.19, f32[128,768]{1,0:T(8,128)} %home_0.1.refs_2_), custom_call_target="tpu_custom_call" | custom-call | tf_op jit(solution)/shard_map/home_1/pallas_call | solution.py:330
  (63 shorter events, 18.9 us)
Async XLA Ops:
  3.2 8.7 %copy-start.10 = (bf16[136,768]{1,0:T(8,128)(2,1)S(1)}, bf16[136,768]{1,0:T(8,128)(2,1)}, u32[]{:S(2)}) copy-start(bf16[136,768]{1,0:T(8,128)(2,1)} %get-tuple-element.33.refs_0_) | copy-start | bytes 626692
  3.2 28.3 %all-to-all-start = ((bf16[32,16,896]{2,1,0:T(8,128)(2,1)}), bf16[32,16,896]{2,1,0:T(8,128)(2,1)S(1)}, u32[]{:S(2)}, u32[]{:S(2)}) async-start(bf16[32,16,896]{2,1,0:T(8,128)(2,1)} %bitcast.20), calls=%async_computation | async-start | bytes 1835008 | tf_op jit(solution)/shard_map/all_to_all | solution.py:268
  12.0 9.0 %collective-permute-start.2 = (bf16[136,768]{1,0:T(8,128)(2,1)S(1)}, bf16[136,768]{1,0:T(8,128)(2,1)S(1)}, u32[]{:S(2)}, u32[]{:S(2)}) collective-permute-start(bf16[136,768]{1,0:T(8,128)(2,1)S(1)} %copy-done.10), channel_id=1, source_target_pairs={{0,2},{1,3},{2,0},{3,1},{4,6},{5,7},{6,4},{7,5},{8,10},{9,11},{10,... | collective-permute-start | bytes 626696 | tf_op jit(solution)/shard_map/ppermute | solution.py:302
  15.6 10.3 %collective-permute-start.1 = (bf16[136,768]{1,0:T(8,128)(2,1)S(1)}, bf16[136,768]{1,0:T(8,128)(2,1)S(1)}, u32[]{:S(2)}, u32[]{:S(2)}) collective-permute-start(bf16[136,768]{1,0:T(8,128)(2,1)S(1)} %copy-done.10), channel_id=1, source_target_pairs={{0,3},{1,0},{2,1},{3,2},{4,7},{5,4},{6,5},{7,6},{8,11},{9,8},{10,9... | collective-permute-start | bytes 626696 | tf_op jit(solution)/shard_map/ppermute | solution.py:302
  16.1 9.9 %collective-permute-start = (bf16[136,768]{1,0:T(8,128)(2,1)S(1)}, bf16[136,768]{1,0:T(8,128)(2,1)S(1)}, u32[]{:S(2)}, u32[]{:S(2)}) collective-permute-start(bf16[136,768]{1,0:T(8,128)(2,1)S(1)} %copy-done.10), channel_id=1, source_target_pairs={{0,1},{1,2},{2,3},{3,0},{4,5},{5,6},{6,7},{7,4},{8,9},{9,10},{10,1... | collective-permute-start | bytes 626696 | tf_op jit(solution)/shard_map/ppermute | solution.py:302
  21.0 5.0 %copy-start.11 = (bf16[136,768]{1,0:T(8,128)(2,1)}, bf16[136,768]{1,0:T(8,128)(2,1)S(1)}, u32[]{:S(2)}) copy-start(bf16[136,768]{1,0:T(8,128)(2,1)S(1)} %collective-permute-done.2.refs_3_) | copy-start | bytes 626692
  25.9 0.7 copy-start.12
  31.5 0.9 copy-start.1
  32.4 72.6 %all-to-all-start.1 = ((bf16[32,64,768]{2,1,0:T(8,128)(2,1)}), bf16[32,64,768]{2,1,0:T(8,128)(2,1)S(1)}, u32[]{:S(2)}, u32[]{:S(2)}) async-start(bf16[32,64,768]{2,1,0:T(8,128)(2,1)} %bitcast.12), calls=%async_computation.1 | async-start | bytes 6291456 | tf_op jit(solution)/shard_map/all_to_all | solution.py:268
  40.5 22.2 %collective-permute-start.4 = (bf16[512,896]{1,0:T(8,128)(2,1)}, bf16[512,896]{1,0:T(8,128)(2,1)S(1)}, u32[]{:S(2)}, u32[]{:S(2)}) collective-permute-start(bf16[512,896]{1,0:T(8,128)(2,1)} %bitcast.13), channel_id=1, source_target_pairs={{0,3},{1,0},{2,1},{3,2},{4,7},{5,4},{6,5},{7,6},{8,11},{9,8},{10,9... | collective-permute-start | bytes 2752520 | tf_op jit(solution)/shard_map/ppermute | solution.py:314
  42.9 24.9 %collective-permute-start.3 = (bf16[512,896]{1,0:T(8,128)(2,1)}, bf16[512,896]{1,0:T(8,128)(2,1)S(1)}, u32[]{:S(2)}, u32[]{:S(2)}) collective-permute-start(bf16[512,896]{1,0:T(8,128)(2,1)} %bitcast.14), channel_id=1, source_target_pairs={{0,1},{1,2},{2,3},{3,0},{4,5},{5,6},{6,7},{7,4},{8,9},{9,10},{10,1... | collective-permute-start | bytes 2752520 | tf_op jit(solution)/shard_map/ppermute | solution.py:313
  62.7 1.0 copy-start.4
  64.5 12.4 %collective-permute-start.6 = (bf16[256,896]{1,0:T(8,128)(2,1)}, bf16[256,896]{1,0:T(8,128)(2,1)}, u32[]{:S(2)}, u32[]{:S(2)}) collective-permute-start(bf16[256,896]{1,0:T(8,128)(2,1)} %slice.41), channel_id=1, source_target_pairs={{0,3},{1,0},{2,1},{3,2},{4,7},{5,4},{6,5},{7,6},{8,11},{9,8},{10,9... | collective-permute-start | bytes 1376264 | tf_op jit(solution)/shard_map/ppermute | solution.py:316
  67.8 0.9 copy-start.5
  69.6 26.1 %collective-permute-start.5 = (bf16[256,896]{1,0:T(8,128)(2,1)}, bf16[256,896]{1,0:T(8,128)(2,1)}, u32[]{:S(2)}, u32[]{:S(2)}) collective-permute-start(bf16[256,896]{1,0:T(8,128)(2,1)} %slice.40), channel_id=1, source_target_pairs={{0,1},{1,2},{2,3},{3,0},{4,5},{5,6},{6,7},{7,4},{8,9},{9,10},{10,1... | collective-permute-start | bytes 1376264 | tf_op jit(solution)/shard_map/ppermute | solution.py:315
  80.4 18.8 %collective-permute-start.13 = (bf16[256,768]{1,0:T(8,128)(2,1)}, bf16[256,768]{1,0:T(8,128)(2,1)}, u32[]{:S(2)}, u32[]{:S(2)}) collective-permute-start(bf16[256,768]{1,0:T(8,128)(2,1)} %get-tuple-element.58), channel_id=1, source_target_pairs={{0,3},{1,0},{2,1},{3,2},{4,7},{5,4},{6,5},{7,6},{8,11},{9,8},{10,9... | collective-permute-start | bytes 1179656 | tf_op jit(solution)/shard_map/ppermute | solution.py:281
  99.2 20.3 %collective-permute-start.11 = (bf16[256,768]{1,0:T(8,128)(2,1)}, bf16[256,768]{1,0:T(8,128)(2,1)}, u32[]{:S(2)}, u32[]{:S(2)}) collective-permute-start(bf16[256,768]{1,0:T(8,128)(2,1)} %get-tuple-element.56), channel_id=1, source_target_pairs={{0,1},{1,2},{2,3},{3,0},{4,5},{5,6},{6,7},{7,4},{8,9},{9,10},{10,1... | collective-permute-start | bytes 1179656 | tf_op jit(solution)/shard_map/ppermute | solution.py:280
  102.4 44.7 %collective-permute-start.14 = (bf16[512,768]{1,0:T(8,128)(2,1)}, bf16[512,768]{1,0:T(8,128)(2,1)}, u32[]{:S(2)}, u32[]{:S(2)}) collective-permute-start(bf16[512,768]{1,0:T(8,128)(2,1)} %pad_maximum_fusion.3), channel_id=1, source_target_pairs={{0,3},{1,0},{2,1},{3,2},{4,7},{5,4},{6,5},{7,6},{8,11},{9,8},{10,9... | collective-permute-start | bytes 2359304 | tf_op jit(solution)/shard_map/ppermute | solution.py:285
  105.0 1.6 copy-start
  119.4 9.3 %collective-permute-start.9 = (bf16[256,768]{1,0:T(8,128)(2,1)}, bf16[256,768]{1,0:T(8,128)(2,1)}, u32[]{:S(2)}, u32[]{:S(2)}) collective-permute-start(bf16[256,768]{1,0:T(8,128)(2,1)} %get-tuple-element.40), channel_id=1, source_target_pairs={{0,3},{1,0},{2,1},{3,2},{4,7},{5,4},{6,5},{7,6},{8,11},{9,8},{10,9... | collective-permute-start | bytes 1179656 | tf_op jit(solution)/shard_map/ppermute | solution.py:281
  120.8 26.3 %collective-permute-start.12 = (bf16[512,768]{1,0:T(8,128)(2,1)S(1)}, bf16[512,768]{1,0:T(8,128)(2,1)S(1)}, u32[]{:S(2)}, u32[]{:S(2)}) collective-permute-start(bf16[512,768]{1,0:T(8,128)(2,1)S(1)} %pad_maximum_fusion.2), channel_id=1, source_target_pairs={{0,1},{1,2},{2,3},{3,0},{4,5},{5,6},{6,7},{7,4},{8,9},{9,10},{10,1... | collective-permute-start | bytes 2359304 | tf_op jit(solution)/shard_map/ppermute | solution.py:284
  122.3 4.8 %copy-start.6 = (bf16[512,768]{1,0:T(8,128)(2,1)S(1)}, bf16[512,768]{1,0:T(8,128)(2,1)}, u32[]{:S(2)}) copy-start(bf16[512,768]{1,0:T(8,128)(2,1)} %get-tuple-element.37) | copy-start | bytes 2359300
  122.3 4.8 %copy-start.7 = (bf16[512,768]{1,0:T(8,128)(2,1)S(1)}, bf16[512,768]{1,0:T(8,128)(2,1)}, u32[]{:S(2)}) copy-start(bf16[512,768]{1,0:T(8,128)(2,1)} %get-tuple-element.39) | copy-start | bytes 2359300
  122.3 24.5 %collective-permute-start.7 = (bf16[256,768]{1,0:T(8,128)(2,1)}, bf16[256,768]{1,0:T(8,128)(2,1)S(1)}, u32[]{:S(2)}, u32[]{:S(2)}) collective-permute-start(bf16[256,768]{1,0:T(8,128)(2,1)} %get-tuple-element.38), channel_id=1, source_target_pairs={{0,1},{1,2},{2,3},{3,0},{4,5},{5,6},{6,7},{7,4},{8,9},{9,10},{10,1... | collective-permute-start | bytes 1179656 | tf_op jit(solution)/shard_map/ppermute | solution.py:280
  129.9 17.2 %copy-start.9 = (bf16[512,768]{1,0:T(8,128)(2,1)S(1)}, bf16[512,768]{1,0:T(8,128)(2,1)}, u32[]{:S(2)}) copy-start(bf16[512,768]{1,0:T(8,128)(2,1)} %get-tuple-element.54) | copy-start | bytes 2359300
  129.9 49.6 %collective-permute-start.10 = (bf16[512,768]{1,0:T(8,128)(2,1)S(1)}, bf16[512,768]{1,0:T(8,128)(2,1)}, u32[]{:S(2)}, u32[]{:S(2)}) collective-permute-start(bf16[512,768]{1,0:T(8,128)(2,1)S(1)} %pad_maximum_fusion.1), channel_id=1, source_target_pairs={{0,3},{1,0},{2,1},{3,2},{4,7},{5,4},{6,5},{7,6},{8,11},{9,8},{10,9... | collective-permute-start | bytes 2359304 | tf_op jit(solution)/shard_map/ppermute | solution.py:285
  146.9 32.6 %collective-permute-start.8 = (bf16[512,768]{1,0:T(8,128)(2,1)S(1)}, bf16[512,768]{1,0:T(8,128)(2,1)}, u32[]{:S(2)}, u32[]{:S(2)}) collective-permute-start(bf16[512,768]{1,0:T(8,128)(2,1)S(1)} %pad_maximum_fusion), channel_id=1, source_target_pairs={{0,1},{1,2},{2,3},{3,0},{4,5},{5,6},{6,7},{7,4},{8,9},{9,10},{10,1... | collective-permute-start | bytes 2359304 | tf_op jit(solution)/shard_map/ppermute | solution.py:284
  149.4 32.7 %all-to-all-start.3 = ((bf16[32,16,768]{2,1,0:T(8,128)(2,1)}), bf16[32,16,768]{2,1,0:T(8,128)(2,1)S(1)}, u32[]{:S(2)}, u32[]{:S(2)}) async-start(bf16[32,16,768]{2,1,0:T(8,128)(2,1)} %bitcast.9), calls=%async_computation.3 | async-start | bytes 1572864 | tf_op jit(solution)/shard_map/all_to_all | solution.py:268
  170.3 9.3 %copy-start.8 = (bf16[512,768]{1,0:T(8,128)(2,1)S(1)}, bf16[512,768]{1,0:T(8,128)(2,1)}, u32[]{:S(2)}) copy-start(bf16[512,768]{1,0:T(8,128)(2,1)} %get-tuple-element.51) | copy-start | bytes 2359300
  182.1 8.2 %copy-start.2 = (bf16[32,16,768]{2,1,0:T(8,128)(2,1)}, bf16[32,16,768]{2,1,0:T(8,128)(2,1)S(1)}, u32[]{:S(2)}) copy-start(bf16[32,16,768]{2,1,0:T(8,128)(2,1)S(1)} %all-to-all-done.3) | copy-start | bytes 2359300
  182.1 21.6 %all-to-all-start.2 = ((bf16[32,16,768]{2,1,0:T(8,128)(2,1)}), bf16[32,16,768]{2,1,0:T(8,128)(2,1)S(1)}, u32[]{:S(2)}, u32[]{:S(2)}) async-start(bf16[32,16,768]{2,1,0:T(8,128)(2,1)} %bitcast.7), calls=%async_computation.2 | async-start | bytes 1572864 | tf_op jit(solution)/shard_map/all_to_all | solution.py:268
  203.7 0.9 copy-start.3
  (1 other events, 0.7 us)

commit v3 on v1

--- a/solution.py
+++ b/solution.py
@@ -4,6 +4,7 @@
 from jax.experimental import pallas as pl
 from jax.experimental.pallas import tpu as pltpu
 from jax.sharding import PartitionSpec as P
+
 
 momentum_decay = 0.9
 step_rate = 0.002
@@ -83,75 +84,79 @@
     raw_ref[NQ:] = jnp.concatenate([row, jnp.zeros((EXTRA - 1, D), jnp.float32)], axis=0).astype(bf)
 
 
-def all_kernel(order_ref, raw_ref, box_ref):
+def all_kernel(*refs):
+    box_ref = refs[LAB]
     for k in range(LAB):
-        s = order_ref[k]
-        extra = raw_ref[s, NQ:].astype(jnp.float32)
+        extra = refs[k][NQ:].astype(jnp.float32)
         parts = [extra[0:1, j * NQ : (j + 1) * NQ] for j in range(VISITS)]
         visits_t = jnp.concatenate(parts, axis=0).astype(jnp.int32)
         filled = jnp.dot(
-            as_bf16(picks(visits_t, 1)), raw_ref[s, :NQ], preferred_element_type=jnp.float32
+            as_bf16(picks(visits_t, 1)), refs[k][:NQ], preferred_element_type=jnp.float32
         )
         box_ref[:, k] = filled.astype(jnp.bfloat16).reshape(CLUS, CAP, D)
 
 
-def home_kernel(visits_ref, first_ref, second_ref, out_ref):
+def home_kernel(visits_ref, homed_ref, out_ref):
     total = jnp.zeros((NQ, D), jnp.float32)
-    for parity, ref in ((0, first_ref), (1, second_ref)):
+    for parity in range(2):
         chosen = as_bf16(picks(visits_ref[...], parity))
+        rows = homed_ref[:, parity * D : (parity + 1) * D]
         total = total + lax.dot_general(
-            chosen, ref[...], (((0,), (0,)), ((), ())), preferred_element_type=jnp.float32
+            chosen, rows, (((0,), (0,)), ((), ())), preferred_element_type=jnp.float32
         )
     out_ref[...] = total
 
 
-def update_kernel(ga_ref, gb_ref, ra_ref, rb_ref, w_ref, m_ref, wo_ref, mo_ref):
-    def apply(grad_ref, rows_ref):
-        label_grad = lax.dot_general(
-            grad_ref[...], rows_ref[...], (((0,), (0,)), ((), ())), preferred_element_type=jnp.float32
-        )
-        fresh = momentum_decay * m_ref[0] + label_grad
+def update_kernel(gn_ref, gf_ref, gb_ref, rn_ref, rf_ref, rb_ref, w_ref, m_ref, wo_ref, mo_ref):
+    def apply(pairs):
+        fresh = momentum_decay * m_ref[0]
+        for grad_ref, rows_ref in pairs:
+            fresh = fresh + lax.dot_general(
+                grad_ref[...],
+                rows_ref[...],
+                (((0,), (0,)), ((), ())),
+                preferred_element_type=jnp.float32,
+            )
         mo_ref[0] = fresh
         wo_ref[0] = (w_ref[0].astype(jnp.float32) - step_rate * fresh).astype(jnp.bfloat16)
 
     @pl.when(pl.program_id(0) == 0)
     def _():
-        apply(ga_ref, ra_ref)
+        apply(((gn_ref, rn_ref), (gf_ref, rf_ref)))
 
     @pl.when(pl.program_id(0) == 1)
     def _():
-        apply(gb_ref, rb_ref)
+        apply(((gb_ref, rb_ref),))
 
 
 def update(grad_a, grad_b, rows_a, rows_b, weights, momentum):
     bands = LABELS // BAND
     n = LAB * ROWS
-    whole = pl.BlockSpec((n, D), lambda c, b: (0, 0))
+    whole = lambda x: pl.BlockSpec(x.shape, lambda c, b: (0, 0))
+    first = lambda x: pl.BlockSpec(
+        (x.shape[0], BAND), lambda c, b: (0, b * (1 - c) + (bands - 1) * c)
+    )
     band = pl.BlockSpec((1, BAND, D), lambda c, b: (c, b, 0))
     return pl.pallas_call(
         update_kernel,
         grid=(2, bands),
-        in_specs=[
-            pl.BlockSpec((n, BAND), lambda c, b: (0, b * (1 - c) + (bands - 1) * c)),
-            pl.BlockSpec((n, BAND), lambda c, b: (0, b * c)),
-            whole,
-            whole,
-            band,
-            band,
-        ],
+        in_specs=[first(g) for g in grad_a]
+        + [pl.BlockSpec((n, BAND), lambda c, b: (0, b * c))]
+        + [whole(r) for r in rows_a]
+        + [whole(rows_b), band, band],
         out_specs=(band, band),
         out_shape=(
             jax.ShapeDtypeStruct(weights.shape, weights.dtype),
             jax.ShapeDtypeStruct(momentum.shape, momentum.dtype),
         ),
         compiler_params=pltpu.CompilerParams(
-            dimension_semantics=("arbitrary", "arbitrary"), vmem_limit_bytes=40 << 20
+            dimension_semantics=("arbitrary", "arbitrary"), vmem_limit_bytes=56 << 20
         ),
         cost_estimate=pl.CostEstimate(
             flops=2 * 2 * n * LABELS * D, bytes_accessed=36 << 20, transcendentals=0
         ),
         name="update",
-    )(grad_a, grad_b, rows_a, rows_b, weights, momentum)
+    )(*grad_a, grad_b, *rows_a, rows_b, weights, momentum)
 
 
 def grads(rows, tag, weights, offsets):
@@ -173,8 +178,9 @@
     return total.astype(jnp.bfloat16)
 
 
-def scatter_sum(own, low, high, far):
-    half = own.shape[0] // 2
+def ring_sum(parts):
+    own, low, high, far = parts
+    half = ROWS // 2
     up = lax.ppermute(far[:half], "lab", ring(1))
     down = lax.ppermute(far[half:], "lab", ring(-1))
     up = jnp.concatenate([add(high[:half], up), high[half:]])
@@ -184,11 +190,10 @@
     return add(own, up, down)
 
 
-def shards(queries, visits, positives, weights, momentum):
+def step(queries, visits, positives, weights, momentum):
     vt, pt = visits.T, positives.T
     bf = jnp.bfloat16
     me = lax.axis_index("lab")
-    order = (me + jnp.array([0, 3, 1, 2], jnp.int32)) & 3
 
     box_a, raw = pl.pallas_call(
         own_kernel,
@@ -198,14 +203,13 @@
         ),
         name="own_box",
     )(vt, pt, queries)
+    peers = [raw] + [lax.ppermute(raw, "lab", ring(s)) for s in (1, -1, 2)]
     got_a = swap(box_a.reshape(CLUS, CAP, D + TAGS)).reshape(ROWS, D + TAGS)
-    peers = lax.all_gather(raw, "lab", axis=0, tiled=False)
     box_b = pl.pallas_call(
         all_kernel,
-        in_specs=[pl.BlockSpec(memory_space=pltpu.SMEM), pl.BlockSpec(memory_space=pltpu.VMEM)],
         out_shape=jax.ShapeDtypeStruct((CLUS, LAB, CAP, D), bf),
         name="all_box",
-    )(order, peers)
+    )(*peers)
     got_a, box_b = lax.optimization_barrier((got_a, box_b))
     got_b = swap(box_b.reshape(CLUS, LAB * CAP, D)).reshape(LAB * ROWS, D)
 
@@ -214,26 +218,29 @@
     from_high = lax.ppermute(got_a, "lab", ring(-1))
     far_low = lax.ppermute(from_low[:half], "lab", ring(1))
     far_high = lax.ppermute(from_high[half:], "lab", ring(-1))
-    pieces = (got_a, from_low, from_high, far_low, far_high)
-    rows_a = jnp.concatenate([p[:, :D] for p in pieces])
-    notes = jnp.concatenate([p[:, D : D + 4] for p in pieces]).astype(jnp.int32)
-    tag_a = notes[:, 0:1] * 64 + notes[:, 1:2]
-    tag_b = notes[:, 2:3] * 64 + notes[:, 3:4]
+    near, far = (got_a, from_low, from_high), (far_low, far_high)
+    rows_a = [jnp.concatenate([p[:, :D] for p in ps]) for ps in (near, far)]
+    notes = [jnp.concatenate([p[:, D : D + 4] for p in ps]).astype(jnp.int32) for ps in (near, far)]
+    tag_a = [x[:, 0:1] * 64 + x[:, 1:2] for x in notes]
+    tag_b = jnp.concatenate([x[:, 2:3] * 64 + x[:, 3:4] for x in notes])
     tag_b = jnp.moveaxis(tag_b.reshape(LAB, CLUS, CAP), 0, 1).reshape(LAB * ROWS, 1)
 
     offsets = me * LABELS + jnp.arange(LABELS, dtype=jnp.int32)
-    grad_a, part_a = grads(rows_a, tag_a, weights[0], offsets)
-    part_a = part_a.reshape(LAB, ROWS, D)
-    home_a = scatter_sum(part_a[0], part_a[1], part_a[2], part_a[3])
+    grad_far, part_far = grads(rows_a[1], tag_a[1], weights[0], offsets)
+    grad_near, part_near = grads(rows_a[0], tag_a[0], weights[0], offsets)
+    part_near = part_near.reshape(LAB - 1, ROWS, D)
+    home_a = ring_sum((part_near[0], part_near[1], part_near[2], part_far))
     grad_b, part_b = grads(got_b, tag_b, weights[1], offsets)
     part_b = part_b.reshape(CLUS, LAB, CAP, D)
-    home_b = scatter_sum(*[part_b[:, k].reshape(ROWS, D) for k in range(LAB)])
-    home_a = swap(home_a.reshape(CLUS, CAP, D)).reshape(ROWS, D)
-    home_b = swap(home_b.reshape(CLUS, CAP, D)).reshape(ROWS, D)
-    weights_new, momentum_new = update(grad_a, grad_b, rows_a, got_b, weights, momentum)
+    home_b = ring_sum([part_b[:, k].reshape(ROWS, D) for k in range(LAB)])
+    both = jnp.concatenate([home_a, home_b], axis=1).reshape(CLUS, CAP, 2 * D)
+    both = swap(both).reshape(ROWS, 2 * D)
+    weights_new, momentum_new = update(
+        (grad_near, grad_far), grad_b, rows_a, got_b, weights, momentum
+    )
     query_grad = pl.pallas_call(
         home_kernel, out_shape=jax.ShapeDtypeStruct((NQ, D), jnp.float32), name="home_sum"
-    )(vt, home_a, home_b)
+    )(vt, both)
     return (query_grad, weights_new, momentum_new)
 
 
@@ -246,4 +253,4 @@
         P("clus", "lab", None),
     )
     out_specs = (P(("clus", "lab"), None), P("clus", "lab", None), P("clus", "lab", None))
-    return jax.shard_map(shards, mesh=mesh, in_specs=in_specs, out_specs=out_specs, check_vma=False)
+    return jax.shard_map(step, mesh=mesh, in_specs=in_specs, out_specs=out_specs, check_vma=False)

time: 188 us -> 182 us (0.968)
  waiting for transfers between devices: 32.5 us -> 53.8 us
  blocking collectives: 15.5 us -> 0 us
  local copies, waits for them, and re-layouts: 29.7 us -> 21.1 us
  starting transfers between devices: 56.3 us -> 47.9 us
  Pallas kernels: 23.1 us -> 26.5 us
  matrix products: 20.1 us -> 23.1 us
    ppermute x12 -> x15, waiting for transfers between devices: 22 us -> 51.8 us  [the longest x2 26.1 us: ring_sum(): up = lax.ppermute(up, 'lab', ring(1))]
    all_gather x1 -> x0, blocking collectives: 15.5 us -> none  [shards(): peers = lax.all_gather(raw, 'lab', axis=0, tiled=False)]
    unnamed x32 -> x46, local copies, waits for them, and re-layouts: 18.1 us -> 4.7 us
    all_to_all x4 -> x3, starting transfers between devices: 40.6 us -> 28.1 us  [swap(): return lax.all_to_all(x, 'clus', split_axis=0, concat_axis=0, tiled=True)]
    all_to_all x4 -> x3, waiting for transfers between devices: 10.5 us -> 1.94 us  [swap(): return lax.all_to_all(x, 'clus', split_axis=0, concat_axis=0, tiled=True)]
    slice x15 -> x21, local copies, waits for them, and re-layouts: 9.54 us -> 16.2 us  [the longest x5 6.76 us: step(): rows_a = [jnp.concatenate([p[:, :D] for p in ps]) for ps in (near, far)]]
    ppermute x12 -> x15, starting transfers between devices: 15.7 us -> 19.8 us  [the longest x2 5.34 us: ring_sum(): down = lax.ppermute(far[half:], 'lab', ring(-1))]
    pallas_call x4, Pallas kernels: 23.1 us -> 26.5 us  [the longest x1 16.9 us: update(): pl.pallas_call(update_kernel, grid=(2, bands), in_specs=[first(g) for g i...]
  transfers between devices with their start and end apart: 16 -> 18, of which waited for: 8 -> 10; matrix products, arithmetic and copies ran while one was open for 26% -> 25% of each run, Pallas kernels for 10% -> 12%
where the time goes in v3:
time: 182 us; the launch traced here: 181 us
  waiting for transfers between devices  53.8 us (30%)
  starting transfers between devices  47.9 us (26%)
  Pallas kernels  26.5 us (15%)
  matrix products  23.1 us (13%)
  local copies, waits for them, and re-layouts  21.1 us (12%)
  other arithmetic  7.66 us (4%)
    all_to_all x3, starting transfers between devices, swap(): return lax.all_to_all(x, 'clus', split_axis=0, concat_axis=0, tiled=True)  28.1 us
    ppermute x2, waiting for transfers between devices, ring_sum(): up = lax.ppermute(up, 'lab', ring(1))  26.1 us
    pallas_call x1, Pallas kernels, update(): pl.pallas_call(update_kernel, grid=(2, bands), in_specs=[first(g) for g i...  16.9 us
    dot_general x3, matrix products, grads(): jnp.einsum('rd,bd->rb', rows, weights, preferred_element_type=jnp.float32)  15.6 us
    ppermute x3, waiting for transfers between devices, step(): peers = [raw] + [lax.ppermute(raw, 'lab', ring(s)) for s in (1, -1, 2)]  9.62 us
    ppermute x1, waiting for transfers between devices, step(): from_low = lax.ppermute(got_a, 'lab', ring(1))  7.98 us
    dot_general x3, matrix products, grads(): jnp.einsum('rb,bd->rd', grad, weights, preferred_element_type=jnp.float32)  7.41 us
    slice x5, local copies, waits for them, and re-layouts, step(): rows_a = [jnp.concatenate([p[:, :D] for p in ps]) for ps in (near, far)]  6.76 us
  transfers between devices with their start and end apart: 18, of which 10 were waited for; matrix products, arithmetic and copies ran while one was open for 25% of the time, Pallas kernels for 12%

profile of v3, /device:TPU:1, one launch (start us, length us, event | category | flops | bytes accessed | tf_op | source)
XLA Modules:
  0.0 181.2 jit_solution(7999315844544652242)
XLA Ops:
  0.6 2.6 %own_box.1 = (bf16[512,896]{1,0:T(8,128)(2,1)}, bf16[136,768]{1,0:T(8,128)(2,1)}) custom-call(s32[4,128]{1,0:T(4,128)} %bitcast.70, s32[4,128]{1,0:T(4,128)} %bitcast.72, bf16[128,768]{1,0:T(8,128)(2,1)} %queries_ref.1), custom_call_target="tpu_custom_call" | custom-call | tf_op jit(solution)/shard_map/own_box/pallas_call | solution.py:198
  3.2 8.6 %all-to-all-start = ((bf16[32,16,896]{2,1,0:T(8,128)(2,1)}), bf16[32,16,896]{2,1,0:T(8,128)(2,1)}, u32[]{:S(2)}, u32[]{:S(2)}) async-start(bf16[32,16,896]{2,1,0:T(8,128)(2,1)} %bitcast.66), calls=%async_computation | async-start | bytes 1835008 | tf_op jit(solution)/shard_map/all_to_all | solution.py:171
  11.9 1.7 collective-permute-start
  13.6 2.2 %collective-permute-start.1 = (bf16[136,768]{1,0:T(8,128)(2,1)}, bf16[136,768]{1,0:T(8,128)(2,1)S(1)}, u32[]{:S(2)}, u32[]{:S(2)}) collective-permute-start(bf16[136,768]{1,0:T(8,128)(2,1)} %get-tuple-element.10.refs_0_), channel_id=1, source_target_pairs={{0,3},{1,0},{2,1},{3,2},{4,7},{5,4},{6,5},{7,6},{8,11},{9,8},{10,9... | collective-permute-start | bytes 626696 | tf_op jit(solution)/shard_map/ppermute | solution.py:206
  17.0 4.3 %collective-permute-done.refs_1_ = bf16[136,768]{1,0:T(8,128)(2,1)S(1)} collective-permute-done((bf16[136,768]{1,0:T(8,128)(2,1)}, bf16[136,768]{1,0:T(8,128)(2,1)S(1)}, u32[]{:S(2)}, u32[]{:S(2)}) %collective-permute-start) | collective-permute-done | bytes 208928 | tf_op jit(solution)/shard_map/ppermute | solution.py:206
  21.3 5.4 %collective-permute-done.2.refs_3_ = bf16[136,768]{1,0:T(8,128)(2,1)S(1)} collective-permute-done((bf16[136,768]{1,0:T(8,128)(2,1)}, bf16[136,768]{1,0:T(8,128)(2,1)S(1)}, u32[]{:S(2)}, u32[]{:S(2)}) %collective-permute-start.2) | collective-permute-done | bytes 208928 | tf_op jit(solution)/shard_map/ppermute | solution.py:206
  27.3 4.3 %all_box.1 = bf16[32,4,16,768]{3,2,1,0:T(8,128)(2,1)} custom-call(bf16[136,768]{1,0:T(8,128)(2,1)} %get-tuple-element.10.refs_0_, bf16[136,768]{1,0:T(8,128)(2,1)} %copy-done.20, bf16[136,768]{1,0:T(8,128)(2,1)} %copy-done.21, bf16[136,768]{1,0:T(8,128)(2,1)} %copy-done.22), custom_call_target="tpu_custom_call" | custom-call | tf_op jit(solution)/shard_map/all_box/pallas_call | solution.py:208
  32.2 2.1 %collective-permute-start.4 = (bf16[512,896]{1,0:T(8,128)(2,1)}, bf16[512,896]{1,0:T(8,128)(2,1)}, u32[]{:S(2)}, u32[]{:S(2)}) collective-permute-start(bf16[512,896]{1,0:T(8,128)(2,1)} %bitcast.3), channel_id=1, source_target_pairs={{0,3},{1,0},{2,1},{3,2},{4,7},{5,4},{6,5},{7,6},{8,11},{9,8},{10,9... | collective-permute-start | bytes 2752520 | tf_op jit(solution)/shard_map/ppermute | solution.py:218
  35.2 2.1 %slice.143 = bf16[512,768]{1,0:T(8,128)(2,1)} slice(bf16[512,896]{1,0:T(8,128)(2,1)} %bitcast.3), slice={[0:512], [0:768]} | slice | bytes 1572864 | tf_op jit(solution)/shard_map/slice | solution.py:222
  37.4 8.6 %all-to-all-start.1 = ((bf16[32,64,768]{2,1,0:T(8,128)(2,1)}), bf16[32,64,768]{2,1,0:T(8,128)(2,1)S(1)}, u32[]{:S(2)}, u32[]{:S(2)}) async-start(bf16[32,64,768]{2,1,0:T(8,128)(2,1)} %bitcast.58), calls=%async_computation.1 | async-start | bytes 6291456 | tf_op jit(solution)/shard_map/all_to_all | solution.py:171
  46.0 8.0 %collective-permute-done.3 = bf16[512,896]{1,0:T(8,128)(2,1)} collective-permute-done((bf16[512,896]{1,0:T(8,128)(2,1)}, bf16[512,896]{1,0:T(8,128)(2,1)}, u32[]{:S(2)}, u32[]{:S(2)}) %collective-permute-start.3) | collective-permute-done | bytes 917536 | tf_op jit(solution)/shard_map/ppermute | solution.py:217
  57.4 1.8 %slice.193 = bf16[256,896]{1,0:T(8,128)(2,1)} slice(bf16[512,896]{1,0:T(8,128)(2,1)} %collective-permute-done.4), slice={[256:512], [0:896]} | slice | bytes 917504 | tf_op jit(solution)/shard_map/slice | solution.py:220
  59.3 2.7 %collective-permute-start.6 = (bf16[256,896]{1,0:T(8,128)(2,1)}, bf16[256,896]{1,0:T(8,128)(2,1)}, u32[]{:S(2)}, u32[]{:S(2)}) collective-permute-start(bf16[256,896]{1,0:T(8,128)(2,1)} %slice.193), channel_id=1, source_target_pairs={{0,3},{1,0},{2,1},{3,2},{4,7},{5,4},{6,5},{7,6},{8,11},{9,8},{10,9... | collective-permute-start | bytes 1376264 | tf_op jit(solution)/shard_map/ppermute | solution.py:220
  64.6 5.6 %subtract_convert_fusion.1.gn_ref = bf16[1536,1024]{1,0:T(8,128)(2,1)S(1)} fusion(s32[1024]{0:T(1024)S(1)} %iota_add_fusion, s32[1536]{0:T(1024)S(1)} %get-tuple-element.27, bf16[2,1024,768]{2,1,0:T(8,128)(2,1)S(1)} %copy-done.8, bf16[512,768]{1,0:T(8,128)(2,1)S(1)} %slice.184, bf16[512,768]{1,0:T(8,128)(2,1)S(1)} %slice.183, bf16[512,768]{1,0:T(8,128)(2,1)S(1)} %copy-done.3), kind=kOutput, calls=%fused_computation.1 | convolution fusion | flops 2434007040 | bytes 7090176 | tf_op jit(solution)/shard_map/rd,bd->rb/dot_general | solution.py:163
  70.3 2.8 %convolution_convert_fusion = bf16[1536,768]{1,0:T(8,128)(2,1)S(1)} fusion(bf16[1536,1024]{1,0:T(8,128)(2,1)S(1)} %subtract_convert_fusion.1.gn_ref, bf16[2,1024,768]{2,1,0:T(8,128)(2,1)S(1)} %copy-done.8), kind=kOutput, calls=%fused_computation.2 | convolution fusion | flops 2417098752 | bytes 7077888 | tf_op jit(solution)/shard_map/rb,bd->rd/dot_general | solution.py:166
  79.1 2.8 %subtract_convert_fusion.2.gf_ref = bf16[512,1024]{1,0:T(8,128)(2,1)S(1)} fusion(s32[1024]{0:T(1024)S(1)} %iota_add_fusion, s32[512]{0:T(512)S(1)} %bitcast.73, bf16[2,1024,768]{2,1,0:T(8,128)(2,1)} %w_ref.1, bf16[256,768]{1,0:T(8,128)(2,1)S(1)} %slice.194, bf16[256,768]{1,0:T(8,128)(2,1)S(1)} %slice.192), kind=kOutput, calls=%fused_computation.5 | convolution fusion | flops 810549248 | bytes 3414016 | tf_op jit(solution)/shard_map/rd,bd->rb/dot_general | solution.py:163
  83.9 2.7 %collective-permute-start.9 = (bf16[256,768]{1,0:T(8,128)(2,1)}, bf16[256,768]{1,0:T(8,128)(2,1)}, u32[]{:S(2)}, u32[]{:S(2)}) collective-permute-start(bf16[256,768]{1,0:T(8,128)(2,1)} %get-tuple-element.26), channel_id=1, source_target_pairs={{0,3},{1,0},{2,1},{3,2},{4,7},{5,4},{6,5},{7,6},{8,11},{9,8},{10,9... | collective-permute-start | bytes 1179656 | tf_op jit(solution)/shard_map/ppermute | solution.py:185
  86.6 7.2 %subtract_convert_fusion.gb_ref = bf16[2048,1024]{1,0:T(8,128)(2,1)S(1)} fusion(bf16[2048,768]{1,0:T(8,128)(2,1)S(1)} %bitcast.59, s32[1024]{0:T(1024)S(1)} %iota_add_fusion, s32[2048]{0:T(1024)S(1)} %eq.53, bf16[2,1024,768]{2,1,0:T(8,128)(2,1)} %w_ref.1), kind=kOutput, calls=%fused_computation | convolution fusion | flops 3235905536 | bytes 8925184 | tf_op jit(solution)/shard_map/rd,bd->rb/dot_general | solution.py:163
  93.7 3.6 %convolution_convert_fusion.1 = bf16[2048,768]{1,0:T(8,128)(2,1)S(1)} fusion(bf16[2048,1024]{1,0:T(8,128)(2,1)S(1)} %subtract_convert_fusion.gb_ref, bf16[2,1024,768]{2,1,0:T(8,128)(2,1)S(1)} %copy-done.10), kind=kOutput, calls=%fused_computation.3 | convolution fusion | flops 3222798336 | bytes 8912896 | tf_op jit(solution)/shard_map/rb,bd->rd/dot_general | solution.py:166
  100.5 2.7 %collective-permute-start.13 = (bf16[256,768]{1,0:T(8,128)(2,1)S(1)}, bf16[256,768]{1,0:T(8,128)(2,1)S(1)}, u32[]{:S(2)}, u32[]{:S(2)}) collective-permute-start(bf16[256,768]{1,0:T(8,128)(2,1)S(1)} %bitcast.67), channel_id=1, source_target_pairs={{0,3},{1,0},{2,1},{3,2},{4,7},{5,4},{6,5},{7,6},{8,11},{9,8},{10,9... | collective-permute-start | bytes 1179656 | tf_op jit(solution)/shard_map/ppermute | solution.py:185
  103.5 3.1 %collective-permute-done.11 = bf16[256,768]{1,0:T(8,128)(2,1)S(1)} collective-permute-done((bf16[256,768]{1,0:T(8,128)(2,1)S(1)}, bf16[256,768]{1,0:T(8,128)(2,1)S(1)}, u32[]{:S(2)}, u32[]{:S(2)}) %collective-permute-start.11) | collective-permute-done | bytes 393248 | tf_op jit(solution)/shard_map/ppermute | solution.py:184
  106.8 1.5 collective-permute-done.13
  108.5 3.5 %collective-permute-start.14 = (bf16[512,768]{1,0:T(8,128)(2,1)S(1)}, bf16[512,768]{1,0:T(8,128)(2,1)S(1)}, u32[]{:S(2)}, u32[]{:S(2)}) collective-permute-start(bf16[512,768]{1,0:T(8,128)(2,1)S(1)} %pad_maximum_fusion.6), channel_id=1, source_target_pairs={{0,3},{1,0},{2,1},{3,2},{4,7},{5,4},{6,5},{7,6},{8,11},{9,8},{10,9... | collective-permute-start | bytes 2359304 | tf_op jit(solution)/shard_map/ppermute | solution.py:189
  112.0 11.4 %collective-permute-done.8 = bf16[512,768]{1,0:T(8,128)(2,1)S(1)} collective-permute-done((bf16[512,768]{1,0:T(8,128)(2,1)S(1)}, bf16[512,768]{1,0:T(8,128)(2,1)S(1)}, u32[]{:S(2)}, u32[]{:S(2)}) %collective-permute-start.8) | collective-permute-done | bytes 786464 | tf_op jit(solution)/shard_map/ppermute | solution.py:188
  123.4 1.8 collective-permute-done.10
  125.6 14.7 %collective-permute-done.12 = bf16[512,768]{1,0:T(8,128)(2,1)S(1)} collective-permute-done((bf16[512,768]{1,0:T(8,128)(2,1)S(1)}, bf16[512,768]{1,0:T(8,128)(2,1)S(1)}, u32[]{:S(2)}, u32[]{:S(2)}) %collective-permute-start.12) | collective-permute-done | bytes 786464 | tf_op jit(solution)/shard_map/ppermute | solution.py:188
  140.3 1.8 collective-permute-done.14
  143.7 10.9 %all-to-all-start.2 = ((bf16[32,16,1536]{2,1,0:T(8,128)(2,1)}), bf16[32,16,1536]{2,1,0:T(8,128)(2,1)S(1)}, u32[]{:S(2)}, u32[]{:S(2)}) async-start(bf16[32,16,1536]{2,1,0:T(8,128)(2,1)} %bitcast.18), calls=%async_computation.2 | async-start | bytes 3145728 | tf_op jit(solution)/shard_map/all_to_all | solution.py:171
  154.6 2.8 %pad_maximum_fusion.rn_ref = bf16[1536,768]{1,0:T(8,128)(2,1)} fusion(bf16[512,768]{1,0:T(8,128)(2,1)} %copy-done.7, bf16[512,768]{1,0:T(8,128)(2,1)S(1)} %copy-done.6, bf16[512,768]{1,0:T(8,128)(2,1)S(1)} %copy-done.4), kind=kLoop, calls=%fused_computation.4 | loop fusion | flops 7077888 | bytes 4718592 | tf_op jit(solution)/shard_map/concatenate | solution.py:222
  158.4 16.9 %update.1 = (bf16[2,1024,768]{2,1,0:T(8,128)(2,1)}, f32[2,1024,768]{2,1,0:T(8,128)}) custom-call(bf16[1536,1024]{1,0:T(8,128)(2,1)} %copy-done.11, bf16[512,1024]{1,0:T(8,128)(2,1)} %copy-done.18, bf16[2048,1024]{1,0:T(8,128)(2,1)} %copy-done.2, bf16[1536,768]{1,0:T(8,128)(2,1)} %pad_maximum_fusion.rn_ref, bf16[512,768]{1,0:T(8,128)(2,1)} %pad_maximum_fusion.2.rf_ref, ...), custom_call_target="tpu_custom_call" | custom-call | flops 6442450944 | bytes 37748736 | tf_op jit(solution)/shard_map/update/pallas_call | solution.py:140
  175.3 1.9 %all-to-all-done.2 = bf16[32,16,1536]{2,1,0:T(8,128)(2,1)S(1)} async-done(((bf16[32,16,1536]{2,1,0:T(8,128)(2,1)}), bf16[32,16,1536]{2,1,0:T(8,128)(2,1)S(1)}, u32[]{:S(2)}, u32[]{:S(2)}) %all-to-all-start.2) | async-done | bytes 1572896 | tf_op jit(solution)/shard_map/all_to_all | solution.py:171
  178.5 2.7 %home_sum.1 = f32[128,768]{1,0:T(8,128)} custom-call(s32[4,128]{1,0:T(4,128)} %bitcast.71, bf16[512,1536]{1,0:T(8,128)(2,1)} %bitcast.61), custom_call_target="tpu_custom_call" | custom-call | tf_op jit(solution)/shard_map/home_sum/pallas_call | solution.py:241
  (102 shorter events, 25.4 us)
Async XLA Ops:
  3.2 28.4 %all-to-all-start = ((bf16[32,16,896]{2,1,0:T(8,128)(2,1)}), bf16[32,16,896]{2,1,0:T(8,128)(2,1)}, u32[]{:S(2)}, u32[]{:S(2)}) async-start(bf16[32,16,896]{2,1,0:T(8,128)(2,1)} %bitcast.66), calls=%async_computation | async-start | bytes 1835008 | tf_op jit(solution)/shard_map/all_to_all | solution.py:171
  11.9 9.4 %collective-permute-start = (bf16[136,768]{1,0:T(8,128)(2,1)}, bf16[136,768]{1,0:T(8,128)(2,1)S(1)}, u32[]{:S(2)}, u32[]{:S(2)}) collective-permute-start(bf16[136,768]{1,0:T(8,128)(2,1)} %get-tuple-element.10.refs_0_), channel_id=1, source_target_pairs={{0,1},{1,2},{2,3},{3,0},{4,5},{5,6},{6,7},{7,4},{8,9},{9,10},{10,1... | collective-permute-start | bytes 626696 | tf_op jit(solution)/shard_map/ppermute | solution.py:206
  13.6 7.7 %collective-permute-start.1 = (bf16[136,768]{1,0:T(8,128)(2,1)}, bf16[136,768]{1,0:T(8,128)(2,1)S(1)}, u32[]{:S(2)}, u32[]{:S(2)}) collective-permute-start(bf16[136,768]{1,0:T(8,128)(2,1)} %get-tuple-element.10.refs_0_), channel_id=1, source_target_pairs={{0,3},{1,0},{2,1},{3,2},{4,7},{5,4},{6,5},{7,6},{8,11},{9,8},{10,9... | collective-permute-start | bytes 626696 | tf_op jit(solution)/shard_map/ppermute | solution.py:206
  15.8 10.8 %collective-permute-start.2 = (bf16[136,768]{1,0:T(8,128)(2,1)}, bf16[136,768]{1,0:T(8,128)(2,1)S(1)}, u32[]{:S(2)}, u32[]{:S(2)}) collective-permute-start(bf16[136,768]{1,0:T(8,128)(2,1)} %get-tuple-element.10.refs_0_), channel_id=1, source_target_pairs={{0,2},{1,3},{2,0},{3,1},{4,6},{5,7},{6,4},{7,5},{8,10},{9,11},{10,... | collective-permute-start | bytes 626696 | tf_op jit(solution)/shard_map/ppermute | solution.py:206
  21.3 5.4 %copy-start.20 = (bf16[136,768]{1,0:T(8,128)(2,1)}, bf16[136,768]{1,0:T(8,128)(2,1)S(1)}, u32[]{:S(2)}) copy-start(bf16[136,768]{1,0:T(8,128)(2,1)S(1)} %collective-permute-done.refs_1_) | copy-start | bytes 626692
  21.3 5.4 %copy-start.21 = (bf16[136,768]{1,0:T(8,128)(2,1)}, bf16[136,768]{1,0:T(8,128)(2,1)S(1)}, u32[]{:S(2)}) copy-start(bf16[136,768]{1,0:T(8,128)(2,1)S(1)} %collective-permute-done.1.refs_2_) | copy-start | bytes 626692
  31.6 22.4 %collective-permute-start.3 = (bf16[512,896]{1,0:T(8,128)(2,1)}, bf16[512,896]{1,0:T(8,128)(2,1)}, u32[]{:S(2)}, u32[]{:S(2)}) collective-permute-start(bf16[512,896]{1,0:T(8,128)(2,1)} %bitcast.3), channel_id=1, source_target_pairs={{0,1},{1,2},{2,3},{3,0},{4,5},{5,6},{6,7},{7,4},{8,9},{9,10},{10,1... | collective-permute-start | bytes 2752520 | tf_op jit(solution)/shard_map/ppermute | solution.py:217
  32.2 22.8 %collective-permute-start.4 = (bf16[512,896]{1,0:T(8,128)(2,1)}, bf16[512,896]{1,0:T(8,128)(2,1)}, u32[]{:S(2)}, u32[]{:S(2)}) collective-permute-start(bf16[512,896]{1,0:T(8,128)(2,1)} %bitcast.3), channel_id=1, source_target_pairs={{0,3},{1,0},{2,1},{3,2},{4,7},{5,4},{6,5},{7,6},{8,11},{9,8},{10,9... | collective-permute-start | bytes 2752520 | tf_op jit(solution)/shard_map/ppermute | solution.py:218
  37.4 49.2 %all-to-all-start.1 = ((bf16[32,64,768]{2,1,0:T(8,128)(2,1)}), bf16[32,64,768]{2,1,0:T(8,128)(2,1)S(1)}, u32[]{:S(2)}, u32[]{:S(2)}) async-start(bf16[32,64,768]{2,1,0:T(8,128)(2,1)} %bitcast.58), calls=%async_computation.1 | async-start | bytes 6291456 | tf_op jit(solution)/shard_map/all_to_all | solution.py:171
  56.1 8.5 %copy-start.3 = (bf16[512,768]{1,0:T(8,128)(2,1)S(1)}, bf16[512,768]{1,0:T(8,128)(2,1)}, u32[]{:S(2)}) copy-start(bf16[512,768]{1,0:T(8,128)(2,1)} %slice.143) | copy-start | bytes 2359300
  56.1 8.5 %copy-start.8 = (bf16[2,1024,768]{2,1,0:T(8,128)(2,1)S(1)}, bf16[2,1024,768]{2,1,0:T(8,128)(2,1)}, u32[]{:S(2)}) copy-start(bf16[2,1024,768]{2,1,0:T(8,128)(2,1)} %w_ref.1) | copy-start | bytes 9437188
  57.3 17.5 %collective-permute-start.5 = (bf16[256,896]{1,0:T(8,128)(2,1)S(1)}, bf16[256,896]{1,0:T(8,128)(2,1)S(1)}, u32[]{:S(2)}, u32[]{:S(2)}) collective-permute-start(bf16[256,896]{1,0:T(8,128)(2,1)S(1)} %slice.191), channel_id=1, source_target_pairs={{0,1},{1,2},{2,3},{3,0},{4,5},{5,6},{6,7},{7,4},{8,9},{9,10},{10,1... | collective-permute-start | bytes 1376264 | tf_op jit(solution)/shard_map/ppermute | solution.py:219
  59.3 16.5 %collective-permute-start.6 = (bf16[256,896]{1,0:T(8,128)(2,1)}, bf16[256,896]{1,0:T(8,128)(2,1)}, u32[]{:S(2)}, u32[]{:S(2)}) collective-permute-start(bf16[256,896]{1,0:T(8,128)(2,1)} %slice.193), channel_id=1, source_target_pairs={{0,3},{1,0},{2,1},{3,2},{4,7},{5,4},{6,5},{7,6},{8,11},{9,8},{10,9... | collective-permute-start | bytes 1376264 | tf_op jit(solution)/shard_map/ppermute | solution.py:220
  63.1 7.2 %copy-start.5 = (bf16[512,768]{1,0:T(8,128)(2,1)}, bf16[512,768]{1,0:T(8,128)(2,1)S(1)}, u32[]{:S(2)}) copy-start(bf16[512,768]{1,0:T(8,128)(2,1)S(1)} %slice.183) | copy-start | bytes 2359300
  64.6 5.7 %copy-start.7 = (bf16[512,768]{1,0:T(8,128)(2,1)}, bf16[512,768]{1,0:T(8,128)(2,1)S(1)}, u32[]{:S(2)}) copy-start(bf16[512,768]{1,0:T(8,128)(2,1)S(1)} %slice.184) | copy-start | bytes 2359300
  79.0 2.9 %copy-start.14 = (bf16[256,768]{1,0:T(8,128)(2,1)}, bf16[256,768]{1,0:T(8,128)(2,1)S(1)}, u32[]{:S(2)}) copy-start(bf16[256,768]{1,0:T(8,128)(2,1)S(1)} %slice.194) | copy-start | bytes 1179652
  79.0 2.9 %copy-start.9 = (bf16[2,1024,768]{2,1,0:T(8,128)(2,1)S(1)}, bf16[2,1024,768]{2,1,0:T(8,128)(2,1)}, u32[]{:S(2)}) copy-start(bf16[2,1024,768]{2,1,0:T(8,128)(2,1)} %w_ref.1) | copy-start | bytes 9437188
  83.9 13.9 %collective-permute-start.7 = (bf16[256,768]{1,0:T(8,128)(2,1)}, bf16[256,768]{1,0:T(8,128)(2,1)}, u32[]{:S(2)}, u32[]{:S(2)}) collective-permute-start(bf16[256,768]{1,0:T(8,128)(2,1)} %get-tuple-element.25), channel_id=1, source_target_pairs={{0,1},{1,2},{2,3},{3,0},{4,5},{5,6},{6,7},{7,4},{8,9},{9,10},{10,1... | collective-permute-start | bytes 1179656 | tf_op jit(solution)/shard_map/ppermute | solution.py:184
  83.9 13.9 %collective-permute-start.9 = (bf16[256,768]{1,0:T(8,128)(2,1)}, bf16[256,768]{1,0:T(8,128)(2,1)}, u32[]{:S(2)}, u32[]{:S(2)}) collective-permute-start(bf16[256,768]{1,0:T(8,128)(2,1)} %get-tuple-element.26), channel_id=1, source_target_pairs={{0,3},{1,0},{2,1},{3,2},{4,7},{5,4},{6,5},{7,6},{8,11},{9,8},{10,9... | collective-permute-start | bytes 1179656 | tf_op jit(solution)/shard_map/ppermute | solution.py:185
  86.5 7.2 %copy-start = (bf16[32,64,768]{2,1,0:T(8,128)(2,1)}, bf16[32,64,768]{2,1,0:T(8,128)(2,1)S(1)}, u32[]{:S(2)}) copy-start(bf16[32,64,768]{2,1,0:T(8,128)(2,1)S(1)} %all-to-all-done.1) | copy-start | bytes 9437188
  86.6 7.2 %copy-start.10 = (bf16[2,1024,768]{2,1,0:T(8,128)(2,1)S(1)}, bf16[2,1024,768]{2,1,0:T(8,128)(2,1)}, u32[]{:S(2)}) copy-start(bf16[2,1024,768]{2,1,0:T(8,128)(2,1)} %w_ref.1) | copy-start | bytes 9437188
  93.7 3.6 %copy-start.2 = (bf16[2048,1024]{1,0:T(8,128)(2,1)}, bf16[2048,1024]{1,0:T(8,128)(2,1)S(1)}, u32[]{:S(2)}) copy-start(bf16[2048,1024]{1,0:T(8,128)(2,1)S(1)} %subtract_convert_fusion.gb_ref) | copy-start | bytes 12582916
  97.6 5.6 %copy-start.16 = (bf16[256,768]{1,0:T(8,128)(2,1)S(1)}, bf16[256,768]{1,0:T(8,128)(2,1)}, u32[]{:S(2)}) copy-start(bf16[256,768]{1,0:T(8,128)(2,1)} %get-tuple-element.24) | copy-start | bytes 1179652
  97.6 8.9 %collective-permute-start.11 = (bf16[256,768]{1,0:T(8,128)(2,1)S(1)}, bf16[256,768]{1,0:T(8,128)(2,1)S(1)}, u32[]{:S(2)}, u32[]{:S(2)}) collective-permute-start(bf16[256,768]{1,0:T(8,128)(2,1)S(1)} %bitcast.68), channel_id=1, source_target_pairs={{0,1},{1,2},{2,3},{3,0},{4,5},{5,6},{6,7},{7,4},{8,9},{9,10},{10,1... | collective-permute-start | bytes 1179656 | tf_op jit(solution)/shard_map/ppermute | solution.py:184
  100.4 23.0 %collective-permute-start.8 = (bf16[512,768]{1,0:T(8,128)(2,1)S(1)}, bf16[512,768]{1,0:T(8,128)(2,1)S(1)}, u32[]{:S(2)}, u32[]{:S(2)}) collective-permute-start(bf16[512,768]{1,0:T(8,128)(2,1)S(1)} %pad_maximum_fusion.3), channel_id=1, source_target_pairs={{0,1},{1,2},{2,3},{3,0},{4,5},{5,6},{6,7},{7,4},{8,9},{9,10},{10,1... | collective-permute-start | bytes 2359304 | tf_op jit(solution)/shard_map/ppermute | solution.py:188
  100.5 7.8 %collective-permute-start.13 = (bf16[256,768]{1,0:T(8,128)(2,1)S(1)}, bf16[256,768]{1,0:T(8,128)(2,1)S(1)}, u32[]{:S(2)}, u32[]{:S(2)}) collective-permute-start(bf16[256,768]{1,0:T(8,128)(2,1)S(1)} %bitcast.67), channel_id=1, source_target_pairs={{0,3},{1,0},{2,1},{3,2},{4,7},{5,4},{6,5},{7,6},{8,11},{9,8},{10,9... | collective-permute-start | bytes 1179656 | tf_op jit(solution)/shard_map/ppermute | solution.py:185
  103.2 21.9 %collective-permute-start.10 = (bf16[512,768]{1,0:T(8,128)(2,1)S(1)}, bf16[512,768]{1,0:T(8,128)(2,1)S(1)}, u32[]{:S(2)}, u32[]{:S(2)}) collective-permute-start(bf16[512,768]{1,0:T(8,128)(2,1)S(1)} %pad_maximum_fusion.4), channel_id=1, source_target_pairs={{0,3},{1,0},{2,1},{3,2},{4,7},{5,4},{6,5},{7,6},{8,11},{9,8},{10,9... | collective-permute-start | bytes 2359304 | tf_op jit(solution)/shard_map/ppermute | solution.py:189
  106.8 33.5 %collective-permute-start.12 = (bf16[512,768]{1,0:T(8,128)(2,1)S(1)}, bf16[512,768]{1,0:T(8,128)(2,1)S(1)}, u32[]{:S(2)}, u32[]{:S(2)}) collective-permute-start(bf16[512,768]{1,0:T(8,128)(2,1)S(1)} %pad_maximum_fusion.5), channel_id=1, source_target_pairs={{0,1},{1,2},{2,3},{3,0},{4,5},{5,6},{6,7},{7,4},{8,9},{9,10},{10,1... | collective-permute-start | bytes 2359304 | tf_op jit(solution)/shard_map/ppermute | solution.py:188
  108.5 33.5 %collective-permute-start.14 = (bf16[512,768]{1,0:T(8,128)(2,1)S(1)}, bf16[512,768]{1,0:T(8,128)(2,1)S(1)}, u32[]{:S(2)}, u32[]{:S(2)}) collective-permute-start(bf16[512,768]{1,0:T(8,128)(2,1)S(1)} %pad_maximum_fusion.6), channel_id=1, source_target_pairs={{0,3},{1,0},{2,1},{3,2},{4,7},{5,4},{6,5},{7,6},{8,11},{9,8},{10,9... | collective-permute-start | bytes 2359304 | tf_op jit(solution)/shard_map/ppermute | solution.py:189
  143.7 10.9 %copy-start.4 = (bf16[512,768]{1,0:T(8,128)(2,1)S(1)}, bf16[512,768]{1,0:T(8,128)(2,1)}, u32[]{:S(2)}) copy-start(bf16[512,768]{1,0:T(8,128)(2,1)} %slice.143) | copy-start | bytes 2359300
  143.7 10.9 %copy-start.6 = (bf16[512,768]{1,0:T(8,128)(2,1)S(1)}, bf16[512,768]{1,0:T(8,128)(2,1)}, u32[]{:S(2)}) copy-start(bf16[512,768]{1,0:T(8,128)(2,1)} %copy-done.5) | copy-start | bytes 2359300
  143.7 33.6 %all-to-all-start.2 = ((bf16[32,16,1536]{2,1,0:T(8,128)(2,1)}), bf16[32,16,1536]{2,1,0:T(8,128)(2,1)S(1)}, u32[]{:S(2)}, u32[]{:S(2)}) async-start(bf16[32,16,1536]{2,1,0:T(8,128)(2,1)} %bitcast.18), calls=%async_computation.2 | async-start | bytes 3145728 | tf_op jit(solution)/shard_map/all_to_all | solution.py:171
  (9 other events, 15.5 us)

commit v4 on v3

--- a/solution.py
+++ b/solution.py
@@ -107,7 +107,10 @@
     out_ref[...] = total
 
 
-def update_kernel(gn_ref, gf_ref, gb_ref, rn_ref, rf_ref, rb_ref, w_ref, m_ref, wo_ref, mo_ref):
+def update_kernel(*refs):
+    ga, gb, ra, rb = refs[:LAB], refs[LAB], refs[LAB + 1 : 2 * LAB + 1], refs[2 * LAB + 1]
+    w_ref, m_ref, wo_ref, mo_ref = refs[2 * LAB + 2 :]
+
     def apply(pairs):
         fresh = momentum_decay * m_ref[0]
         for grad_ref, rows_ref in pairs:
@@ -122,11 +125,11 @@
 
     @pl.when(pl.program_id(0) == 0)
     def _():
-        apply(((gn_ref, rn_ref), (gf_ref, rf_ref)))
+        apply(tuple(zip(ga, ra)))
 
     @pl.when(pl.program_id(0) == 1)
     def _():
-        apply(((gb_ref, rb_ref),))
+        apply(((gb, rb),))
 
 
 def update(grad_a, grad_b, rows_a, rows_b, weights, momentum):
@@ -214,30 +217,31 @@
     got_b = swap(box_b.reshape(CLUS, LAB * CAP, D)).reshape(LAB * ROWS, D)
 
     half = ROWS // 2
-    from_low = lax.ppermute(got_a, "lab", ring(1))
-    from_high = lax.ppermute(got_a, "lab", ring(-1))
-    far_low = lax.ppermute(from_low[:half], "lab", ring(1))
-    far_high = lax.ppermute(from_high[half:], "lab", ring(-1))
-    near, far = (got_a, from_low, from_high), (far_low, far_high)
-    rows_a = [jnp.concatenate([p[:, :D] for p in ps]) for ps in (near, far)]
-    notes = [jnp.concatenate([p[:, D : D + 4] for p in ps]).astype(jnp.int32) for ps in (near, far)]
-    tag_a = [x[:, 0:1] * 64 + x[:, 1:2] for x in notes]
-    tag_b = jnp.concatenate([x[:, 2:3] * 64 + x[:, 3:4] for x in notes])
-    tag_b = jnp.moveaxis(tag_b.reshape(LAB, CLUS, CAP), 0, 1).reshape(LAB * ROWS, 1)
-
+    low_a = lax.ppermute(got_a[:half], "lab", ring(1))
+    high_b = lax.ppermute(got_a[half:], "lab", ring(-1))
+    low_b = lax.ppermute(got_a[half:], "lab", ring(1))
+    high_a = lax.ppermute(got_a[:half], "lab", ring(-1))
+    far_a = lax.ppermute(low_a, "lab", ring(1))
+    far_b = lax.ppermute(high_b, "lab", ring(-1))
+    blocks = ((got_a,), (low_a, low_b), (high_a, high_b), (far_a, far_b))
     offsets = me * LABELS + jnp.arange(LABELS, dtype=jnp.int32)
-    grad_far, part_far = grads(rows_a[1], tag_a[1], weights[0], offsets)
-    grad_near, part_near = grads(rows_a[0], tag_a[0], weights[0], offsets)
-    part_near = part_near.reshape(LAB - 1, ROWS, D)
-    home_a = ring_sum((part_near[0], part_near[1], part_near[2], part_far))
+    rows_a, grads_a, parts_a, tags_b = [], [], [], []
+    for block in blocks:
+        rows = jnp.concatenate([p[:, :D] for p in block])
+        notes = jnp.concatenate([p[:, D : D + 4] for p in block]).astype(jnp.int32)
+        grad, part = grads(rows, notes[:, 0:1] * 64 + notes[:, 1:2], weights[0], offsets)
+        rows_a.append(rows)
+        grads_a.append(grad)
+        parts_a.append(part)
+        tags_b.append((notes[:, 2] * 64 + notes[:, 3]).reshape(CLUS, CAP))
+    tag_b = jnp.stack(tags_b, axis=1).reshape(LAB * ROWS, 1)
+    home_a = ring_sum(parts_a)
     grad_b, part_b = grads(got_b, tag_b, weights[1], offsets)
     part_b = part_b.reshape(CLUS, LAB, CAP, D)
     home_b = ring_sum([part_b[:, k].reshape(ROWS, D) for k in range(LAB)])
     both = jnp.concatenate([home_a, home_b], axis=1).reshape(CLUS, CAP, 2 * D)
     both = swap(both).reshape(ROWS, 2 * D)
-    weights_new, momentum_new = update(
-        (grad_near, grad_far), grad_b, rows_a, got_b, weights, momentum
-    )
+    weights_new, momentum_new = update(grads_a, grad_b, rows_a, got_b, weights, momentum)
     query_grad = pl.pallas_call(
         home_kernel, out_shape=jax.ShapeDtypeStruct((NQ, D), jnp.float32), name="home_sum"
     )(vt, both)

time: 182 us -> 206 us (1.13)
  local copies, waits for them, and re-layouts: 21.1 us -> 36.2 us
  other arithmetic: 7.66 us -> 14 us
  matrix products: 23.1 us -> 25.5 us
    slice x17 -> x22, local copies, waits for them, and re-layouts: 13.9 us -> 24.9 us  [the longest x12 15 us: step(): notes = jnp.concatenate([p[:, D:D + 4] for p in block]).astype(jnp.int32)]
    ppermute x2, waiting for transfers between devices: 3.1 us -> 7.88 us  [ring_sum(): up = lax.ppermute(far[:half], 'lab', ring(1))]
    add x0 -> x4, local copies, waits for them, and re-layouts: none -> 4.16 us  [step(): tags_b.append((notes[:, 2] * 64 + notes[:, 3]).reshape(CLUS, CAP))]
    add x2 -> x3, other arithmetic: 0.05 us -> 3.62 us  [step(): notes[:, 0:1] * 64 + notes[:, 1:2]]
    ppermute x4 -> x6, waiting for transfers between devices: 7.98 us -> 5.3 us  [the longest x1 5.29 us: step(): high_a = lax.ppermute(got_a[:half], 'lab', ring(-1))]
    all_to_all x3, starting transfers between devices: 28.1 us -> 25.9 us  [swap(): return lax.all_to_all(x, 'clus', split_axis=0, concat_axis=0, tiled=True)]
    dot_general x3 -> x5, matrix products: 7.41 us -> 9.31 us  [grads(): jnp.einsum('rb,bd->rd', grad, weights, preferred_element_type=jnp.float32)]
    ppermute x4 -> x6, starting transfers between devices: 5.41 us -> 7.15 us  [the longest x1 3.41 us: step(): far_b = lax.ppermute(high_b, 'lab', ring(-1))]
  transfers between devices with their start and end apart: 18 -> 20, of which waited for: 10 -> 11; matrix products, arithmetic and copies ran while one was open for 25% -> 33% of each run, Pallas kernels for 12% -> 10%
where the time goes in v4:
time: 206 us; the launch traced here: 204 us
  waiting for transfers between devices  53 us (26%)
  starting transfers between devices  48 us (23%)
  local copies, waits for them, and re-layouts  36.2 us (18%)
  Pallas kernels  26.6 us (13%)
  matrix products  25.5 us (12%)
  other arithmetic  14 us (7%)
    all_to_all x3, starting transfers between devices, swap(): return lax.all_to_all(x, 'clus', split_axis=0, concat_axis=0, tiled=True)  25.9 us
    ppermute x2, waiting for transfers between devices, ring_sum(): up = lax.ppermute(up, 'lab', ring(1))  25.5 us
    pallas_call x1, Pallas kernels, update(): pl.pallas_call(update_kernel, grid=(2, bands), in_specs=[first(g) for g i...  17 us
    dot_general x5, matrix products, grads(): jnp.einsum('rd,bd->rb', rows, weights, preferred_element_type=jnp.float32)  16.2 us
    slice x12, local copies, waits for them, and re-layouts, step(): notes = jnp.concatenate([p[:, D:D + 4] for p in block]).astype(jnp.int32)  15 us
    ppermute x3, waiting for transfers between devices, step(): peers = [raw] + [lax.ppermute(raw, 'lab', ring(s)) for s in (1, -1, 2)]  9.58 us
    dot_general x5, matrix products, grads(): jnp.einsum('rb,bd->rd', grad, weights, preferred_element_type=jnp.float32)  9.31 us
    slice x7, local copies, waits for them, and re-layouts, step(): rows = jnp.concatenate([p[:, :D] for p in block])  8.76 us
  transfers between devices with their start and end apart: 20, of which 11 were waited for; matrix products, arithmetic and copies ran while one was open for 33% of the time, Pallas kernels for 10%

profile of v4, /device:TPU:1, one launch (start us, length us, event | category | flops | bytes accessed | tf_op | source)
XLA Modules:
  0.0 204.5 jit_solution(13469427352016889535)
XLA Ops:
  0.6 2.6 %own_box.1 = (bf16[512,896]{1,0:T(8,128)(2,1)}, bf16[136,768]{1,0:T(8,128)(2,1)}) custom-call(s32[4,128]{1,0:T(4,128)} %bitcast.92, s32[4,128]{1,0:T(4,128)} %bitcast.94, bf16[128,768]{1,0:T(8,128)(2,1)} %queries_ref.1), custom_call_target="tpu_custom_call" | custom-call | tf_op jit(solution)/shard_map/own_box/pallas_call | solution.py:201
  3.2 8.6 %all-to-all-start = ((bf16[32,16,896]{2,1,0:T(8,128)(2,1)}), bf16[32,16,896]{2,1,0:T(8,128)(2,1)S(1)}, u32[]{:S(2)}, u32[]{:S(2)}) async-start(bf16[32,16,896]{2,1,0:T(8,128)(2,1)} %bitcast.89), calls=%async_computation | async-start | bytes 1835008 | tf_op jit(solution)/shard_map/all_to_all | solution.py:174
  11.8 1.7 collective-permute-start
  13.5 2.2 %collective-permute-start.1 = (bf16[136,768]{1,0:T(8,128)(2,1)}, bf16[136,768]{1,0:T(8,128)(2,1)S(1)}, u32[]{:S(2)}, u32[]{:S(2)}) collective-permute-start(bf16[136,768]{1,0:T(8,128)(2,1)} %get-tuple-element.10.refs_0_), channel_id=1, source_target_pairs={{0,3},{1,0},{2,1},{3,2},{4,7},{5,4},{6,5},{7,6},{8,11},{9,8},{10,9... | collective-permute-start | bytes 626696 | tf_op jit(solution)/shard_map/ppermute | solution.py:209
  17.0 4.2 %collective-permute-done.refs_1_ = bf16[136,768]{1,0:T(8,128)(2,1)S(1)} collective-permute-done((bf16[136,768]{1,0:T(8,128)(2,1)}, bf16[136,768]{1,0:T(8,128)(2,1)S(1)}, u32[]{:S(2)}, u32[]{:S(2)}) %collective-permute-start) | collective-permute-done | bytes 208928 | tf_op jit(solution)/shard_map/ppermute | solution.py:209
  21.2 5.4 %collective-permute-done.2.refs_3_ = bf16[136,768]{1,0:T(8,128)(2,1)S(1)} collective-permute-done((bf16[136,768]{1,0:T(8,128)(2,1)}, bf16[136,768]{1,0:T(8,128)(2,1)S(1)}, u32[]{:S(2)}, u32[]{:S(2)}) %collective-permute-start.2) | collective-permute-done | bytes 208928 | tf_op jit(solution)/shard_map/ppermute | solution.py:209
  27.2 4.3 %all_box.1 = bf16[32,4,16,768]{3,2,1,0:T(8,128)(2,1)} custom-call(bf16[136,768]{1,0:T(8,128)(2,1)} %get-tuple-element.10.refs_0_, bf16[136,768]{1,0:T(8,128)(2,1)} %copy-done.25, bf16[136,768]{1,0:T(8,128)(2,1)} %copy-done.26, bf16[136,768]{1,0:T(8,128)(2,1)} %copy-done.27), custom_call_target="tpu_custom_call" | custom-call | tf_op jit(solution)/shard_map/all_box/pallas_call | solution.py:211
  32.6 2.2 %collective-permute-start.4 = (bf16[256,896]{1,0:T(8,128)(2,1)}, bf16[256,896]{1,0:T(8,128)(2,1)}, u32[]{:S(2)}, u32[]{:S(2)}) collective-permute-start(bf16[256,896]{1,0:T(8,128)(2,1)} %get-tuple-element.24), channel_id=1, source_target_pairs={{0,3},{1,0},{2,1},{3,2},{4,7},{5,4},{6,5},{7,6},{8,11},{9,8},{10,9... | collective-permute-start | bytes 1376264 | tf_op jit(solution)/shard_map/ppermute | solution.py:221
  38.0 8.9 %all-to-all-start.1 = ((bf16[32,64,768]{2,1,0:T(8,128)(2,1)}), bf16[32,64,768]{2,1,0:T(8,128)(2,1)S(1)}, u32[]{:S(2)}, u32[]{:S(2)}) async-start(bf16[32,64,768]{2,1,0:T(8,128)(2,1)} %bitcast.8), calls=%async_computation.1 | async-start | bytes 6291456 | tf_op jit(solution)/shard_map/all_to_all | solution.py:174
  48.5 5.3 %collective-permute-done.3 = bf16[256,896]{1,0:T(8,128)(2,1)} collective-permute-done((bf16[256,896]{1,0:T(8,128)(2,1)}, bf16[256,896]{1,0:T(8,128)(2,1)}, u32[]{:S(2)}, u32[]{:S(2)}) %collective-permute-start.3) | collective-permute-done | bytes 458784 | tf_op jit(solution)/shard_map/ppermute | solution.py:223
  55.3 3.4 %collective-permute-start.7 = (bf16[256,896]{1,0:T(8,128)(2,1)}, bf16[256,896]{1,0:T(8,128)(2,1)}, u32[]{:S(2)}, u32[]{:S(2)}) collective-permute-start(bf16[256,896]{1,0:T(8,128)(2,1)} %collective-permute-done.4), channel_id=1, source_target_pairs={{0,3},{1,0},{2,1},{3,2},{4,7},{5,4},{6,5},{7,6},{8,11},{9,8},{10,9... | collective-permute-start | bytes 1376264 | tf_op jit(solution)/shard_map/ppermute | solution.py:225
  62.2 3.7 %subtract_convert_fusion.3.refs_2_ = bf16[512,1024]{1,0:T(8,128)(2,1)} fusion(s32[1024]{0:T(1024)} %iota_add_fusion, s32[512]{0:T(512)S(1)} %bitcast.97, bf16[2,1024,768]{2,1,0:T(8,128)(2,1)} %refs_10_.1, bf16[256,768]{1,0:T(8,128)(2,1)S(1)} %slice.223, bf16[256,768]{1,0:T(8,128)(2,1)S(1)} %slice.222), kind=kOutput, calls=%fused_computation.4 | convolution fusion | flops 810549248 | bytes 3414016 | tf_op jit(solution)/shard_map/rd,bd->rb/dot_general | solution.py:166
  70.3 1.5 copy.61
  73.2 2.7 %fusion.19 = bf16[512,768]{1,0:T(8,128)(2,1)S(1)} fusion(bf16[512,1024]{1,0:T(8,128)(2,1)} %subtract_convert_fusion.3.refs_2_, bf16[2,1024,768]{2,1,0:T(8,128)(2,1)} %refs_10_.1), kind=kOutput, calls=%fused_computation.26 | convolution fusion | flops 805699584 | bytes 3407872 | tf_op jit(solution)/shard_map/rb,bd->rd/dot_general | solution.py:169
  76.9 1.8 slice.237
  78.6 1.8 slice.238
  85.5 1.5 copy.59
  87.7 2.0 %slice_add_fusion.5 = (s32[512,1]{0,1:T(1,128)}, s32[512]{0:T(512)}, s32[512]{0:T(512)}, s32[512,1]{0,1:T(1,128)}) fusion(s32[512,4]{0,1:T(4,128)} %maximum_convert_fusion.2, s32[512,4]{0,1:T(4,128)S(1)} %maximum_convert_fusion.1), kind=kLoop, calls=%fused_computation.73 | loop fusion | flops 4096 | bytes 24576 | tf_op jit(solution)/shard_map/add | solution.py:232
  97.8 2.8 %subtract_convert_fusion.2.refs_3_ = bf16[512,1024]{1,0:T(8,128)(2,1)S(1)} fusion(s32[1024]{0:T(1024)} %iota_add_fusion, s32[512]{0:T(512)} %bitcast.96, bf16[2,1024,768]{2,1,0:T(8,128)(2,1)} %refs_10_.1, bf16[256,768]{1,0:T(8,128)(2,1)S(1)} %slice.230, bf16[256,768]{1,0:T(8,128)(2,1)S(1)} %slice.229), kind=kOutput, calls=%fused_computation.3 | convolution fusion | flops 810549248 | bytes 3414016 | tf_op jit(solution)/shard_map/rd,bd->rb/dot_general | solution.py:166
  102.5 2.7 %collective-permute-start.11 = (bf16[256,768]{1,0:T(8,128)(2,1)}, bf16[256,768]{1,0:T(8,128)(2,1)}, u32[]{:S(2)}, u32[]{:S(2)}) collective-permute-start(bf16[256,768]{1,0:T(8,128)(2,1)} %get-tuple-element.26), channel_id=1, source_target_pairs={{0,3},{1,0},{2,1},{3,2},{4,7},{5,4},{6,5},{7,6},{8,11},{9,8},{10,9... | collective-permute-start | bytes 1179656 | tf_op jit(solution)/shard_map/ppermute | solution.py:188
  107.5 4.7 %collective-permute-done.8 = bf16[256,768]{1,0:T(8,128)(2,1)S(1)} collective-permute-done((bf16[256,768]{1,0:T(8,128)(2,1)S(1)}, bf16[256,768]{1,0:T(8,128)(2,1)S(1)}, u32[]{:S(2)}, u32[]{:S(2)}) %collective-permute-start.8) | collective-permute-done | bytes 393248 | tf_op jit(solution)/shard_map/ppermute | solution.py:187
  113.0 7.2 %subtract_convert_fusion.refs_4_ = bf16[2048,1024]{1,0:T(8,128)(2,1)S(1)} fusion(bf16[2048,768]{1,0:T(8,128)(2,1)S(1)} %bitcast.77, s32[1024]{0:T(1024)S(1)} %copy-done.30, s32[2048]{0:T(1024)S(1)} %eq.82, bf16[2,1024,768]{2,1,0:T(8,128)(2,1)} %refs_10_.1), kind=kOutput, calls=%fused_computation | convolution fusion | flops 3235905536 | bytes 8925184 | tf_op jit(solution)/shard_map/rd,bd->rb/dot_general | solution.py:166
  120.2 3.6 %convolution_convert_fusion = bf16[2048,768]{1,0:T(8,128)(2,1)S(1)} fusion(bf16[2048,1024]{1,0:T(8,128)(2,1)S(1)} %subtract_convert_fusion.refs_4_, bf16[2,1024,768]{2,1,0:T(8,128)(2,1)S(1)} %copy-done.6), kind=kOutput, calls=%fused_computation.1 | convolution fusion | flops 3222798336 | bytes 8912896 | tf_op jit(solution)/shard_map/rb,bd->rd/dot_general | solution.py:169
  126.3 2.6 %collective-permute-start.15 = (bf16[256,768]{1,0:T(8,128)(2,1)S(1)}, bf16[256,768]{1,0:T(8,128)(2,1)S(1)}, u32[]{:S(2)}, u32[]{:S(2)}) collective-permute-start(bf16[256,768]{1,0:T(8,128)(2,1)S(1)} %bitcast.90), channel_id=1, source_target_pairs={{0,3},{1,0},{2,1},{3,2},{4,7},{5,4},{6,5},{7,6},{8,11},{9,8},{10,9... | collective-permute-start | bytes 1179656 | tf_op jit(solution)/shard_map/ppermute | solution.py:188
  129.8 3.2 %collective-permute-done.13 = bf16[256,768]{1,0:T(8,128)(2,1)S(1)} collective-permute-done((bf16[256,768]{1,0:T(8,128)(2,1)S(1)}, bf16[256,768]{1,0:T(8,128)(2,1)S(1)}, u32[]{:S(2)}, u32[]{:S(2)}) %collective-permute-start.13) | collective-permute-done | bytes 393248 | tf_op jit(solution)/shard_map/ppermute | solution.py:187
  134.2 3.5 %collective-permute-start.16 = (bf16[512,768]{1,0:T(8,128)(2,1)S(1)}, bf16[512,768]{1,0:T(8,128)(2,1)S(1)}, u32[]{:S(2)}, u32[]{:S(2)}) collective-permute-start(bf16[512,768]{1,0:T(8,128)(2,1)S(1)} %pad_maximum_fusion.7), channel_id=1, source_target_pairs={{0,3},{1,0},{2,1},{3,2},{4,7},{5,4},{6,5},{7,6},{8,11},{9,8},{10,9... | collective-permute-start | bytes 2359304 | tf_op jit(solution)/shard_map/ppermute | solution.py:192
  139.0 10.8 %collective-permute-done.9 = bf16[512,768]{1,0:T(8,128)(2,1)S(1)} collective-permute-done((bf16[512,768]{1,0:T(8,128)(2,1)S(1)}, bf16[512,768]{1,0:T(8,128)(2,1)S(1)}, u32[]{:S(2)}, u32[]{:S(2)}) %collective-permute-start.9) | collective-permute-done | bytes 786464 | tf_op jit(solution)/shard_map/ppermute | solution.py:191
  152.0 14.7 %collective-permute-done.14 = bf16[512,768]{1,0:T(8,128)(2,1)S(1)} collective-permute-done((bf16[512,768]{1,0:T(8,128)(2,1)S(1)}, bf16[512,768]{1,0:T(8,128)(2,1)S(1)}, u32[]{:S(2)}, u32[]{:S(2)}) %collective-permute-start.14) | collective-permute-done | bytes 786464 | tf_op jit(solution)/shard_map/ppermute | solution.py:191
  169.5 8.4 %all-to-all-start.2 = ((bf16[32,16,1536]{2,1,0:T(8,128)(2,1)}), bf16[32,16,1536]{2,1,0:T(8,128)(2,1)S(1)}, u32[]{:S(2)}, u32[]{:S(2)}) async-start(bf16[32,16,1536]{2,1,0:T(8,128)(2,1)} %bitcast.84), calls=%async_computation.2 | async-start | bytes 3145728 | tf_op jit(solution)/shard_map/all_to_all | solution.py:174
  181.8 17.0 %update.1 = (bf16[2,1024,768]{2,1,0:T(8,128)(2,1)}, f32[2,1024,768]{2,1,0:T(8,128)}) custom-call(bf16[512,1024]{1,0:T(8,128)(2,1)} %copy-done.24, bf16[512,1024]{1,0:T(8,128)(2,1)} %copy-done.23, bf16[512,1024]{1,0:T(8,128)(2,1)} %subtract_convert_fusion.3.refs_2_, bf16[512,1024]{1,0:T(8,128)(2,1)} %copy-done.22, bf16[2048,1024]{1,0:T(8,128)(2,1)} %copy-done.4, ...), custom_call_target="tpu_custom_call" | custom-call | flops 6442450944 | bytes 37748736 | tf_op jit(solution)/shard_map/update/pallas_call | solution.py:143
  198.8 1.8 all-to-all-done.2
  201.8 2.7 %home_sum.1 = f32[128,768]{1,0:T(8,128)} custom-call(s32[4,128]{1,0:T(4,128)} %bitcast.93, bf16[512,1536]{1,0:T(8,128)(2,1)} %bitcast.83), custom_call_target="tpu_custom_call" | custom-call | tf_op jit(solution)/shard_map/home_sum/pallas_call | solution.py:245
  (143 shorter events, 53.7 us)
Async XLA Ops:
  3.2 28.3 %all-to-all-start = ((bf16[32,16,896]{2,1,0:T(8,128)(2,1)}), bf16[32,16,896]{2,1,0:T(8,128)(2,1)S(1)}, u32[]{:S(2)}, u32[]{:S(2)}) async-start(bf16[32,16,896]{2,1,0:T(8,128)(2,1)} %bitcast.89), calls=%async_computation | async-start | bytes 1835008 | tf_op jit(solution)/shard_map/all_to_all | solution.py:174
  11.8 9.3 %collective-permute-start = (bf16[136,768]{1,0:T(8,128)(2,1)}, bf16[136,768]{1,0:T(8,128)(2,1)S(1)}, u32[]{:S(2)}, u32[]{:S(2)}) collective-permute-start(bf16[136,768]{1,0:T(8,128)(2,1)} %get-tuple-element.10.refs_0_), channel_id=1, source_target_pairs={{0,1},{1,2},{2,3},{3,0},{4,5},{5,6},{6,7},{7,4},{8,9},{9,10},{10,1... | collective-permute-start | bytes 626696 | tf_op jit(solution)/shard_map/ppermute | solution.py:209
  13.5 7.6 %collective-permute-start.1 = (bf16[136,768]{1,0:T(8,128)(2,1)}, bf16[136,768]{1,0:T(8,128)(2,1)S(1)}, u32[]{:S(2)}, u32[]{:S(2)}) collective-permute-start(bf16[136,768]{1,0:T(8,128)(2,1)} %get-tuple-element.10.refs_0_), channel_id=1, source_target_pairs={{0,3},{1,0},{2,1},{3,2},{4,7},{5,4},{6,5},{7,6},{8,11},{9,8},{10,9... | collective-permute-start | bytes 626696 | tf_op jit(solution)/shard_map/ppermute | solution.py:209
  15.7 10.8 %collective-permute-start.2 = (bf16[136,768]{1,0:T(8,128)(2,1)}, bf16[136,768]{1,0:T(8,128)(2,1)S(1)}, u32[]{:S(2)}, u32[]{:S(2)}) collective-permute-start(bf16[136,768]{1,0:T(8,128)(2,1)} %get-tuple-element.10.refs_0_), channel_id=1, source_target_pairs={{0,2},{1,3},{2,0},{3,1},{4,6},{5,7},{6,4},{7,5},{8,10},{9,11},{10,... | collective-permute-start | bytes 626696 | tf_op jit(solution)/shard_map/ppermute | solution.py:209
  21.2 5.4 %copy-start.25 = (bf16[136,768]{1,0:T(8,128)(2,1)}, bf16[136,768]{1,0:T(8,128)(2,1)S(1)}, u32[]{:S(2)}) copy-start(bf16[136,768]{1,0:T(8,128)(2,1)S(1)} %collective-permute-done.refs_1_) | copy-start | bytes 626692
  21.2 5.4 %copy-start.26 = (bf16[136,768]{1,0:T(8,128)(2,1)}, bf16[136,768]{1,0:T(8,128)(2,1)S(1)}, u32[]{:S(2)}) copy-start(bf16[136,768]{1,0:T(8,128)(2,1)S(1)} %collective-permute-done.1.refs_2_) | copy-start | bytes 626692
  31.5 6.5 %copy-start.1 = (bf16[32,16,896]{2,1,0:T(8,128)(2,1)}, bf16[32,16,896]{2,1,0:T(8,128)(2,1)S(1)}, u32[]{:S(2)}) copy-start(bf16[32,16,896]{2,1,0:T(8,128)(2,1)S(1)} %all-to-all-done) | copy-start | bytes 2752516
  32.6 14.4 %collective-permute-start.4 = (bf16[256,896]{1,0:T(8,128)(2,1)}, bf16[256,896]{1,0:T(8,128)(2,1)}, u32[]{:S(2)}, u32[]{:S(2)}) collective-permute-start(bf16[256,896]{1,0:T(8,128)(2,1)} %get-tuple-element.24), channel_id=1, source_target_pairs={{0,3},{1,0},{2,1},{3,2},{4,7},{5,4},{6,5},{7,6},{8,11},{9,8},{10,9... | collective-permute-start | bytes 1376264 | tf_op jit(solution)/shard_map/ppermute | solution.py:221
  34.8 18.9 %collective-permute-start.3 = (bf16[256,896]{1,0:T(8,128)(2,1)}, bf16[256,896]{1,0:T(8,128)(2,1)}, u32[]{:S(2)}, u32[]{:S(2)}) collective-permute-start(bf16[256,896]{1,0:T(8,128)(2,1)} %get-tuple-element.23), channel_id=1, source_target_pairs={{0,3},{1,0},{2,1},{3,2},{4,7},{5,4},{6,5},{7,6},{8,11},{9,8},{10,9... | collective-permute-start | bytes 1376264 | tf_op jit(solution)/shard_map/ppermute | solution.py:223
  35.5 26.7 %collective-permute-start.5 = (bf16[256,896]{1,0:T(8,128)(2,1)}, bf16[256,896]{1,0:T(8,128)(2,1)}, u32[]{:S(2)}, u32[]{:S(2)}) collective-permute-start(bf16[256,896]{1,0:T(8,128)(2,1)} %get-tuple-element.23), channel_id=1, source_target_pairs={{0,1},{1,2},{2,3},{3,0},{4,5},{5,6},{6,7},{7,4},{8,9},{9,10},{10,1... | collective-permute-start | bytes 1376264 | tf_op jit(solution)/shard_map/ppermute | solution.py:220
  36.9 31.9 %collective-permute-start.10 = (bf16[256,896]{1,0:T(8,128)(2,1)}, bf16[256,896]{1,0:T(8,128)(2,1)}, u32[]{:S(2)}, u32[]{:S(2)}) collective-permute-start(bf16[256,896]{1,0:T(8,128)(2,1)} %get-tuple-element.24), channel_id=1, source_target_pairs={{0,1},{1,2},{2,3},{3,0},{4,5},{5,6},{6,7},{7,4},{8,9},{9,10},{10,1... | collective-permute-start | bytes 1376264 | tf_op jit(solution)/shard_map/ppermute | solution.py:222
  38.0 75.0 %all-to-all-start.1 = ((bf16[32,64,768]{2,1,0:T(8,128)(2,1)}), bf16[32,64,768]{2,1,0:T(8,128)(2,1)S(1)}, u32[]{:S(2)}, u32[]{:S(2)}) async-start(bf16[32,64,768]{2,1,0:T(8,128)(2,1)} %bitcast.8), calls=%async_computation.1 | async-start | bytes 6291456 | tf_op jit(solution)/shard_map/all_to_all | solution.py:174
  55.3 28.7 %collective-permute-start.7 = (bf16[256,896]{1,0:T(8,128)(2,1)}, bf16[256,896]{1,0:T(8,128)(2,1)}, u32[]{:S(2)}, u32[]{:S(2)}) collective-permute-start(bf16[256,896]{1,0:T(8,128)(2,1)} %collective-permute-done.4), channel_id=1, source_target_pairs={{0,3},{1,0},{2,1},{3,2},{4,7},{5,4},{6,5},{7,6},{8,11},{9,8},{10,9... | collective-permute-start | bytes 1376264 | tf_op jit(solution)/shard_map/ppermute | solution.py:225
  60.8 5.1 %copy-start.7 = (bf16[256,768]{1,0:T(8,128)(2,1)}, bf16[256,768]{1,0:T(8,128)(2,1)S(1)}, u32[]{:S(2)}) copy-start(bf16[256,768]{1,0:T(8,128)(2,1)S(1)} %slice.222) | copy-start | bytes 1179652
  62.2 18.8 %collective-permute-start.6 = (bf16[256,896]{1,0:T(8,128)(2,1)}, bf16[256,896]{1,0:T(8,128)(2,1)}, u32[]{:S(2)}, u32[]{:S(2)}) collective-permute-start(bf16[256,896]{1,0:T(8,128)(2,1)} %collective-permute-done.5), channel_id=1, source_target_pairs={{0,1},{1,2},{2,3},{3,0},{4,5},{5,6},{6,7},{7,4},{8,9},{9,10},{10,1... | collective-permute-start | bytes 1376264 | tf_op jit(solution)/shard_map/ppermute | solution.py:224
  102.5 9.7 %collective-permute-start.8 = (bf16[256,768]{1,0:T(8,128)(2,1)S(1)}, bf16[256,768]{1,0:T(8,128)(2,1)S(1)}, u32[]{:S(2)}, u32[]{:S(2)}) collective-permute-start(bf16[256,768]{1,0:T(8,128)(2,1)S(1)} %get-tuple-element.25), channel_id=1, source_target_pairs={{0,1},{1,2},{2,3},{3,0},{4,5},{5,6},{6,7},{7,4},{8,9},{9,10},{10,1... | collective-permute-start | bytes 1179656 | tf_op jit(solution)/shard_map/ppermute | solution.py:187
  102.5 22.6 %collective-permute-start.11 = (bf16[256,768]{1,0:T(8,128)(2,1)}, bf16[256,768]{1,0:T(8,128)(2,1)}, u32[]{:S(2)}, u32[]{:S(2)}) collective-permute-start(bf16[256,768]{1,0:T(8,128)(2,1)} %get-tuple-element.26), channel_id=1, source_target_pairs={{0,3},{1,0},{2,1},{3,2},{4,7},{5,4},{6,5},{7,6},{8,11},{9,8},{10,9... | collective-permute-start | bytes 1179656 | tf_op jit(solution)/shard_map/ppermute | solution.py:188
  106.5 5.7 %copy-start.18 = (bf16[512,768]{1,0:T(8,128)(2,1)S(1)}, bf16[512,768]{1,0:T(8,128)(2,1)}, u32[]{:S(2)}) copy-start(bf16[512,768]{1,0:T(8,128)(2,1)} %copy-done.17) | copy-start | bytes 2359300
  107.5 4.7 %copy-start.19 = (bf16[512,768]{1,0:T(8,128)(2,1)}, bf16[512,768]{1,0:T(8,128)(2,1)S(1)}, u32[]{:S(2)}) copy-start(bf16[512,768]{1,0:T(8,128)(2,1)S(1)} %fusion.25) | copy-start | bytes 2359300
  113.0 7.2 %copy-start = (bf16[32,64,768]{2,1,0:T(8,128)(2,1)}, bf16[32,64,768]{2,1,0:T(8,128)(2,1)S(1)}, u32[]{:S(2)}) copy-start(bf16[32,64,768]{2,1,0:T(8,128)(2,1)S(1)} %all-to-all-done.1) | copy-start | bytes 9437188
  113.0 7.2 %copy-start.6 = (bf16[2,1024,768]{2,1,0:T(8,128)(2,1)S(1)}, bf16[2,1024,768]{2,1,0:T(8,128)(2,1)}, u32[]{:S(2)}) copy-start(bf16[2,1024,768]{2,1,0:T(8,128)(2,1)} %refs_10_.1) | copy-start | bytes 9437188
  124.1 4.8 %slice-start.1 = ((bf16[512,768]{1,0:T(8,128)(2,1)}), bf16[256,768]{1,0:T(8,128)(2,1)S(1)}, s32[]{:S(2)}) async-start(bf16[512,768]{1,0:T(8,128)(2,1)} %copy-done.19), calls=%async_computation.4 | async-start | bytes 786432 | tf_op jit(solution)/shard_map/slice | solution.py:190
  124.1 8.9 %collective-permute-start.13 = (bf16[256,768]{1,0:T(8,128)(2,1)S(1)}, bf16[256,768]{1,0:T(8,128)(2,1)S(1)}, u32[]{:S(2)}, u32[]{:S(2)}) collective-permute-start(bf16[256,768]{1,0:T(8,128)(2,1)S(1)} %bitcast.91), channel_id=1, source_target_pairs={{0,1},{1,2},{2,3},{3,0},{4,5},{5,6},{6,7},{7,4},{8,9},{9,10},{10,1... | collective-permute-start | bytes 1179656 | tf_op jit(solution)/shard_map/ppermute | solution.py:187
  125.0 24.8 %collective-permute-start.9 = (bf16[512,768]{1,0:T(8,128)(2,1)S(1)}, bf16[512,768]{1,0:T(8,128)(2,1)S(1)}, u32[]{:S(2)}, u32[]{:S(2)}) collective-permute-start(bf16[512,768]{1,0:T(8,128)(2,1)S(1)} %pad_maximum_fusion.3), channel_id=1, source_target_pairs={{0,1},{1,2},{2,3},{3,0},{4,5},{5,6},{6,7},{7,4},{8,9},{9,10},{10,1... | collective-permute-start | bytes 2359304 | tf_op jit(solution)/shard_map/ppermute | solution.py:191
  126.3 7.7 %collective-permute-start.15 = (bf16[256,768]{1,0:T(8,128)(2,1)S(1)}, bf16[256,768]{1,0:T(8,128)(2,1)S(1)}, u32[]{:S(2)}, u32[]{:S(2)}) collective-permute-start(bf16[256,768]{1,0:T(8,128)(2,1)S(1)} %bitcast.90), channel_id=1, source_target_pairs={{0,3},{1,0},{2,1},{3,2},{4,7},{5,4},{6,5},{7,6},{8,11},{9,8},{10,9... | collective-permute-start | bytes 1179656 | tf_op jit(solution)/shard_map/ppermute | solution.py:188
  129.0 21.9 %collective-permute-start.12 = (bf16[512,768]{1,0:T(8,128)(2,1)S(1)}, bf16[512,768]{1,0:T(8,128)(2,1)S(1)}, u32[]{:S(2)}, u32[]{:S(2)}) collective-permute-start(bf16[512,768]{1,0:T(8,128)(2,1)S(1)} %pad_maximum_fusion.5), channel_id=1, source_target_pairs={{0,3},{1,0},{2,1},{3,2},{4,7},{5,4},{6,5},{7,6},{8,11},{9,8},{10,9... | collective-permute-start | bytes 2359304 | tf_op jit(solution)/shard_map/ppermute | solution.py:192
  133.1 4.6 %copy-start.2 = (bf16[32,16,896]{2,1,0:T(8,128)(2,1)S(1)}, bf16[32,16,896]{2,1,0:T(8,128)(2,1)}, u32[]{:S(2)}) copy-start(bf16[32,16,896]{2,1,0:T(8,128)(2,1)} %copy-done.1) | copy-start | bytes 2752516
  133.2 33.5 %collective-permute-start.14 = (bf16[512,768]{1,0:T(8,128)(2,1)S(1)}, bf16[512,768]{1,0:T(8,128)(2,1)S(1)}, u32[]{:S(2)}, u32[]{:S(2)}) collective-permute-start(bf16[512,768]{1,0:T(8,128)(2,1)S(1)} %pad_maximum_fusion.6), channel_id=1, source_target_pairs={{0,1},{1,2},{2,3},{3,0},{4,5},{5,6},{6,7},{7,4},{8,9},{9,10},{10,1... | collective-permute-start | bytes 2359304 | tf_op jit(solution)/shard_map/ppermute | solution.py:191
  134.2 33.5 %collective-permute-start.16 = (bf16[512,768]{1,0:T(8,128)(2,1)S(1)}, bf16[512,768]{1,0:T(8,128)(2,1)S(1)}, u32[]{:S(2)}, u32[]{:S(2)}) collective-permute-start(bf16[512,768]{1,0:T(8,128)(2,1)S(1)} %pad_maximum_fusion.7), channel_id=1, source_target_pairs={{0,3},{1,0},{2,1},{3,2},{4,7},{5,4},{6,5},{7,6},{8,11},{9,8},{10,9... | collective-permute-start | bytes 2359304 | tf_op jit(solution)/shard_map/ppermute | solution.py:192
  139.0 12.9 %copy-start.24 = (bf16[512,1024]{1,0:T(8,128)(2,1)}, bf16[512,1024]{1,0:T(8,128)(2,1)S(1)}, u32[]{:S(2)}) copy-start(bf16[512,1024]{1,0:T(8,128)(2,1)S(1)} %subtract_convert_fusion.4.refs_0_) | copy-start | bytes 3145732
  169.5 9.4 %copy-start.8 = (bf16[256,768]{1,0:T(8,128)(2,1)S(1)}, bf16[256,768]{1,0:T(8,128)(2,1)}, u32[]{:S(2)}) copy-start(bf16[256,768]{1,0:T(8,128)(2,1)} %copy-done.7) | copy-start | bytes 1179652
  169.5 31.1 %all-to-all-start.2 = ((bf16[32,16,1536]{2,1,0:T(8,128)(2,1)}), bf16[32,16,1536]{2,1,0:T(8,128)(2,1)S(1)}, u32[]{:S(2)}, u32[]{:S(2)}) async-start(bf16[32,16,1536]{2,1,0:T(8,128)(2,1)} %bitcast.84), calls=%async_computation.2 | async-start | bytes 3145728 | tf_op jit(solution)/shard_map/all_to_all | solution.py:174
  (23 other events, 56.0 us)

commit v5 on v2

--- a/solution.py
+++ b/solution.py
@@ -4,6 +4,7 @@
 from jax.experimental import pallas as pl
 from jax.experimental.pallas import tpu as pltpu
 from jax.sharding import PartitionSpec as P
+
 
 momentum_decay = 0.9
 step_rate = 0.002
@@ -98,11 +99,15 @@
         box_ref[:, k] = filled.astype(jnp.bfloat16).reshape(CLUS, CAP, D)
 
 
-def home_kernel(parity, visits_ref, homed_ref, before_ref, out_ref):
-    chosen = as_bf16(picks(visits_ref[...], parity))
-    out_ref[...] = before_ref[...] + lax.dot_general(
-        chosen, homed_ref[...], (((0,), (0,)), ((), ())), preferred_element_type=jnp.float32
-    )
+def home_kernel(visits_ref, homed_ref, out_ref):
+    total = jnp.zeros((NQ, D), jnp.float32)
+    for parity in range(2):
+        chosen = as_bf16(picks(visits_ref[...], parity))
+        rows = homed_ref[:, parity * D : (parity + 1) * D]
+        total = total + lax.dot_general(
+            chosen, rows, (((0,), (0,)), ((), ())), preferred_element_type=jnp.float32
+        )
+    out_ref[...] = total
 
 
 def tile_grads(rows, high, low, first, w_ref):
@@ -123,48 +128,58 @@
     return grad, part.astype(jnp.bfloat16)
 
 
-def first_kernel(lab_ref, rows_ref, w_ref, grad_ref, part_ref):
-    for t in range(0, rows_ref.shape[0], TILE):
-        notes = rows_ref[t : t + TILE, D:].astype(jnp.float32)
-        grad, part = tile_grads(
-            rows_ref[t : t + TILE, :D], notes[:, 0:1], notes[:, 1:2], lab_ref[0] * LABELS, w_ref
-        )
-        grad_ref[t : t + TILE] = grad
-        part_ref[t : t + TILE] = part
-
-
-def first_grads(lab, rows, weights):
-    n = rows.shape[0]
-    vmem = pltpu.VMEM
+def first_kernel(count, lab_ref, *refs):
+    pieces, w_ref, grad_ref, parts = refs[:count], refs[count], refs[count + 1], refs[count + 2 :]
+    at = 0
+    for k, piece in enumerate(pieces):
+        for t in range(0, piece.shape[0], TILE):
+            notes = piece[t : t + TILE, D:].astype(jnp.float32)
+            grad, part = tile_grads(
+                piece[t : t + TILE, :D], notes[:, 0:1], notes[:, 1:2], lab_ref[0] * LABELS, w_ref
+            )
+            grad_ref[at : at + TILE] = grad
+            if len(parts) == 1:
+                parts[0][at : at + TILE] = part
+            else:
+                parts[k][t : t + TILE] = part
+            at += TILE
+
+
+def whole(shape):
+    return pl.BlockSpec(shape, lambda *_: (0,) * len(shape))
+
+
+def first_grads(lab, pieces, weights, apart=False):
+    bf = jnp.bfloat16
+    n = sum(p.shape[0] for p in pieces)
+    sizes = [p.shape[0] for p in pieces] if apart else [n]
+    count = len(pieces)
     return pl.pallas_call(
-        first_kernel,
+        lambda *refs: first_kernel(count, *refs),
         grid=(1,),
-        in_specs=[
-            pl.BlockSpec(memory_space=pltpu.SMEM),
-            pl.BlockSpec((n, D + TAGS), lambda i: (0, 0), memory_space=vmem),
-            pl.BlockSpec((1, LABELS, D), lambda i: (0, 0, 0), memory_space=vmem),
-        ],
-        out_specs=(
-            pl.BlockSpec((n, LABELS), lambda i: (0, 0), memory_space=vmem),
-            pl.BlockSpec((n, D), lambda i: (0, 0), memory_space=vmem),
-        ),
-        out_shape=(
-            jax.ShapeDtypeStruct((n, LABELS), jnp.bfloat16),
-            jax.ShapeDtypeStruct((n, D), jnp.bfloat16),
-        ),
+        in_specs=[pl.BlockSpec(memory_space=pltpu.SMEM)]
+        + [whole(p.shape) for p in pieces]
+        + [whole((1, LABELS, D))],
+        out_specs=[whole((n, LABELS))] + [whole((m, D)) for m in sizes],
+        out_shape=[jax.ShapeDtypeStruct((n, LABELS), bf)]
+        + [jax.ShapeDtypeStruct((m, D), bf) for m in sizes],
         cost_estimate=pl.CostEstimate(
             flops=4 * n * LABELS * D, bytes_accessed=2 * n * 3000, transcendentals=n * LABELS
         ),
         name="first_grads",
-    )(lab, rows, weights)
-
-
-def second_kernel(lab_ref, rows_ref, own, low, high, far_a, far_b, w_ref, grad_ref, *parts):
+    )(lab, *pieces, weights)
+
+
+def second_kernel(lab_ref, rows_ref, *refs):
+    notes_refs, w_ref, grad_ref, parts = refs[:7], refs[7], refs[8], refs[9:]
     step = pl.program_id(0)
     early = step < STEPS // 2
     f32 = jnp.float32
-    far = jnp.where(early, far_a[...].astype(f32), far_b[...].astype(f32))
-    notes = [own[...].astype(f32), low[...].astype(f32), high[...].astype(f32), far]
+    notes = [notes_refs[0][...].astype(f32)]
+    for k in range(1, 7, 2):
+        notes.append(
+            jnp.where(early, notes_refs[k][...].astype(f32), notes_refs[k + 1][...].astype(f32))
+        )
     notes = jnp.stack([x.reshape(SRC, CAP, TAGS) for x in notes], axis=1).reshape(TILE, TAGS)
     rows = rows_ref[...].reshape(TILE, D)
     grad, part = tile_grads(rows, notes[:, 2:3], notes[:, 3:4], lab_ref[0] * LABELS, w_ref)
@@ -187,7 +202,7 @@
     bf = jnp.bfloat16
     last = STEPS // 2 - 1
     here = SRC * CAP
-    whole = lambda i: (i, D // TAGS)
+    each = lambda i: (i, D // TAGS)
     early = lambda i: (jnp.minimum(i, last), D // TAGS)
     late = lambda i: (jnp.maximum(i - last - 1, 0), D // TAGS)
     note = lambda at: pl.BlockSpec((here, TAGS), at)
@@ -197,13 +212,10 @@
         in_specs=[
             pl.BlockSpec(memory_space=pltpu.SMEM),
             pl.BlockSpec((SRC, LAB * CAP, D), lambda i: (i, 0, 0)),
-            note(whole),
-            note(whole),
-            note(whole),
-            note(early),
-            note(late),
-            pl.BlockSpec((1, LABELS, D), lambda i: (1, 0, 0)),
-        ],
+            note(each),
+        ]
+        + [note(early), note(late)] * 3
+        + [pl.BlockSpec((1, LABELS, D), lambda i: (1, 0, 0))],
         out_specs=(
             pl.BlockSpec((TILE, LABELS), lambda i: (i, 0)),
             pl.BlockSpec((here, D), lambda i: (i, 0)),
@@ -222,43 +234,49 @@
     )(lab, rows, *pieces, weights)
 
 
-def update_kernel(count, *refs):
-    grads, rows = refs[:count], refs[count : 2 * count]
-    w_ref, m_ref = refs[2 * count : 2 * count + 2]
-    wo_ref, mo_ref = refs[-2:]
+def update_kernel(counts, *refs):
+    grads, rest = refs[: len(counts)], refs[len(counts) :]
+    rows, rest = rest[: sum(counts)], rest[sum(counts) :]
+    w_ref, m_ref, wo_ref, mo_ref = rest[0], rest[1], rest[-2], rest[-1]
     fresh = momentum_decay * m_ref[0]
-    for grad_ref, rows_ref in zip(grads, rows):
-        fresh = fresh + lax.dot_general(
-            grad_ref[...],
-            rows_ref[:, :D],
-            (((0,), (0,)), ((), ())),
-            preferred_element_type=jnp.float32,
-        )
+    k = 0
+    for grad_ref, count in zip(grads, counts):
+        at = 0
+        for rows_ref in rows[k : k + count]:
+            size = rows_ref.shape[0]
+            fresh = fresh + lax.dot_general(
+                grad_ref[at : at + size],
+                rows_ref[:, :D],
+                (((0,), (0,)), ((), ())),
+                preferred_element_type=jnp.float32,
+            )
+            at += size
+        k += count
     mo_ref[0] = fresh
     wo_ref[0] = (w_ref[0].astype(jnp.float32) - step_rate * fresh).astype(jnp.bfloat16)
 
 
-def update(cluster, grads, rows, weights, momentum, before=()):
+def update(cluster, grads, blocks, weights, momentum, before=()):
     bands = LABELS // BAND
     band = pl.BlockSpec((1, BAND, D), lambda b: (cluster, b, 0))
-    n = sum(r.shape[0] for r in rows)
-    count = len(grads)
-    keep = [pl.BlockSpec(memory_space=pl.ANY) for _ in before]
+    counts = tuple(len(block) for block in blocks)
+    rows = [piece for block in blocks for piece in block]
+    first = len(grads) + len(rows) + 2
     return pl.pallas_call(
-        lambda *refs: update_kernel(count, *refs),
+        lambda *refs: update_kernel(counts, *refs),
         grid=(bands,),
         in_specs=[pl.BlockSpec((g.shape[0], BAND), lambda b: (0, b)) for g in grads]
-        + [pl.BlockSpec(r.shape, lambda b: (0, 0)) for r in rows]
+        + [whole(r.shape) for r in rows]
         + [band, band]
-        + keep,
+        + [pl.BlockSpec(memory_space=pl.ANY) for _ in before],
         out_specs=(band, band),
         out_shape=(
             jax.ShapeDtypeStruct(weights.shape, weights.dtype),
             jax.ShapeDtypeStruct(momentum.shape, momentum.dtype),
         ),
-        input_output_aliases={2 * count + 2 + k: k for k in range(len(before))},
+        input_output_aliases={first + k: k for k in range(len(before))},
         cost_estimate=pl.CostEstimate(
-            flops=2 * n * LABELS * D, bytes_accessed=18 << 20, transcendentals=0
+            flops=2 * LAB * ROWS * LABELS * D, bytes_accessed=18 << 20, transcendentals=0
         ),
         name="update",
     )(*grads, *rows, weights, momentum, *before)
@@ -275,7 +293,8 @@
     return total.astype(jnp.bfloat16)
 
 
-def scatter_sum(own, low, high, far_a, far_b):
+def ring_sum(parts):
+    own, low, high, far_a, far_b = parts
     half = ROWS // 2
     up = lax.ppermute(far_a, "lab", ring(1))
     down = lax.ppermute(far_b, "lab", ring(-1))
@@ -283,10 +302,10 @@
     down = jnp.concatenate([low[:half], add(low[half:], down)])
     up = lax.ppermute(up, "lab", ring(1))
     down = lax.ppermute(down, "lab", ring(-1))
-    return own, up, down
-
-
-def shards(queries, visits, positives, weights, momentum):
+    return add(own, up, down)
+
+
+def step(queries, visits, positives, weights, momentum):
     vt, pt = visits.T, positives.T
     bf = jnp.bfloat16
     lab = lax.axis_index("lab").reshape(1).astype(jnp.int32)
@@ -310,29 +329,31 @@
     got_b = swap(box_b.reshape(CLUS, LAB * CAP, D))
 
     half = ROWS // 2
-    from_low = lax.ppermute(got_a, "lab", ring(1))
-    from_high = lax.ppermute(got_a, "lab", ring(-1))
-    far_a = lax.ppermute(from_low[:half], "lab", ring(1))
-    far_b = lax.ppermute(from_high[half:], "lab", ring(-1))
-    pieces = (got_a, from_low, from_high, far_a, far_b)
-    grads_a, parts_a = zip(*[first_grads(lab, p, weights) for p in pieces])
-    own, up, down = scatter_sum(*parts_a)
-    home_a = swap(add(own, up, down).reshape(CLUS, CAP, D)).reshape(ROWS, D)
+    low_a = lax.ppermute(got_a[:half], "lab", ring(1))
+    high_b = lax.ppermute(got_a[half:], "lab", ring(-1))
+    low_b = lax.ppermute(got_a[half:], "lab", ring(1))
+    high_a = lax.ppermute(got_a[:half], "lab", ring(-1))
+    far_a = lax.ppermute(low_a, "lab", ring(1))
+    far_b = lax.ppermute(high_b, "lab", ring(-1))
+    blocks = ((got_a,), (low_a, low_b), (high_a, high_b), (far_a, far_b))
+    grads_a, parts_a = [], []
+    for block, place in zip(blocks, ("here", "near1", "near2", "far")):
+        grad, *parts = first_grads(lab, block, weights, apart=place == "far")
+        grads_a.append(grad)
+        parts_a += parts
+    home_a = ring_sum(parts_a)
+    pieces = [p for block in blocks for p in block]
     grad_b, *parts_b = second_grads(lab, got_b, pieces, weights)
-    own, up, down = scatter_sum(*parts_b)
-    new = update(0, grads_a, pieces, weights, momentum)
-    new = update(1, (grad_b,), (got_b.reshape(LAB * ROWS, D),), weights, momentum, new)
-    own, up, down, new = lax.optimization_barrier((own, up, down, new))
-    home_b = swap(add(own, up, down).reshape(CLUS, CAP, D)).reshape(ROWS, D)
-
-    total = jnp.zeros((NQ, D), jnp.float32)
-    for parity, homed in ((0, home_a), (1, home_b)):
-        total = pl.pallas_call(
-            lambda *refs, parity=parity: home_kernel(parity, *refs),
-            out_shape=jax.ShapeDtypeStruct((NQ, D), jnp.float32),
-            name=f"home_{parity}",
-        )(vt, homed, total)
-    return (total, *new)
+    home_b = ring_sum(parts_b)
+    both = jnp.concatenate([home_a, home_b], axis=1).reshape(CLUS, CAP, 2 * D)
+    both = swap(both).reshape(ROWS, 2 * D)
+    new = update(0, grads_a, blocks, weights, momentum)
+    rows_b = ((got_b.reshape(LAB * ROWS, D),),)
+    new = update(1, (grad_b,), rows_b, weights, momentum, new)
+    query_grad = pl.pallas_call(
+        home_kernel, out_shape=jax.ShapeDtypeStruct((NQ, D), jnp.float32), name="home_sum"
+    )(vt, both)
+    return (query_grad, *new)
 
 
 def solution(mesh):
@@ -344,4 +365,4 @@
         P("clus", "lab", None),
     )
     out_specs = (P(("clus", "lab"), None), P("clus", "lab", None), P("clus", "lab", None))
-    return jax.shard_map(shards, mesh=mesh, in_specs=in_specs, out_specs=out_specs, check_vma=False)
+    return jax.shard_map(step, mesh=mesh, in_specs=in_specs, out_specs=out_specs, check_vma=False)

time: 208 us -> 196 us (0.942)
  starting transfers between devices: 57.8 us -> 50.4 us
  Pallas kernels: 63.9 us -> 59 us
  waiting for transfers between devices: 62 us -> 65.8 us
  local copies, waits for them, and re-layouts: 12 us -> 9.52 us
    ppermute x15 -> x17, waiting for transfers between devices: 51 us -> 61.6 us  [the longest x2 15.8 us: ring_sum(): down = lax.ppermute(down, 'lab', ring(-1))]
    all_to_all x4 -> x3, starting transfers between devices: 35.6 us -> 26.8 us  [swap(): return lax.all_to_all(x, 'clus', split_axis=0, concat_axis=0, tiled=True)]
    all_to_all x4 -> x3, waiting for transfers between devices: 11 us -> 4.15 us  [swap(): return lax.all_to_all(x, 'clus', split_axis=0, concat_axis=0, tiled=True)]
    pallas_call x11 -> x9, Pallas kernels: 51.2 us -> 46.2 us  [the longest x2 18.5 us: update(): pl.pallas_call(lambda *refs: update_kernel(counts, *refs), grid=(bands,),...]
    unnamed x28 -> x24, local copies, waits for them, and re-layouts: 6.74 us -> 4.47 us
    ppermute x15 -> x17, starting transfers between devices: 22.2 us -> 23.6 us  [the longest x3 5.13 us: step(): peers = [raw] + [lax.ppermute(raw, 'lab', ring(s)) for s in (1, -1, 2)]]
    slice x6 -> x5, local copies, waits for them, and re-layouts: 4.46 us -> 5.05 us  [the longest x1 2.18 us: step(): high_b = lax.ppermute(got_a[half:], 'lab', ring(-1))]
  transfers between devices with their start and end apart: 19 -> 20, of which waited for: 7 -> 12; matrix products, arithmetic and copies ran while one was open for 8% -> 6% of each run, Pallas kernels for 28% -> 27%
where the time goes in v5:
time: 196 us; the launch traced here: 195 us
  waiting for transfers between devices  65.8 us (34%)
  Pallas kernels  59 us (30%)
  starting transfers between devices  50.4 us (26%)
  other arithmetic  9.7 us (5%)
  local copies, waits for them, and re-layouts  9.52 us (5%)
    all_to_all x3, starting transfers between devices, swap(): return lax.all_to_all(x, 'clus', split_axis=0, concat_axis=0, tiled=True)  26.8 us
    pallas_call x2, Pallas kernels, update(): pl.pallas_call(lambda *refs: update_kernel(counts, *refs), grid=(bands,),...  18.5 us
    pallas_call x4, Pallas kernels, first_grads(): pl.pallas_call(lambda *refs: first_kernel(count, *refs), grid=(1,), in_sp...  18.2 us
    ppermute x2, waiting for transfers between devices, ring_sum(): down = lax.ppermute(down, 'lab', ring(-1))  15.8 us
    pallas_call x1, Pallas kernels, second_grads(): pl.pallas_call(second_kernel, grid=(STEPS,), in_specs=[pl.BlockSpec(memor...  12.7 us
    ppermute x2, waiting for transfers between devices, ring_sum(): up = lax.ppermute(up, 'lab', ring(1))  11.3 us
    ppermute x1, waiting for transfers between devices, step(): low_a = lax.ppermute(got_a[:half], 'lab', ring(1))  10.7 us
    ppermute x3, waiting for transfers between devices, step(): peers = [raw] + [lax.ppermute(raw, 'lab', ring(s)) for s in (1, -1, 2)]  9.37 us
  transfers between devices with their start and end apart: 20, of which 12 were waited for; matrix products, arithmetic and copies ran while one was open for 6% of the time, Pallas kernels for 27%

profile of v5, /device:TPU:1, one launch (start us, length us, event | category | flops | bytes accessed | tf_op | source)
XLA Modules:
  0.0 195.2 jit_solution(1303903760701222664)
XLA Ops:
  0.6 2.6 %own_box.1 = (bf16[512,896]{1,0:T(8,128)(2,1)}, bf16[136,768]{1,0:T(8,128)(2,1)}) custom-call(s32[4,128]{1,0:T(4,128)} %bitcast.17, s32[4,128]{1,0:T(4,128)} %bitcast.19, bf16[128,768]{1,0:T(8,128)(2,1)} %queries_ref.1), custom_call_target="tpu_custom_call" | custom-call | tf_op jit(solution)/shard_map/own_box/pallas_call | solution.py:313
  3.2 8.7 %all-to-all-start = ((bf16[32,16,896]{2,1,0:T(8,128)(2,1)}), bf16[32,16,896]{2,1,0:T(8,128)(2,1)S(1)}, u32[]{:S(2)}, u32[]{:S(2)}) async-start(bf16[32,16,896]{2,1,0:T(8,128)(2,1)} %bitcast.16), calls=%async_computation | async-start | bytes 1835008 | tf_op jit(solution)/shard_map/all_to_all | solution.py:286
  13.7 2.2 %collective-permute-start.1 = (bf16[136,768]{1,0:T(8,128)(2,1)S(1)}, bf16[136,768]{1,0:T(8,128)(2,1)S(1)}, u32[]{:S(2)}, u32[]{:S(2)}) collective-permute-start(bf16[136,768]{1,0:T(8,128)(2,1)S(1)} %copy-done.7), channel_id=1, source_target_pairs={{0,3},{1,0},{2,1},{3,2},{4,7},{5,4},{6,5},{7,6},{8,11},{9,8},{10,9... | collective-permute-start | bytes 626696 | tf_op jit(solution)/shard_map/ppermute | solution.py:321
  17.1 4.0 %collective-permute-done.refs_1_ = bf16[136,768]{1,0:T(8,128)(2,1)S(1)} collective-permute-done((bf16[136,768]{1,0:T(8,128)(2,1)S(1)}, bf16[136,768]{1,0:T(8,128)(2,1)S(1)}, u32[]{:S(2)}, u32[]{:S(2)}) %collective-permute-start) | collective-permute-done | bytes 208928 | tf_op jit(solution)/shard_map/ppermute | solution.py:321
  21.1 5.4 %collective-permute-done.2.refs_3_ = bf16[136,768]{1,0:T(8,128)(2,1)S(1)} collective-permute-done((bf16[136,768]{1,0:T(8,128)(2,1)S(1)}, bf16[136,768]{1,0:T(8,128)(2,1)S(1)}, u32[]{:S(2)}, u32[]{:S(2)}) %collective-permute-start.2) | collective-permute-done | bytes 208928 | tf_op jit(solution)/shard_map/ppermute | solution.py:321
  27.2 4.2 %all_box.1 = bf16[32,4,16,768]{3,2,1,0:T(8,128)(2,1)} custom-call(bf16[136,768]{1,0:T(8,128)(2,1)} %get-tuple-element.27.refs_0_, bf16[136,768]{1,0:T(8,128)(2,1)} %copy-done.8, bf16[136,768]{1,0:T(8,128)(2,1)} %copy-done.9, bf16[136,768]{1,0:T(8,128)(2,1)} %copy-done.10), custom_call_target="tpu_custom_call" | custom-call | tf_op jit(solution)/shard_map/all_box/pallas_call | solution.py:323
  32.3 8.1 %all-to-all-start.1 = ((bf16[32,64,768]{2,1,0:T(8,128)(2,1)}), bf16[32,64,768]{2,1,0:T(8,128)(2,1)S(1)}, u32[]{:S(2)}, u32[]{:S(2)}) async-start(bf16[32,64,768]{2,1,0:T(8,128)(2,1)} %bitcast.10), calls=%async_computation.1 | async-start | bytes 6291456 | tf_op jit(solution)/shard_map/all_to_all | solution.py:286
  40.4 2.2 %fusion = (bf16[256,896]{1,0:T(8,128)(2,1)}, bf16[256,896]{1,0:T(8,128)(2,1)}) fusion(bf16[512,896]{1,0:T(8,128)(2,1)} %bitcast.11), kind=kLoop, calls=%fused_computation.11 | loop fusion | bytes 1835008 | tf_op jit(solution)/shard_map/slice | solution.py:333
  45.3 10.7 %collective-permute-done.5.refs_1_.refs_5_ = bf16[256,896]{1,0:T(8,128)(2,1)} collective-permute-done((bf16[256,896]{1,0:T(8,128)(2,1)}, bf16[256,896]{1,0:T(8,128)(2,1)}, u32[]{:S(2)}, u32[]{:S(2)}) %collective-permute-start.5) | collective-permute-done | bytes 458784 | tf_op jit(solution)/shard_map/ppermute | solution.py:332
  56.0 2.7 %collective-permute-start.7 = (bf16[256,896]{1,0:T(8,128)(2,1)}, bf16[256,896]{1,0:T(8,128)(2,1)}, u32[]{:S(2)}, u32[]{:S(2)}) collective-permute-start(bf16[256,896]{1,0:T(8,128)(2,1)} %collective-permute-done.4.refs_2_.refs_4_.refs_8_), channel_id=1, source_target_pairs={{0,3},{1,0},{2,1},{3,2},{4,7},{5,4},{6,5},{7,6},{8,11},{9,8},{10,9... | collective-permute-start | bytes 1376264 | tf_op jit(solution)/shard_map/ppermute | solution.py:337
  58.7 2.7 %collective-permute-start.3 = (bf16[256,896]{1,0:T(8,128)(2,1)}, bf16[256,896]{1,0:T(8,128)(2,1)}, u32[]{:S(2)}, u32[]{:S(2)}) collective-permute-start(bf16[256,896]{1,0:T(8,128)(2,1)} %get-tuple-element.50), channel_id=1, source_target_pairs={{0,3},{1,0},{2,1},{3,2},{4,7},{5,4},{6,5},{7,6},{8,11},{9,8},{10,9... | collective-permute-start | bytes 1376264 | tf_op jit(solution)/shard_map/ppermute | solution.py:335
  61.3 7.2 %collective-permute-done.6.refs_1_.refs_5_.refs_9_ = bf16[256,896]{1,0:T(8,128)(2,1)} collective-permute-done((bf16[256,896]{1,0:T(8,128)(2,1)}, bf16[256,896]{1,0:T(8,128)(2,1)}, u32[]{:S(2)}, u32[]{:S(2)}) %collective-permute-start.6) | collective-permute-done | bytes 458784 | tf_op jit(solution)/shard_map/ppermute | solution.py:336
  68.5 4.4 %first_grads.6 = (bf16[512,1024]{1,0:T(8,128)(2,1)}, bf16[256,768]{1,0:T(8,128)(2,1)}, bf16[256,768]{1,0:T(8,128)(2,1)}) custom-call(s32[1]{0:T(128)} %bitcast.1.refs_0_.lab_ref, bf16[256,896]{1,0:T(8,128)(2,1)} %collective-permute-done.6.refs_1_.refs_5_.refs_9_, bf16[256,896]{1,0:T(8,128)(2,1)} %collective-permute-done.7.refs_2_.refs_6_.refs_10_, ...), custom_call_target="tpu_custom_call" | custom-call | flops 1610612736 | bytes 3072000 | tf_op jit(solution)/shard_map/first_grads/pallas_call | solution.py:157
  72.9 2.4 %collective-permute-start.11 = (bf16[256,768]{1,0:T(8,128)(2,1)}, bf16[256,768]{1,0:T(8,128)(2,1)}, u32[]{:S(2)}, u32[]{:S(2)}) collective-permute-start(bf16[256,768]{1,0:T(8,128)(2,1)} %get-tuple-element.33), channel_id=1, source_target_pairs={{0,3},{1,0},{2,1},{3,2},{4,7},{5,4},{6,5},{7,6},{8,11},{9,8},{10,9... | collective-permute-start | bytes 1179656 | tf_op jit(solution)/shard_map/ppermute | solution.py:300
  75.3 3.0 %collective-permute-done.10.refs_2_.refs_6_ = bf16[256,896]{1,0:T(8,128)(2,1)} collective-permute-done((bf16[256,896]{1,0:T(8,128)(2,1)}, bf16[256,896]{1,0:T(8,128)(2,1)}, u32[]{:S(2)}, u32[]{:S(2)}) %collective-permute-start.10) | collective-permute-done | bytes 458784 | tf_op jit(solution)/shard_map/ppermute | solution.py:334
  78.3 4.6 %first_grads.7 = (bf16[512,1024]{1,0:T(8,128)(2,1)}, bf16[512,768]{1,0:T(8,128)(2,1)}) custom-call(s32[1]{0:T(128)} %bitcast.1.refs_0_.lab_ref, bf16[256,896]{1,0:T(8,128)(2,1)} %collective-permute-done.5.refs_1_.refs_5_, bf16[256,896]{1,0:T(8,128)(2,1)} %collective-permute-done.10.refs_2_.refs_6_, bf16[2,1024,768]{2,1,0:T(8,128)(2,1)} %refs_2_.3), custom_call_target="tpu_custom_call" | custom-call | flops 1610612736 | bytes 3072000 | tf_op jit(solution)/shard_map/first_grads/pallas_call | solution.py:157
  84.7 4.6 %first_grads.5 = (bf16[512,1024]{1,0:T(8,128)(2,1)}, bf16[512,768]{1,0:T(8,128)(2,1)}) custom-call(s32[1]{0:T(128)} %bitcast.1.refs_0_.lab_ref, bf16[256,896]{1,0:T(8,128)(2,1)} %collective-permute-done.3.refs_1_.refs_3_.refs_7_, bf16[256,896]{1,0:T(8,128)(2,1)} %collective-permute-done.4.refs_2_.refs_4_.refs_8_, bf16[2,1024,768]{2,1,0:T(8,128)(2,1)} %refs_2_.3), custom_call_target="tpu_custom_call" | custom-call | flops 1610612736 | bytes 3072000 | tf_op jit(solution)/shard_map/first_grads/pallas_call | solution.py:157
  90.6 2.0 %add_convert_fusion.4 = bf16[256,768]{1,0:T(8,128)(2,1)} fusion(bf16[256,768]{1,0:T(8,128)(2,1)} %collective-permute-done.11, bf16[512,768]{1,0:T(8,128)(2,1)} %get-tuple-element.32), kind=kLoop, calls=%fused_computation.9 | loop fusion | flops 786432 | bytes 1179648 | tf_op jit(solution)/shard_map/convert_element_type | solution.py:293
  94.3 12.7 %second_grads.1 = (bf16[2048,1024]{1,0:T(8,128)(2,1)}, bf16[512,768]{1,0:T(8,128)(2,1)}, bf16[512,768]{1,0:T(8,128)(2,1)}, bf16[512,768]{1,0:T(8,128)(2,1)}, bf1...) custom-call(s32[1]{0:T(128)} %bitcast.1.refs_0_.lab_ref, bf16[32,64,768]{2,1,0:T(8,128)(2,1)} %copy-done, ...), custom_call_target="tpu_custom_call" | custom-call | flops 6442450944 | bytes 12288000 | tf_op jit(solution)/shard_map/second_grads/pallas_call | solution.py:209
  107.0 2.7 %collective-permute-start.15 = (bf16[256,768]{1,0:T(8,128)(2,1)}, bf16[256,768]{1,0:T(8,128)(2,1)S(1)}, u32[]{:S(2)}, u32[]{:S(2)}) collective-permute-start(bf16[256,768]{1,0:T(8,128)(2,1)} %get-tuple-element.39), channel_id=1, source_target_pairs={{0,3},{1,0},{2,1},{3,2},{4,7},{5,4},{6,5},{7,6},{8,11},{9,8},{10,9... | collective-permute-start | bytes 1179656 | tf_op jit(solution)/shard_map/ppermute | solution.py:300
  113.9 2.4 %collective-permute-done.15 = bf16[256,768]{1,0:T(8,128)(2,1)S(1)} collective-permute-done((bf16[256,768]{1,0:T(8,128)(2,1)}, bf16[256,768]{1,0:T(8,128)(2,1)S(1)}, u32[]{:S(2)}, u32[]{:S(2)}) %collective-permute-start.15) | collective-permute-done | bytes 393248 | tf_op jit(solution)/shard_map/ppermute | solution.py:300
  116.5 3.4 %collective-permute-start.16 = (bf16[512,768]{1,0:T(8,128)(2,1)S(1)}, bf16[512,768]{1,0:T(8,128)(2,1)}, u32[]{:S(2)}, u32[]{:S(2)}) collective-permute-start(bf16[512,768]{1,0:T(8,128)(2,1)S(1)} %pad_maximum_fusion.4), channel_id=1, source_target_pairs={{0,3},{1,0},{2,1},{3,2},{4,7},{5,4},{6,5},{7,6},{8,11},{9,8},{10,9... | collective-permute-start | bytes 2359304 | tf_op jit(solution)/shard_map/ppermute | solution.py:304
  122.0 4.6 %first_grads.4 = (bf16[512,1024]{1,0:T(8,128)(2,1)}, bf16[512,768]{1,0:T(8,128)(2,1)}) custom-call(s32[1]{0:T(128)} %bitcast.1.refs_0_.lab_ref, bf16[512,896]{1,0:T(8,128)(2,1)} %bitcast.13, bf16[2,1024,768]{2,1,0:T(8,128)(2,1)} %refs_2_.3), custom_call_target="tpu_custom_call" | custom-call | flops 1610612736 | bytes 3072000 | tf_op jit(solution)/shard_map/first_grads/pallas_call | solution.py:157
  126.5 6.5 %collective-permute-done.12 = bf16[512,768]{1,0:T(8,128)(2,1)} collective-permute-done((bf16[512,768]{1,0:T(8,128)(2,1)S(1)}, bf16[512,768]{1,0:T(8,128)(2,1)}, u32[]{:S(2)}, u32[]{:S(2)}) %collective-permute-start.12) | collective-permute-done | bytes 786464 | tf_op jit(solution)/shard_map/ppermute | solution.py:304
  133.1 5.6 %collective-permute-done.9 = bf16[512,768]{1,0:T(8,128)(2,1)} collective-permute-done((bf16[512,768]{1,0:T(8,128)(2,1)S(1)}, bf16[512,768]{1,0:T(8,128)(2,1)}, u32[]{:S(2)}, u32[]{:S(2)}) %collective-permute-start.9) | collective-permute-done | bytes 786464 | tf_op jit(solution)/shard_map/ppermute | solution.py:303
  140.7 9.2 %collective-permute-done.16 = bf16[512,768]{1,0:T(8,128)(2,1)} collective-permute-done((bf16[512,768]{1,0:T(8,128)(2,1)S(1)}, bf16[512,768]{1,0:T(8,128)(2,1)}, u32[]{:S(2)}, u32[]{:S(2)}) %collective-permute-start.16) | collective-permute-done | bytes 786464 | tf_op jit(solution)/shard_map/ppermute | solution.py:304
  149.9 5.6 %collective-permute-done.14 = bf16[512,768]{1,0:T(8,128)(2,1)} collective-permute-done((bf16[512,768]{1,0:T(8,128)(2,1)S(1)}, bf16[512,768]{1,0:T(8,128)(2,1)}, u32[]{:S(2)}, u32[]{:S(2)}) %collective-permute-start.14) | collective-permute-done | bytes 786464 | tf_op jit(solution)/shard_map/ppermute | solution.py:303
  158.6 10.0 %all-to-all-start.2 = ((bf16[32,16,1536]{2,1,0:T(8,128)(2,1)}), bf16[32,16,1536]{2,1,0:T(8,128)(2,1)S(1)}, u32[]{:S(2)}, u32[]{:S(2)}) async-start(bf16[32,16,1536]{2,1,0:T(8,128)(2,1)} %bitcast.6), calls=%async_computation.2 | async-start | bytes 3145728 | tf_op jit(solution)/shard_map/all_to_all | solution.py:286
  168.7 9.3 %update.2 = (bf16[2,1024,768]{2,1,0:T(8,128)(2,1)}, f32[2,1024,768]{2,1,0:T(8,128)}) custom-call(bf16[512,1024]{1,0:T(8,128)(2,1)} %get-tuple-element.41.refs_0_, bf16[512,1024]{1,0:T(8,128)(2,1)} %get-tuple-element.42.refs_1_, bf16[512,1024]{1,0:T(8,128)(2,1)} %get-tuple-element.43.refs_2_, bf16[512,1024]{1,0:T(8,128)(2,1)} %get-tuple-element.44.refs_3_, ...), custom_call_target="tpu_custom_call" | custom-call | flops 3221225472 | bytes 18874368 | tf_op jit(solution)/shard_map/update/pallas_call | solution.py:265
  178.0 9.2 %update.3 = (bf16[2,1024,768]{2,1,0:T(8,128)(2,1)}, f32[2,1024,768]{2,1,0:T(8,128)}) custom-call(bf16[2048,1024]{1,0:T(8,128)(2,1)} %get-tuple-element.40.refs_0_, bf16[2048,768]{1,0:T(8,128)(2,1)} %bitcast.9, bf16[2,1024,768]{2,1,0:T(8,128)(2,1)} %refs_2_.3, f32[2,1024,768]{2,1,0:T(8,128)} %refs_3_.7, ...), custom_call_target="tpu_custom_call", output_to_operand_aliasing={{0}: (4, {}), {1}: (5, {})} | custom-call | flops 3221225472 | bytes 18874368 | tf_op jit(solution)/shard_map/update/pallas_call | solution.py:265
  187.2 4.1 %all-to-all-done.2 = bf16[32,16,1536]{2,1,0:T(8,128)(2,1)S(1)} async-done(((bf16[32,16,1536]{2,1,0:T(8,128)(2,1)}), bf16[32,16,1536]{2,1,0:T(8,128)(2,1)S(1)}, u32[]{:S(2)}, u32[]{:S(2)}) %all-to-all-start.2) | async-done | bytes 1572896 | tf_op jit(solution)/shard_map/all_to_all | solution.py:286
  192.5 2.7 %home_sum.1 = f32[128,768]{1,0:T(8,128)} custom-call(s32[4,128]{1,0:T(4,128)} %bitcast.18, bf16[512,1536]{1,0:T(8,128)(2,1)} %bitcast.15), custom_call_target="tpu_custom_call" | custom-call | tf_op jit(solution)/shard_map/home_sum/pallas_call | solution.py:353
  (58 shorter events, 24.5 us)
Async XLA Ops:
  3.2 8.7 %copy-start.7 = (bf16[136,768]{1,0:T(8,128)(2,1)S(1)}, bf16[136,768]{1,0:T(8,128)(2,1)}, u32[]{:S(2)}) copy-start(bf16[136,768]{1,0:T(8,128)(2,1)} %get-tuple-element.27.refs_0_) | copy-start | bytes 626692
  3.2 28.2 %all-to-all-start = ((bf16[32,16,896]{2,1,0:T(8,128)(2,1)}), bf16[32,16,896]{2,1,0:T(8,128)(2,1)S(1)}, u32[]{:S(2)}, u32[]{:S(2)}) async-start(bf16[32,16,896]{2,1,0:T(8,128)(2,1)} %bitcast.16), calls=%async_computation | async-start | bytes 1835008 | tf_op jit(solution)/shard_map/all_to_all | solution.py:286
  12.0 9.1 %collective-permute-start = (bf16[136,768]{1,0:T(8,128)(2,1)S(1)}, bf16[136,768]{1,0:T(8,128)(2,1)S(1)}, u32[]{:S(2)}, u32[]{:S(2)}) collective-permute-start(bf16[136,768]{1,0:T(8,128)(2,1)S(1)} %copy-done.7), channel_id=1, source_target_pairs={{0,1},{1,2},{2,3},{3,0},{4,5},{5,6},{6,7},{7,4},{8,9},{9,10},{10,1... | collective-permute-start | bytes 626696 | tf_op jit(solution)/shard_map/ppermute | solution.py:321
  13.7 7.4 %collective-permute-start.1 = (bf16[136,768]{1,0:T(8,128)(2,1)S(1)}, bf16[136,768]{1,0:T(8,128)(2,1)S(1)}, u32[]{:S(2)}, u32[]{:S(2)}) collective-permute-start(bf16[136,768]{1,0:T(8,128)(2,1)S(1)} %copy-done.7), channel_id=1, source_target_pairs={{0,3},{1,0},{2,1},{3,2},{4,7},{5,4},{6,5},{7,6},{8,11},{9,8},{10,9... | collective-permute-start | bytes 626696 | tf_op jit(solution)/shard_map/ppermute | solution.py:321
  15.9 10.6 %collective-permute-start.2 = (bf16[136,768]{1,0:T(8,128)(2,1)S(1)}, bf16[136,768]{1,0:T(8,128)(2,1)S(1)}, u32[]{:S(2)}, u32[]{:S(2)}) collective-permute-start(bf16[136,768]{1,0:T(8,128)(2,1)S(1)} %copy-done.7), channel_id=1, source_target_pairs={{0,2},{1,3},{2,0},{3,1},{4,6},{5,7},{6,4},{7,5},{8,10},{9,11},{10,... | collective-permute-start | bytes 626696 | tf_op jit(solution)/shard_map/ppermute | solution.py:321
  21.1 5.4 %copy-start.8 = (bf16[136,768]{1,0:T(8,128)(2,1)}, bf16[136,768]{1,0:T(8,128)(2,1)S(1)}, u32[]{:S(2)}) copy-start(bf16[136,768]{1,0:T(8,128)(2,1)S(1)} %collective-permute-done.refs_1_) | copy-start | bytes 626692
  21.1 5.4 %copy-start.9 = (bf16[136,768]{1,0:T(8,128)(2,1)}, bf16[136,768]{1,0:T(8,128)(2,1)S(1)}, u32[]{:S(2)}) copy-start(bf16[136,768]{1,0:T(8,128)(2,1)S(1)} %collective-permute-done.1.refs_2_) | copy-start | bytes 626692
  26.5 0.7 copy-start.10
  31.4 0.9 copy-start.1
  32.3 60.3 %all-to-all-start.1 = ((bf16[32,64,768]{2,1,0:T(8,128)(2,1)}), bf16[32,64,768]{2,1,0:T(8,128)(2,1)S(1)}, u32[]{:S(2)}, u32[]{:S(2)}) async-start(bf16[32,64,768]{2,1,0:T(8,128)(2,1)} %bitcast.10), calls=%async_computation.1 | async-start | bytes 6291456 | tf_op jit(solution)/shard_map/all_to_all | solution.py:286
  42.6 13.4 %collective-permute-start.5 = (bf16[256,896]{1,0:T(8,128)(2,1)}, bf16[256,896]{1,0:T(8,128)(2,1)}, u32[]{:S(2)}, u32[]{:S(2)}) collective-permute-start(bf16[256,896]{1,0:T(8,128)(2,1)} %get-tuple-element.50), channel_id=1, source_target_pairs={{0,1},{1,2},{2,3},{3,0},{4,5},{5,6},{6,7},{7,4},{8,9},{9,10},{10,1... | collective-permute-start | bytes 1376264 | tf_op jit(solution)/shard_map/ppermute | solution.py:332
  43.5 12.5 %collective-permute-start.4 = (bf16[256,896]{1,0:T(8,128)(2,1)}, bf16[256,896]{1,0:T(8,128)(2,1)}, u32[]{:S(2)}, u32[]{:S(2)}) collective-permute-start(bf16[256,896]{1,0:T(8,128)(2,1)} %get-tuple-element.49), channel_id=1, source_target_pairs={{0,3},{1,0},{2,1},{3,2},{4,7},{5,4},{6,5},{7,6},{8,11},{9,8},{10,9... | collective-permute-start | bytes 1376264 | tf_op jit(solution)/shard_map/ppermute | solution.py:333
  56.0 12.5 %collective-permute-start.6 = (bf16[256,896]{1,0:T(8,128)(2,1)}, bf16[256,896]{1,0:T(8,128)(2,1)}, u32[]{:S(2)}, u32[]{:S(2)}) collective-permute-start(bf16[256,896]{1,0:T(8,128)(2,1)} %collective-permute-done.5.refs_1_.refs_5_), channel_id=1, source_target_pairs={{0,1},{1,2},{2,3},{3,0},{4,5},{5,6},{6,7},{7,4},{8,9},{9,10},{10,1... | collective-permute-start | bytes 1376264 | tf_op jit(solution)/shard_map/ppermute | solution.py:336
  56.0 12.5 %collective-permute-start.7 = (bf16[256,896]{1,0:T(8,128)(2,1)}, bf16[256,896]{1,0:T(8,128)(2,1)}, u32[]{:S(2)}, u32[]{:S(2)}) collective-permute-start(bf16[256,896]{1,0:T(8,128)(2,1)} %collective-permute-done.4.refs_2_.refs_4_.refs_8_), channel_id=1, source_target_pairs={{0,3},{1,0},{2,1},{3,2},{4,7},{5,4},{6,5},{7,6},{8,11},{9,8},{10,9... | collective-permute-start | bytes 1376264 | tf_op jit(solution)/shard_map/ppermute | solution.py:337
  58.7 19.7 %collective-permute-start.10 = (bf16[256,896]{1,0:T(8,128)(2,1)}, bf16[256,896]{1,0:T(8,128)(2,1)}, u32[]{:S(2)}, u32[]{:S(2)}) collective-permute-start(bf16[256,896]{1,0:T(8,128)(2,1)} %get-tuple-element.49), channel_id=1, source_target_pairs={{0,1},{1,2},{2,3},{3,0},{4,5},{5,6},{6,7},{7,4},{8,9},{9,10},{10,1... | collective-permute-start | bytes 1376264 | tf_op jit(solution)/shard_map/ppermute | solution.py:334
  58.7 26.0 %collective-permute-start.3 = (bf16[256,896]{1,0:T(8,128)(2,1)}, bf16[256,896]{1,0:T(8,128)(2,1)}, u32[]{:S(2)}, u32[]{:S(2)}) collective-permute-start(bf16[256,896]{1,0:T(8,128)(2,1)} %get-tuple-element.50), channel_id=1, source_target_pairs={{0,3},{1,0},{2,1},{3,2},{4,7},{5,4},{6,5},{7,6},{8,11},{9,8},{10,9... | collective-permute-start | bytes 1376264 | tf_op jit(solution)/shard_map/ppermute | solution.py:335
  72.9 17.7 %collective-permute-start.11 = (bf16[256,768]{1,0:T(8,128)(2,1)}, bf16[256,768]{1,0:T(8,128)(2,1)}, u32[]{:S(2)}, u32[]{:S(2)}) collective-permute-start(bf16[256,768]{1,0:T(8,128)(2,1)} %get-tuple-element.33), channel_id=1, source_target_pairs={{0,3},{1,0},{2,1},{3,2},{4,7},{5,4},{6,5},{7,6},{8,11},{9,8},{10,9... | collective-permute-start | bytes 1179656 | tf_op jit(solution)/shard_map/ppermute | solution.py:300
  90.3 20.8 %collective-permute-start.8 = (bf16[256,768]{1,0:T(8,128)(2,1)}, bf16[256,768]{1,0:T(8,128)(2,1)}, u32[]{:S(2)}, u32[]{:S(2)}) collective-permute-start(bf16[256,768]{1,0:T(8,128)(2,1)} %get-tuple-element.31), channel_id=1, source_target_pairs={{0,1},{1,2},{2,3},{3,0},{4,5},{5,6},{6,7},{7,4},{8,9},{9,10},{10,1... | collective-permute-start | bytes 1179656 | tf_op jit(solution)/shard_map/ppermute | solution.py:299
  92.6 1.6 copy-start
  107.0 4.1 %copy-start.4 = (bf16[512,768]{1,0:T(8,128)(2,1)S(1)}, bf16[512,768]{1,0:T(8,128)(2,1)}, u32[]{:S(2)}) copy-start(bf16[512,768]{1,0:T(8,128)(2,1)} %get-tuple-element.30) | copy-start | bytes 2359300
  107.0 5.3 %copy-start.11 = (bf16[256,768]{1,0:T(8,128)(2,1)S(1)}, bf16[256,768]{1,0:T(8,128)(2,1)}, u32[]{:S(2)}) copy-start(bf16[256,768]{1,0:T(8,128)(2,1)} %get-tuple-element.37) | copy-start | bytes 1179652
  107.0 9.3 %collective-permute-start.15 = (bf16[256,768]{1,0:T(8,128)(2,1)}, bf16[256,768]{1,0:T(8,128)(2,1)S(1)}, u32[]{:S(2)}, u32[]{:S(2)}) collective-permute-start(bf16[256,768]{1,0:T(8,128)(2,1)} %get-tuple-element.39), channel_id=1, source_target_pairs={{0,3},{1,0},{2,1},{3,2},{4,7},{5,4},{6,5},{7,6},{8,11},{9,8},{10,9... | collective-permute-start | bytes 1179656 | tf_op jit(solution)/shard_map/ppermute | solution.py:300
  110.9 2.9 %copy-start.5 = (bf16[512,768]{1,0:T(8,128)(2,1)S(1)}, bf16[512,768]{1,0:T(8,128)(2,1)}, u32[]{:S(2)}) copy-start(bf16[512,768]{1,0:T(8,128)(2,1)} %get-tuple-element.38) | copy-start | bytes 2359300
  110.9 2.9 %copy-start.3 = (bf16[512,768]{1,0:T(8,128)(2,1)S(1)}, bf16[512,768]{1,0:T(8,128)(2,1)}, u32[]{:S(2)}) copy-start(bf16[512,768]{1,0:T(8,128)(2,1)} %get-tuple-element.36) | copy-start | bytes 2359300
  110.9 22.1 %collective-permute-start.12 = (bf16[512,768]{1,0:T(8,128)(2,1)S(1)}, bf16[512,768]{1,0:T(8,128)(2,1)}, u32[]{:S(2)}, u32[]{:S(2)}) collective-permute-start(bf16[512,768]{1,0:T(8,128)(2,1)S(1)} %pad_maximum_fusion.2), channel_id=1, source_target_pairs={{0,3},{1,0},{2,1},{3,2},{4,7},{5,4},{6,5},{7,6},{8,11},{9,8},{10,9... | collective-permute-start | bytes 2359304 | tf_op jit(solution)/shard_map/ppermute | solution.py:304
  112.3 9.4 %collective-permute-start.13 = (bf16[256,768]{1,0:T(8,128)(2,1)S(1)}, bf16[256,768]{1,0:T(8,128)(2,1)S(1)}, u32[]{:S(2)}, u32[]{:S(2)}) collective-permute-start(bf16[256,768]{1,0:T(8,128)(2,1)S(1)} %copy-done.11), channel_id=1, source_target_pairs={{0,1},{1,2},{2,3},{3,0},{4,5},{5,6},{6,7},{7,4},{8,9},{9,10},{10,1... | collective-permute-start | bytes 1179656 | tf_op jit(solution)/shard_map/ppermute | solution.py:299
  113.7 25.0 %collective-permute-start.9 = (bf16[512,768]{1,0:T(8,128)(2,1)S(1)}, bf16[512,768]{1,0:T(8,128)(2,1)}, u32[]{:S(2)}, u32[]{:S(2)}) collective-permute-start(bf16[512,768]{1,0:T(8,128)(2,1)S(1)} %pad_maximum_fusion.1), channel_id=1, source_target_pairs={{0,1},{1,2},{2,3},{3,0},{4,5},{5,6},{6,7},{7,4},{8,9},{9,10},{10,1... | collective-permute-start | bytes 2359304 | tf_op jit(solution)/shard_map/ppermute | solution.py:303
  116.5 33.4 %collective-permute-start.16 = (bf16[512,768]{1,0:T(8,128)(2,1)S(1)}, bf16[512,768]{1,0:T(8,128)(2,1)}, u32[]{:S(2)}, u32[]{:S(2)}) collective-permute-start(bf16[512,768]{1,0:T(8,128)(2,1)S(1)} %pad_maximum_fusion.4), channel_id=1, source_target_pairs={{0,3},{1,0},{2,1},{3,2},{4,7},{5,4},{6,5},{7,6},{8,11},{9,8},{10,9... | collective-permute-start | bytes 2359304 | tf_op jit(solution)/shard_map/ppermute | solution.py:304
  121.9 33.7 %collective-permute-start.14 = (bf16[512,768]{1,0:T(8,128)(2,1)S(1)}, bf16[512,768]{1,0:T(8,128)(2,1)}, u32[]{:S(2)}, u32[]{:S(2)}) collective-permute-start(bf16[512,768]{1,0:T(8,128)(2,1)S(1)} %pad_maximum_fusion.3), channel_id=1, source_target_pairs={{0,1},{1,2},{2,3},{3,0},{4,5},{5,6},{6,7},{7,4},{8,9},{9,10},{10,1... | collective-permute-start | bytes 2359304 | tf_op jit(solution)/shard_map/ppermute | solution.py:303
  138.7 16.9 %copy-start.6 = (bf16[512,768]{1,0:T(8,128)(2,1)S(1)}, bf16[512,768]{1,0:T(8,128)(2,1)}, u32[]{:S(2)}) copy-start(bf16[512,768]{1,0:T(8,128)(2,1)} %get-tuple-element.35) | copy-start | bytes 2359300
  158.6 32.7 %all-to-all-start.2 = ((bf16[32,16,1536]{2,1,0:T(8,128)(2,1)}), bf16[32,16,1536]{2,1,0:T(8,128)(2,1)S(1)}, u32[]{:S(2)}, u32[]{:S(2)}) async-start(bf16[32,16,1536]{2,1,0:T(8,128)(2,1)} %bitcast.6), calls=%async_computation.2 | async-start | bytes 3145728 | tf_op jit(solution)/shard_map/all_to_all | solution.py:286
  191.3 1.2 copy-start.2

commit v6 on v5

--- a/solution.py
+++ b/solution.py
@@ -18,8 +18,6 @@
 EXTRA = 8
 TAGS = 128
 TILE = 256
-SRC = TILE // (LAB * CAP)
-STEPS = CLUS // SRC
 LABELS = 1024
 BAND = 256
 ROWS = CLUS * CAP
@@ -170,63 +168,58 @@
     )(lab, *pieces, weights)
 
 
-def second_kernel(lab_ref, rows_ref, *refs):
-    notes_refs, w_ref, grad_ref, parts = refs[:7], refs[7], refs[8], refs[9:]
-    step = pl.program_id(0)
-    early = step < STEPS // 2
-    f32 = jnp.float32
-    notes = [notes_refs[0][...].astype(f32)]
-    for k in range(1, 7, 2):
-        notes.append(
-            jnp.where(early, notes_refs[k][...].astype(f32), notes_refs[k + 1][...].astype(f32))
-        )
-    notes = jnp.stack([x.reshape(SRC, CAP, TAGS) for x in notes], axis=1).reshape(TILE, TAGS)
+def second_kernel(near, lab_ref, rows_ref, *refs):
+    count = 5 if near else 2
+    notes_refs, w_ref, grad_ref, parts = refs[:count], refs[count], refs[count + 1], refs[count + 2 :]
+    block, early = pl.program_id(0), pl.program_id(1) == 0
+    notes = [ref[...].astype(jnp.float32) for ref in notes_refs]
+    pair = lambda k: jnp.where(early, notes[k], notes[k + 1])
+    if near:
+        notes = jnp.where(block == 0, notes[0], jnp.where(block == 1, pair(1), pair(3)))
+    else:
+        notes = pair(0)
     rows = rows_ref[...].reshape(TILE, D)
     grad, part = tile_grads(rows, notes[:, 2:3], notes[:, 3:4], lab_ref[0] * LABELS, w_ref)
     grad_ref[...] = grad
-    part = part.reshape(SRC, LAB, CAP, D)
-    for k in range(3):
-        parts[k][...] = part[:, k].reshape(SRC * CAP, D)
+    if near:
+        parts[0][0] = part
+        return
 
     @pl.when(early)
     def _():
-        parts[3][...] = part[:, 3].reshape(SRC * CAP, D)
+        parts[0][...] = part
 
     @pl.when(jnp.logical_not(early))
     def _():
-        parts[4][...] = part[:, 3].reshape(SRC * CAP, D)
-
-
-def second_grads(lab, rows, pieces, weights):
-    n = LAB * ROWS
+        parts[1][...] = part
+
+
+def second_grads(lab, rows, blocks, weights, near):
     bf = jnp.bfloat16
-    last = STEPS // 2 - 1
-    here = SRC * CAP
-    each = lambda i: (i, D // TAGS)
-    early = lambda i: (jnp.minimum(i, last), D // TAGS)
-    late = lambda i: (jnp.maximum(i - last - 1, 0), D // TAGS)
-    note = lambda at: pl.BlockSpec((here, TAGS), at)
+    pieces = [p for block in blocks for p in block]
+    first, count = (0, LAB - 1) if near else (LAB - 1, 1)
+    n = count * ROWS
+    source = TILE // CAP
+    still = pl.BlockSpec((TILE, TAGS), lambda k, i: (0, D // TAGS))
+    each = pl.BlockSpec((TILE, TAGS), lambda k, i: (i, D // TAGS))
+    if near:
+        part_specs = [pl.BlockSpec((1, TILE, D), lambda k, i: (k, i, 0))]
+        part_shapes = [jax.ShapeDtypeStruct((count, ROWS, D), bf)]
+    else:
+        part_specs = [whole((TILE, D))] * 2
+        part_shapes = [jax.ShapeDtypeStruct((TILE, D), bf)] * 2
     return pl.pallas_call(
-        second_kernel,
-        grid=(STEPS,),
+        lambda *refs: second_kernel(near, *refs),
+        grid=(count, 2),
         in_specs=[
             pl.BlockSpec(memory_space=pltpu.SMEM),
-            pl.BlockSpec((SRC, LAB * CAP, D), lambda i: (i, 0, 0)),
-            note(each),
+            pl.BlockSpec((source, CAP, D), lambda k, i: (i, first + k, 0)),
         ]
-        + [note(early), note(late)] * 3
-        + [pl.BlockSpec((1, LABELS, D), lambda i: (1, 0, 0))],
-        out_specs=(
-            pl.BlockSpec((TILE, LABELS), lambda i: (i, 0)),
-            pl.BlockSpec((here, D), lambda i: (i, 0)),
-            pl.BlockSpec((here, D), lambda i: (i, 0)),
-            pl.BlockSpec((here, D), lambda i: (i, 0)),
-            pl.BlockSpec((here, D), lambda i: (jnp.minimum(i, last), 0)),
-            pl.BlockSpec((here, D), lambda i: (jnp.maximum(i - last - 1, 0), 0)),
-        ),
-        out_shape=(jax.ShapeDtypeStruct((n, LABELS), bf),)
-        + (jax.ShapeDtypeStruct((ROWS, D), bf),) * 3
-        + (jax.ShapeDtypeStruct((ROWS // 2, D), bf),) * 2,
+        + ([each] if near else [])
+        + [still] * (4 if near else 2)
+        + [pl.BlockSpec((1, LABELS, D), lambda k, i: (1, 0, 0))],
+        out_specs=[pl.BlockSpec((TILE, LABELS), lambda k, i: (2 * k + i, 0))] + part_specs,
+        out_shape=[jax.ShapeDtypeStruct((n, LABELS), bf)] + part_shapes,
         cost_estimate=pl.CostEstimate(
             flops=4 * n * LABELS * D, bytes_accessed=2 * n * 3000, transcendentals=n * LABELS
         ),
@@ -236,22 +229,31 @@
 
 def update_kernel(counts, *refs):
     grads, rest = refs[: len(counts)], refs[len(counts) :]
-    rows, rest = rest[: sum(counts)], rest[sum(counts) :]
+    many = max(sum(counts), 1)
+    rows, rest = rest[:many], rest[many:]
     w_ref, m_ref, wo_ref, mo_ref = rest[0], rest[1], rest[-2], rest[-1]
+    terms = []
+    if sum(counts):
+        k = 0
+        for grad_ref, count in zip(grads, counts):
+            at = 0
+            for rows_ref in rows[k : k + count]:
+                size = rows_ref.shape[0]
+                terms.append((grad_ref[at : at + size], rows_ref[:, :D]))
+                at += size
+            k += count
+    else:
+        k = 0
+        for grad_ref in grads:
+            for at in range(0, grad_ref.shape[0], ROWS):
+                slots = rows[0][:, k * CAP : (k + 1) * CAP].reshape(ROWS, D)
+                terms.append((grad_ref[at : at + ROWS], slots))
+                k += 1
     fresh = momentum_decay * m_ref[0]
-    k = 0
-    for grad_ref, count in zip(grads, counts):
-        at = 0
-        for rows_ref in rows[k : k + count]:
-            size = rows_ref.shape[0]
-            fresh = fresh + lax.dot_general(
-                grad_ref[at : at + size],
-                rows_ref[:, :D],
-                (((0,), (0,)), ((), ())),
-                preferred_element_type=jnp.float32,
-            )
-            at += size
-        k += count
+    for grad, values in terms:
+        fresh = fresh + lax.dot_general(
+            grad, values, (((0,), (0,)), ((), ())), preferred_element_type=jnp.float32
+        )
     mo_ref[0] = fresh
     wo_ref[0] = (w_ref[0].astype(jnp.float32) - step_rate * fresh).astype(jnp.bfloat16)
 
@@ -259,8 +261,9 @@
 def update(cluster, grads, blocks, weights, momentum, before=()):
     bands = LABELS // BAND
     band = pl.BlockSpec((1, BAND, D), lambda b: (cluster, b, 0))
-    counts = tuple(len(block) for block in blocks)
-    rows = [piece for block in blocks for piece in block]
+    shared = not isinstance(blocks, tuple)
+    counts = (0,) * len(grads) if shared else tuple(len(block) for block in blocks)
+    rows = [blocks] if shared else [piece for block in blocks for piece in block]
     first = len(grads) + len(rows) + 2
     return pl.pallas_call(
         lambda *refs: update_kernel(counts, *refs),
@@ -342,14 +345,13 @@
         grads_a.append(grad)
         parts_a += parts
     home_a = ring_sum(parts_a)
-    pieces = [p for block in blocks for p in block]
-    grad_b, *parts_b = second_grads(lab, got_b, pieces, weights)
-    home_b = ring_sum(parts_b)
+    grad_far, *far_b_parts = second_grads(lab, got_b, blocks[3:], weights, near=False)
+    grad_near, parts_near = second_grads(lab, got_b, blocks[:3], weights, near=True)
+    home_b = ring_sum([parts_near[0], parts_near[1], parts_near[2]] + far_b_parts)
     both = jnp.concatenate([home_a, home_b], axis=1).reshape(CLUS, CAP, 2 * D)
     both = swap(both).reshape(ROWS, 2 * D)
     new = update(0, grads_a, blocks, weights, momentum)
-    rows_b = ((got_b.reshape(LAB * ROWS, D),),)
-    new = update(1, (grad_b,), rows_b, weights, momentum, new)
+    new = update(1, (grad_near, grad_far), got_b, weights, momentum, new)
     query_grad = pl.pallas_call(
         home_kernel, out_shape=jax.ShapeDtypeStruct((NQ, D), jnp.float32), name="home_sum"
     )(vt, both)

time: 196 us -> 181 us (0.923)
  waiting for transfers between devices: 65.8 us -> 49.4 us
  Pallas kernels: 59 us -> 61.1 us
    ppermute x2, waiting for transfers between devices: 11.3 us -> 1.36 us  [ring_sum(): up = lax.ppermute(up, 'lab', ring(1))]
    ppermute x2, waiting for transfers between devices: 15.8 us -> 7.69 us  [ring_sum(): down = lax.ppermute(down, 'lab', ring(-1))]
    ppermute x2, waiting for transfers between devices: 1.9 us -> 5.95 us  [ring_sum(): up = lax.ppermute(far_a, 'lab', ring(1))]
    ppermute x2, waiting for transfers between devices: 2.43 us -> 0.01 us  [ring_sum(): down = lax.ppermute(far_b, 'lab', ring(-1))]
    pallas_call x1 -> x2, Pallas kernels: 12.7 us -> 14.9 us  [second_grads(): pl.pallas_call(lambda *refs: second_kernel(near, *refs), grid=(count, 2),...]
    convert_element_type x6 -> x5, other arithmetic: 7.02 us -> 5.87 us  [add(): return total.astype(jnp.bfloat16)]
    unnamed x24 -> x18, local copies, waits for them, and re-layouts: 4.47 us -> 4.45 us
  transfers between devices with their start and end apart: 20 -> 20, of which waited for: 12 -> 9; matrix products, arithmetic and copies ran while one was open for 6% -> 7% of each run, Pallas kernels for 27% -> 31%
where the time goes in v6:
time: 181 us; the launch traced here: 180 us
  Pallas kernels  61.1 us (34%)
  starting transfers between devices  50.1 us (28%)
  waiting for transfers between devices  49.4 us (27%)
  local copies, waits for them, and re-layouts  9.91 us (5%)
  other arithmetic  9.14 us (5%)
    all_to_all x3, starting transfers between devices, swap(): return lax.all_to_all(x, 'clus', split_axis=0, concat_axis=0, tiled=True)  27.5 us
    pallas_call x2, Pallas kernels, update(): pl.pallas_call(lambda *refs: update_kernel(counts, *refs), grid=(bands,),...  18.4 us
    pallas_call x4, Pallas kernels, first_grads(): pl.pallas_call(lambda *refs: first_kernel(count, *refs), grid=(1,), in_sp...  18.2 us
    pallas_call x2, Pallas kernels, second_grads(): pl.pallas_call(lambda *refs: second_kernel(near, *refs), grid=(count, 2),...  14.9 us
    ppermute x1, waiting for transfers between devices, step(): low_a = lax.ppermute(got_a[:half], 'lab', ring(1))  10.7 us
    ppermute x3, waiting for transfers between devices, step(): peers = [raw] + [lax.ppermute(raw, 'lab', ring(s)) for s in (1, -1, 2)]  9.37 us
    ppermute x2, waiting for transfers between devices, ring_sum(): down = lax.ppermute(down, 'lab', ring(-1))  7.69 us
    ppermute x1, waiting for transfers between devices, step(): far_a = lax.ppermute(low_a, 'lab', ring(1))  7.15 us
  transfers between devices with their start and end apart: 20, of which 9 were waited for; matrix products, arithmetic and copies ran while one was open for 7% of the time, Pallas kernels for 31%

profile of v6, /device:TPU:1, one launch (start us, length us, event | category | flops | bytes accessed | tf_op | source)
XLA Modules:
  0.0 180.5 jit_solution(6479791542112648669)
XLA Ops:
  0.6 2.6 %own_box.1 = (bf16[512,896]{1,0:T(8,128)(2,1)}, bf16[136,768]{1,0:T(8,128)(2,1)}) custom-call(s32[4,128]{1,0:T(4,128)} %bitcast.28, s32[4,128]{1,0:T(4,128)} %bitcast.30, bf16[128,768]{1,0:T(8,128)(2,1)} %queries_ref.1), custom_call_target="tpu_custom_call" | custom-call | tf_op jit(solution)/shard_map/own_box/pallas_call | solution.py:316
  3.2 8.7 %all-to-all-start = ((bf16[32,16,896]{2,1,0:T(8,128)(2,1)}), bf16[32,16,896]{2,1,0:T(8,128)(2,1)S(1)}, u32[]{:S(2)}, u32[]{:S(2)}) async-start(bf16[32,16,896]{2,1,0:T(8,128)(2,1)} %bitcast.27), calls=%async_computation | async-start | bytes 1835008 | tf_op jit(solution)/shard_map/all_to_all | solution.py:289
  12.0 1.7 collective-permute-start
  13.7 2.2 %collective-permute-start.1 = (bf16[136,768]{1,0:T(8,128)(2,1)S(1)}, bf16[136,768]{1,0:T(8,128)(2,1)S(1)}, u32[]{:S(2)}, u32[]{:S(2)}) collective-permute-start(bf16[136,768]{1,0:T(8,128)(2,1)S(1)} %copy-done.5), channel_id=1, source_target_pairs={{0,3},{1,0},{2,1},{3,2},{4,7},{5,4},{6,5},{7,6},{8,11},{9,8},{10,9... | collective-permute-start | bytes 626696 | tf_op jit(solution)/shard_map/ppermute | solution.py:324
  17.1 4.0 %collective-permute-done.refs_1_ = bf16[136,768]{1,0:T(8,128)(2,1)S(1)} collective-permute-done((bf16[136,768]{1,0:T(8,128)(2,1)S(1)}, bf16[136,768]{1,0:T(8,128)(2,1)S(1)}, u32[]{:S(2)}, u32[]{:S(2)}) %collective-permute-start) | collective-permute-done | bytes 208928 | tf_op jit(solution)/shard_map/ppermute | solution.py:324
  21.1 5.4 %collective-permute-done.2.refs_3_ = bf16[136,768]{1,0:T(8,128)(2,1)S(1)} collective-permute-done((bf16[136,768]{1,0:T(8,128)(2,1)S(1)}, bf16[136,768]{1,0:T(8,128)(2,1)S(1)}, u32[]{:S(2)}, u32[]{:S(2)}) %collective-permute-start.2) | collective-permute-done | bytes 208928 | tf_op jit(solution)/shard_map/ppermute | solution.py:324
  27.2 4.2 %all_box.1 = bf16[32,4,16,768]{3,2,1,0:T(8,128)(2,1)} custom-call(bf16[136,768]{1,0:T(8,128)(2,1)} %get-tuple-element.26.refs_0_, bf16[136,768]{1,0:T(8,128)(2,1)} %copy-done.6, bf16[136,768]{1,0:T(8,128)(2,1)} %copy-done.7, bf16[136,768]{1,0:T(8,128)(2,1)} %copy-done.8), custom_call_target="tpu_custom_call" | custom-call | tf_op jit(solution)/shard_map/all_box/pallas_call | solution.py:326
  32.3 8.1 %all-to-all-start.1 = ((bf16[32,64,768]{2,1,0:T(8,128)(2,1)}), bf16[32,64,768]{2,1,0:T(8,128)(2,1)S(1)}, u32[]{:S(2)}, u32[]{:S(2)}) async-start(bf16[32,64,768]{2,1,0:T(8,128)(2,1)} %bitcast.21), calls=%async_computation.1 | async-start | bytes 6291456 | tf_op jit(solution)/shard_map/all_to_all | solution.py:289
  40.4 2.2 %fusion.4 = (bf16[256,896]{1,0:T(8,128)(2,1)}, bf16[256,896]{1,0:T(8,128)(2,1)}) fusion(bf16[512,896]{1,0:T(8,128)(2,1)} %bitcast.22), kind=kLoop, calls=%fused_computation.17 | loop fusion | bytes 1835008 | tf_op jit(solution)/shard_map/slice | solution.py:336
  43.5 1.8 %collective-permute-start.4 = (bf16[256,896]{1,0:T(8,128)(2,1)}, bf16[256,896]{1,0:T(8,128)(2,1)}, u32[]{:S(2)}, u32[]{:S(2)}) collective-permute-start(bf16[256,896]{1,0:T(8,128)(2,1)} %get-tuple-element.51), channel_id=1, source_target_pairs={{0,3},{1,0},{2,1},{3,2},{4,7},{5,4},{6,5},{7,6},{8,11},{9,8},{10,9... | collective-permute-start | bytes 1376264 | tf_op jit(solution)/shard_map/ppermute | solution.py:336
  45.3 10.7 %collective-permute-done.5.refs_1_.refs_3_.refs_5_ = bf16[256,896]{1,0:T(8,128)(2,1)} collective-permute-done((bf16[256,896]{1,0:T(8,128)(2,1)}, bf16[256,896]{1,0:T(8,128)(2,1)}, u32[]{:S(2)}, u32[]{:S(2)}) %collective-permute-start.5) | collective-permute-done | bytes 458784 | tf_op jit(solution)/shard_map/ppermute | solution.py:335
  56.0 2.7 %collective-permute-start.7 = (bf16[256,896]{1,0:T(8,128)(2,1)}, bf16[256,896]{1,0:T(8,128)(2,1)}, u32[]{:S(2)}, u32[]{:S(2)}) collective-permute-start(bf16[256,896]{1,0:T(8,128)(2,1)} %collective-permute-done.4.refs_2_.refs_6_.refs_8_), channel_id=1, source_target_pairs={{0,3},{1,0},{2,1},{3,2},{4,7},{5,4},{6,5},{7,6},{8,11},{9,8},{10,9... | collective-permute-start | bytes 1376264 | tf_op jit(solution)/shard_map/ppermute | solution.py:340
  58.7 2.7 %collective-permute-start.3 = (bf16[256,896]{1,0:T(8,128)(2,1)}, bf16[256,896]{1,0:T(8,128)(2,1)}, u32[]{:S(2)}, u32[]{:S(2)}) collective-permute-start(bf16[256,896]{1,0:T(8,128)(2,1)} %get-tuple-element.52), channel_id=1, source_target_pairs={{0,3},{1,0},{2,1},{3,2},{4,7},{5,4},{6,5},{7,6},{8,11},{9,8},{10,9... | collective-permute-start | bytes 1376264 | tf_op jit(solution)/shard_map/ppermute | solution.py:338
  61.3 7.2 %collective-permute-done.6.refs_1_.refs_2_.refs_9_ = bf16[256,896]{1,0:T(8,128)(2,1)} collective-permute-done((bf16[256,896]{1,0:T(8,128)(2,1)}, bf16[256,896]{1,0:T(8,128)(2,1)}, u32[]{:S(2)}, u32[]{:S(2)}) %collective-permute-start.6) | collective-permute-done | bytes 458784 | tf_op jit(solution)/shard_map/ppermute | solution.py:339
  68.5 4.4 %first_grads.6 = (bf16[512,1024]{1,0:T(8,128)(2,1)}, bf16[256,768]{1,0:T(8,128)(2,1)}, bf16[256,768]{1,0:T(8,128)(2,1)}) custom-call(s32[1]{0:T(128)} %bitcast.1.refs_0_, bf16[256,896]{1,0:T(8,128)(2,1)} %collective-permute-done.6.refs_1_.refs_2_.refs_9_, bf16[256,896]{1,0:T(8,128)(2,1)} %collective-permute-done.7.refs_2_.refs_3_.refs_10_, ...), custom_call_target="tpu_custom_call" | custom-call | flops 1610612736 | bytes 3072000 | tf_op jit(solution)/shard_map/first_grads/pallas_call | solution.py:155
  72.9 2.4 %collective-permute-start.11 = (bf16[256,768]{1,0:T(8,128)(2,1)}, bf16[256,768]{1,0:T(8,128)(2,1)}, u32[]{:S(2)}, u32[]{:S(2)}) collective-permute-start(bf16[256,768]{1,0:T(8,128)(2,1)} %get-tuple-element.32), channel_id=1, source_target_pairs={{0,3},{1,0},{2,1},{3,2},{4,7},{5,4},{6,5},{7,6},{8,11},{9,8},{10,9... | collective-permute-start | bytes 1179656 | tf_op jit(solution)/shard_map/ppermute | solution.py:303
  75.3 3.0 %collective-permute-done.10.refs_2_.refs_4_.refs_6_ = bf16[256,896]{1,0:T(8,128)(2,1)} collective-permute-done((bf16[256,896]{1,0:T(8,128)(2,1)}, bf16[256,896]{1,0:T(8,128)(2,1)}, u32[]{:S(2)}, u32[]{:S(2)}) %collective-permute-start.10) | collective-permute-done | bytes 458784 | tf_op jit(solution)/shard_map/ppermute | solution.py:337
  78.3 4.6 %first_grads.7 = (bf16[512,1024]{1,0:T(8,128)(2,1)}, bf16[512,768]{1,0:T(8,128)(2,1)}) custom-call(s32[1]{0:T(128)} %bitcast.1.refs_0_, bf16[256,896]{1,0:T(8,128)(2,1)} %collective-permute-done.5.refs_1_.refs_3_.refs_5_, bf16[256,896]{1,0:T(8,128)(2,1)} %collective-permute-done.10.refs_2_.refs_4_.refs_6_, bf16[2,1024,768]{2,1,0:T(8,128)(2,1)} %refs_3_.7), custom_call_target="tpu_custom_call" | custom-call | flops 1610612736 | bytes 3072000 | tf_op jit(solution)/shard_map/first_grads/pallas_call | solution.py:155
  82.9 4.6 %first_grads.5 = (bf16[512,1024]{1,0:T(8,128)(2,1)}, bf16[512,768]{1,0:T(8,128)(2,1)}) custom-call(s32[1]{0:T(128)} %bitcast.1.refs_0_, bf16[256,896]{1,0:T(8,128)(2,1)} %collective-permute-done.3.refs_1_.refs_5_.refs_7_, bf16[256,896]{1,0:T(8,128)(2,1)} %collective-permute-done.4.refs_2_.refs_6_.refs_8_, bf16[2,1024,768]{2,1,0:T(8,128)(2,1)} %refs_3_.7), custom_call_target="tpu_custom_call" | custom-call | flops 1610612736 | bytes 3072000 | tf_op jit(solution)/shard_map/first_grads/pallas_call | solution.py:155
  91.8 2.7 %collective-permute-start.12 = (bf16[512,768]{1,0:T(8,128)(2,1)}, bf16[512,768]{1,0:T(8,128)(2,1)}, u32[]{:S(2)}, u32[]{:S(2)}) collective-permute-start(bf16[512,768]{1,0:T(8,128)(2,1)} %pad_maximum_fusion.2), channel_id=1, source_target_pairs={{0,3},{1,0},{2,1},{3,2},{4,7},{5,4},{6,5},{7,6},{8,11},{9,8},{10,9... | collective-permute-start | bytes 2359304 | tf_op jit(solution)/shard_map/ppermute | solution.py:307
  97.2 5.1 %second_grads.3 = (bf16[512,1024]{1,0:T(8,128)(2,1)}, bf16[256,768]{1,0:T(8,128)(2,1)}, bf16[256,768]{1,0:T(8,128)(2,1)}) custom-call(s32[1]{0:T(128)} %bitcast.1.refs_0_, bf16[32,64,768]{2,1,0:T(8,128)(2,1)} %copy-done, bf16[256,896]{1,0:T(8,128)(2,1)} %collective-permute-done.6.refs_1_.refs_2_.refs_9_, ...), custom_call_target="tpu_custom_call" | custom-call | flops 1610612736 | bytes 3072000 | tf_op jit(solution)/shard_map/second_grads/pallas_call | solution.py:211
  102.3 2.7 %collective-permute-start.15 = (bf16[256,768]{1,0:T(8,128)(2,1)}, bf16[256,768]{1,0:T(8,128)(2,1)S(1)}, u32[]{:S(2)}, u32[]{:S(2)}) collective-permute-start(bf16[256,768]{1,0:T(8,128)(2,1)} %get-tuple-element.36), channel_id=1, source_target_pairs={{0,3},{1,0},{2,1},{3,2},{4,7},{5,4},{6,5},{7,6},{8,11},{9,8},{10,9... | collective-permute-start | bytes 1179656 | tf_op jit(solution)/shard_map/ppermute | solution.py:303
  105.0 9.8 %second_grads.2 = (bf16[1536,1024]{1,0:T(8,128)(2,1)}, bf16[3,512,768]{2,1,0:T(8,128)(2,1)}) custom-call(s32[1]{0:T(128)} %bitcast.1.refs_0_, bf16[32,64,768]{2,1,0:T(8,128)(2,1)} %copy-done, bf16[512,896]{1,0:T(8,128)(2,1)} %bitcast.23, bf16[256,896]{1,0:T(8,128)(2,1)} %collective-permute-done.5.refs_1_.refs_3_.refs_5_, ...), custom_call_target="tpu_custom_call" | custom-call | flops 4831838208 | bytes 9216000 | tf_op jit(solution)/shard_map/second_grads/pallas_call | solution.py:211
  116.0 5.9 %collective-permute-done.13 = bf16[256,768]{1,0:T(8,128)(2,1)S(1)} collective-permute-done((bf16[256,768]{1,0:T(8,128)(2,1)}, bf16[256,768]{1,0:T(8,128)(2,1)S(1)}, u32[]{:S(2)}, u32[]{:S(2)}) %collective-permute-start.13) | collective-permute-done | bytes 393248 | tf_op jit(solution)/shard_map/ppermute | solution.py:302
  125.0 4.6 %first_grads.4 = (bf16[512,1024]{1,0:T(8,128)(2,1)}, bf16[512,768]{1,0:T(8,128)(2,1)}) custom-call(s32[1]{0:T(128)} %bitcast.1.refs_0_, bf16[512,896]{1,0:T(8,128)(2,1)} %bitcast.24, bf16[2,1024,768]{2,1,0:T(8,128)(2,1)} %refs_3_.7), custom_call_target="tpu_custom_call" | custom-call | flops 1610612736 | bytes 3072000 | tf_op jit(solution)/shard_map/first_grads/pallas_call | solution.py:155
  129.5 1.9 %add_convert_fusion = bf16[512,768]{1,0:T(8,128)(2,1)S(1)} fusion(bf16[512,768]{1,0:T(8,128)(2,1)} %collective-permute-done.12, bf16[512,768]{1,0:T(8,128)(2,1)} %collective-permute-done.9, bf16[512,768]{1,0:T(8,128)(2,1)} %get-tuple-element.28), kind=kLoop, calls=%fused_computation.4 | loop fusion | flops 2359296 | bytes 3145728 | tf_op jit(solution)/shard_map/convert_element_type | solution.py:296
  131.4 7.7 %collective-permute-done.16 = bf16[512,768]{1,0:T(8,128)(2,1)S(1)} collective-permute-done((bf16[512,768]{1,0:T(8,128)(2,1)S(1)}, bf16[512,768]{1,0:T(8,128)(2,1)S(1)}, u32[]{:S(2)}, u32[]{:S(2)}) %collective-permute-start.16) | collective-permute-done | bytes 786464 | tf_op jit(solution)/shard_map/ppermute | solution.py:307
  143.2 10.7 %all-to-all-start.2 = ((bf16[32,16,1536]{2,1,0:T(8,128)(2,1)}), bf16[32,16,1536]{2,1,0:T(8,128)(2,1)S(1)}, u32[]{:S(2)}, u32[]{:S(2)}) async-start(bf16[32,16,1536]{2,1,0:T(8,128)(2,1)} %bitcast.11), calls=%async_computation.2 | async-start | bytes 3145728 | tf_op jit(solution)/shard_map/all_to_all | solution.py:289
  153.9 9.3 %update.2 = (bf16[2,1024,768]{2,1,0:T(8,128)(2,1)}, f32[2,1024,768]{2,1,0:T(8,128)}) custom-call(bf16[512,1024]{1,0:T(8,128)(2,1)} %get-tuple-element.39.refs_0_, bf16[512,1024]{1,0:T(8,128)(2,1)} %get-tuple-element.40.refs_1_, bf16[512,1024]{1,0:T(8,128)(2,1)} %get-tuple-element.41.refs_2_, bf16[512,1024]{1,0:T(8,128)(2,1)} %get-tuple-element.42.refs_3_, ...), custom_call_target="tpu_custom_call" | custom-call | flops 3221225472 | bytes 18874368 | tf_op jit(solution)/shard_map/update/pallas_call | solution.py:268
  163.3 9.1 %update.3 = (bf16[2,1024,768]{2,1,0:T(8,128)(2,1)}, f32[2,1024,768]{2,1,0:T(8,128)}) custom-call(bf16[1536,1024]{1,0:T(8,128)(2,1)} %get-tuple-element.37.refs_0_, bf16[512,1024]{1,0:T(8,128)(2,1)} %get-tuple-element.38.refs_1_, bf16[32,64,768]{2,1,0:T(8,128)(2,1)} %copy-done, ...), custom_call_target="tpu_custom_call", output_to_operand_aliasing={{0}: (5, {}), {1}: (6, {})} | custom-call | flops 3221225472 | bytes 18874368 | tf_op jit(solution)/shard_map/update/pallas_call | solution.py:268
  172.4 4.2 %all-to-all-done.2 = bf16[32,16,1536]{2,1,0:T(8,128)(2,1)S(1)} async-done(((bf16[32,16,1536]{2,1,0:T(8,128)(2,1)}), bf16[32,16,1536]{2,1,0:T(8,128)(2,1)S(1)}, u32[]{:S(2)}, u32[]{:S(2)}) %all-to-all-start.2) | async-done | bytes 1572896 | tf_op jit(solution)/shard_map/all_to_all | solution.py:289
  177.8 2.7 %home_sum.1 = f32[128,768]{1,0:T(8,128)} custom-call(s32[4,128]{1,0:T(4,128)} %bitcast.29, bf16[512,1536]{1,0:T(8,128)(2,1)} %bitcast.26), custom_call_target="tpu_custom_call" | custom-call | tf_op jit(solution)/shard_map/home_sum/pallas_call | solution.py:355
  (51 shorter events, 20.1 us)
Async XLA Ops:
  3.2 8.7 %copy-start.5 = (bf16[136,768]{1,0:T(8,128)(2,1)S(1)}, bf16[136,768]{1,0:T(8,128)(2,1)}, u32[]{:S(2)}) copy-start(bf16[136,768]{1,0:T(8,128)(2,1)} %get-tuple-element.26.refs_0_) | copy-start | bytes 626692
  3.2 28.2 %all-to-all-start = ((bf16[32,16,896]{2,1,0:T(8,128)(2,1)}), bf16[32,16,896]{2,1,0:T(8,128)(2,1)S(1)}, u32[]{:S(2)}, u32[]{:S(2)}) async-start(bf16[32,16,896]{2,1,0:T(8,128)(2,1)} %bitcast.27), calls=%async_computation | async-start | bytes 1835008 | tf_op jit(solution)/shard_map/all_to_all | solution.py:289
  12.0 9.1 %collective-permute-start = (bf16[136,768]{1,0:T(8,128)(2,1)S(1)}, bf16[136,768]{1,0:T(8,128)(2,1)S(1)}, u32[]{:S(2)}, u32[]{:S(2)}) collective-permute-start(bf16[136,768]{1,0:T(8,128)(2,1)S(1)} %copy-done.5), channel_id=1, source_target_pairs={{0,1},{1,2},{2,3},{3,0},{4,5},{5,6},{6,7},{7,4},{8,9},{9,10},{10,1... | collective-permute-start | bytes 626696 | tf_op jit(solution)/shard_map/ppermute | solution.py:324
  13.7 7.4 %collective-permute-start.1 = (bf16[136,768]{1,0:T(8,128)(2,1)S(1)}, bf16[136,768]{1,0:T(8,128)(2,1)S(1)}, u32[]{:S(2)}, u32[]{:S(2)}) collective-permute-start(bf16[136,768]{1,0:T(8,128)(2,1)S(1)} %copy-done.5), channel_id=1, source_target_pairs={{0,3},{1,0},{2,1},{3,2},{4,7},{5,4},{6,5},{7,6},{8,11},{9,8},{10,9... | collective-permute-start | bytes 626696 | tf_op jit(solution)/shard_map/ppermute | solution.py:324
  15.9 10.6 %collective-permute-start.2 = (bf16[136,768]{1,0:T(8,128)(2,1)S(1)}, bf16[136,768]{1,0:T(8,128)(2,1)S(1)}, u32[]{:S(2)}, u32[]{:S(2)}) collective-permute-start(bf16[136,768]{1,0:T(8,128)(2,1)S(1)} %copy-done.5), channel_id=1, source_target_pairs={{0,2},{1,3},{2,0},{3,1},{4,6},{5,7},{6,4},{7,5},{8,10},{9,11},{10,... | collective-permute-start | bytes 626696 | tf_op jit(solution)/shard_map/ppermute | solution.py:324
  21.1 5.4 %copy-start.6 = (bf16[136,768]{1,0:T(8,128)(2,1)}, bf16[136,768]{1,0:T(8,128)(2,1)S(1)}, u32[]{:S(2)}) copy-start(bf16[136,768]{1,0:T(8,128)(2,1)S(1)} %collective-permute-done.refs_1_) | copy-start | bytes 626692
  21.1 5.4 %copy-start.7 = (bf16[136,768]{1,0:T(8,128)(2,1)}, bf16[136,768]{1,0:T(8,128)(2,1)S(1)}, u32[]{:S(2)}) copy-start(bf16[136,768]{1,0:T(8,128)(2,1)S(1)} %collective-permute-done.1.refs_2_) | copy-start | bytes 626692
  26.5 0.7 copy-start.8
  31.4 0.9 copy-start.1
  32.3 63.2 %all-to-all-start.1 = ((bf16[32,64,768]{2,1,0:T(8,128)(2,1)}), bf16[32,64,768]{2,1,0:T(8,128)(2,1)S(1)}, u32[]{:S(2)}, u32[]{:S(2)}) async-start(bf16[32,64,768]{2,1,0:T(8,128)(2,1)} %bitcast.21), calls=%async_computation.1 | async-start | bytes 6291456 | tf_op jit(solution)/shard_map/all_to_all | solution.py:289
  42.6 13.4 %collective-permute-start.5 = (bf16[256,896]{1,0:T(8,128)(2,1)}, bf16[256,896]{1,0:T(8,128)(2,1)}, u32[]{:S(2)}, u32[]{:S(2)}) collective-permute-start(bf16[256,896]{1,0:T(8,128)(2,1)} %get-tuple-element.52), channel_id=1, source_target_pairs={{0,1},{1,2},{2,3},{3,0},{4,5},{5,6},{6,7},{7,4},{8,9},{9,10},{10,1... | collective-permute-start | bytes 1376264 | tf_op jit(solution)/shard_map/ppermute | solution.py:335
  43.5 12.5 %collective-permute-start.4 = (bf16[256,896]{1,0:T(8,128)(2,1)}, bf16[256,896]{1,0:T(8,128)(2,1)}, u32[]{:S(2)}, u32[]{:S(2)}) collective-permute-start(bf16[256,896]{1,0:T(8,128)(2,1)} %get-tuple-element.51), channel_id=1, source_target_pairs={{0,3},{1,0},{2,1},{3,2},{4,7},{5,4},{6,5},{7,6},{8,11},{9,8},{10,9... | collective-permute-start | bytes 1376264 | tf_op jit(solution)/shard_map/ppermute | solution.py:336
  56.0 12.5 %collective-permute-start.6 = (bf16[256,896]{1,0:T(8,128)(2,1)}, bf16[256,896]{1,0:T(8,128)(2,1)}, u32[]{:S(2)}, u32[]{:S(2)}) collective-permute-start(bf16[256,896]{1,0:T(8,128)(2,1)} %collective-permute-done.5.refs_1_.refs_3_.refs_5_), channel_id=1, source_target_pairs={{0,1},{1,2},{2,3},{3,0},{4,5},{5,6},{6,7},{7,4},{8,9},{9,10},{10,1... | collective-permute-start | bytes 1376264 | tf_op jit(solution)/shard_map/ppermute | solution.py:339
  56.0 12.5 %collective-permute-start.7 = (bf16[256,896]{1,0:T(8,128)(2,1)}, bf16[256,896]{1,0:T(8,128)(2,1)}, u32[]{:S(2)}, u32[]{:S(2)}) collective-permute-start(bf16[256,896]{1,0:T(8,128)(2,1)} %collective-permute-done.4.refs_2_.refs_6_.refs_8_), channel_id=1, source_target_pairs={{0,3},{1,0},{2,1},{3,2},{4,7},{5,4},{6,5},{7,6},{8,11},{9,8},{10,9... | collective-permute-start | bytes 1376264 | tf_op jit(solution)/shard_map/ppermute | solution.py:340
  58.7 19.7 %collective-permute-start.10 = (bf16[256,896]{1,0:T(8,128)(2,1)}, bf16[256,896]{1,0:T(8,128)(2,1)}, u32[]{:S(2)}, u32[]{:S(2)}) collective-permute-start(bf16[256,896]{1,0:T(8,128)(2,1)} %get-tuple-element.51), channel_id=1, source_target_pairs={{0,1},{1,2},{2,3},{3,0},{4,5},{5,6},{6,7},{7,4},{8,9},{9,10},{10,1... | collective-permute-start | bytes 1376264 | tf_op jit(solution)/shard_map/ppermute | solution.py:337
  58.7 24.2 %collective-permute-start.3 = (bf16[256,896]{1,0:T(8,128)(2,1)}, bf16[256,896]{1,0:T(8,128)(2,1)}, u32[]{:S(2)}, u32[]{:S(2)}) collective-permute-start(bf16[256,896]{1,0:T(8,128)(2,1)} %get-tuple-element.52), channel_id=1, source_target_pairs={{0,3},{1,0},{2,1},{3,2},{4,7},{5,4},{6,5},{7,6},{8,11},{9,8},{10,9... | collective-permute-start | bytes 1376264 | tf_op jit(solution)/shard_map/ppermute | solution.py:338
  72.9 16.7 %collective-permute-start.11 = (bf16[256,768]{1,0:T(8,128)(2,1)}, bf16[256,768]{1,0:T(8,128)(2,1)}, u32[]{:S(2)}, u32[]{:S(2)}) collective-permute-start(bf16[256,768]{1,0:T(8,128)(2,1)} %get-tuple-element.32), channel_id=1, source_target_pairs={{0,3},{1,0},{2,1},{3,2},{4,7},{5,4},{6,5},{7,6},{8,11},{9,8},{10,9... | collective-permute-start | bytes 1179656 | tf_op jit(solution)/shard_map/ppermute | solution.py:303
  82.9 11.6 %collective-permute-start.8 = (bf16[256,768]{1,0:T(8,128)(2,1)}, bf16[256,768]{1,0:T(8,128)(2,1)S(1)}, u32[]{:S(2)}, u32[]{:S(2)}) collective-permute-start(bf16[256,768]{1,0:T(8,128)(2,1)} %get-tuple-element.30), channel_id=1, source_target_pairs={{0,1},{1,2},{2,3},{3,0},{4,5},{5,6},{6,7},{7,4},{8,9},{9,10},{10,1... | collective-permute-start | bytes 1179656 | tf_op jit(solution)/shard_map/ppermute | solution.py:302
  87.5 2.1 %copy-start.4 = (bf16[512,768]{1,0:T(8,128)(2,1)S(1)}, bf16[512,768]{1,0:T(8,128)(2,1)}, u32[]{:S(2)}) copy-start(bf16[512,768]{1,0:T(8,128)(2,1)} %get-tuple-element.31) | copy-start | bytes 2359300
  89.6 4.8 %copy-start.3 = (bf16[512,768]{1,0:T(8,128)(2,1)S(1)}, bf16[512,768]{1,0:T(8,128)(2,1)}, u32[]{:S(2)}) copy-start(bf16[512,768]{1,0:T(8,128)(2,1)} %get-tuple-element.29) | copy-start | bytes 2359300
  91.8 37.7 %collective-permute-start.12 = (bf16[512,768]{1,0:T(8,128)(2,1)}, bf16[512,768]{1,0:T(8,128)(2,1)}, u32[]{:S(2)}, u32[]{:S(2)}) collective-permute-start(bf16[512,768]{1,0:T(8,128)(2,1)} %pad_maximum_fusion.2), channel_id=1, source_target_pairs={{0,3},{1,0},{2,1},{3,2},{4,7},{5,4},{6,5},{7,6},{8,11},{9,8},{10,9... | collective-permute-start | bytes 2359304 | tf_op jit(solution)/shard_map/ppermute | solution.py:307
  95.5 34.0 %collective-permute-start.9 = (bf16[512,768]{1,0:T(8,128)(2,1)}, bf16[512,768]{1,0:T(8,128)(2,1)}, u32[]{:S(2)}, u32[]{:S(2)}) collective-permute-start(bf16[512,768]{1,0:T(8,128)(2,1)} %pad_maximum_fusion.1), channel_id=1, source_target_pairs={{0,1},{1,2},{2,3},{3,0},{4,5},{5,6},{6,7},{7,4},{8,9},{9,10},{10,1... | collective-permute-start | bytes 2359304 | tf_op jit(solution)/shard_map/ppermute | solution.py:306
  95.5 1.6 copy-start
  102.3 19.7 %collective-permute-start.13 = (bf16[256,768]{1,0:T(8,128)(2,1)}, bf16[256,768]{1,0:T(8,128)(2,1)S(1)}, u32[]{:S(2)}, u32[]{:S(2)}) collective-permute-start(bf16[256,768]{1,0:T(8,128)(2,1)} %get-tuple-element.35), channel_id=1, source_target_pairs={{0,1},{1,2},{2,3},{3,0},{4,5},{5,6},{6,7},{7,4},{8,9},{9,10},{10,1... | collective-permute-start | bytes 1179656 | tf_op jit(solution)/shard_map/ppermute | solution.py:302
  102.3 19.7 %collective-permute-start.15 = (bf16[256,768]{1,0:T(8,128)(2,1)}, bf16[256,768]{1,0:T(8,128)(2,1)S(1)}, u32[]{:S(2)}, u32[]{:S(2)}) collective-permute-start(bf16[256,768]{1,0:T(8,128)(2,1)} %get-tuple-element.36), channel_id=1, source_target_pairs={{0,3},{1,0},{2,1},{3,2},{4,7},{5,4},{6,5},{7,6},{8,11},{9,8},{10,9... | collective-permute-start | bytes 1179656 | tf_op jit(solution)/shard_map/ppermute | solution.py:303
  123.3 15.8 %collective-permute-start.16 = (bf16[512,768]{1,0:T(8,128)(2,1)S(1)}, bf16[512,768]{1,0:T(8,128)(2,1)S(1)}, u32[]{:S(2)}, u32[]{:S(2)}) collective-permute-start(bf16[512,768]{1,0:T(8,128)(2,1)S(1)} %pad_maximum_fusion.4), channel_id=1, source_target_pairs={{0,3},{1,0},{2,1},{3,2},{4,7},{5,4},{6,5},{7,6},{8,11},{9,8},{10,9... | collective-permute-start | bytes 2359304 | tf_op jit(solution)/shard_map/ppermute | solution.py:307
  123.5 17.0 %collective-permute-start.14 = (bf16[512,768]{1,0:T(8,128)(2,1)S(1)}, bf16[512,768]{1,0:T(8,128)(2,1)S(1)}, u32[]{:S(2)}, u32[]{:S(2)}) collective-permute-start(bf16[512,768]{1,0:T(8,128)(2,1)S(1)} %pad_maximum_fusion.3), channel_id=1, source_target_pairs={{0,1},{1,2},{2,3},{3,0},{4,5},{5,6},{6,7},{7,4},{8,9},{9,10},{10,1... | collective-permute-start | bytes 2359304 | tf_op jit(solution)/shard_map/ppermute | solution.py:306
  143.2 33.4 %all-to-all-start.2 = ((bf16[32,16,1536]{2,1,0:T(8,128)(2,1)}), bf16[32,16,1536]{2,1,0:T(8,128)(2,1)S(1)}, u32[]{:S(2)}, u32[]{:S(2)}) async-start(bf16[32,16,1536]{2,1,0:T(8,128)(2,1)} %bitcast.11), calls=%async_computation.2 | async-start | bytes 3145728 | tf_op jit(solution)/shard_map/all_to_all | solution.py:289
  176.6 1.2 copy-start.2

commit v7 on v6

--- a/solution.py
+++ b/solution.py
@@ -97,15 +97,14 @@
         box_ref[:, k] = filled.astype(jnp.bfloat16).reshape(CLUS, CAP, D)
 
 
-def home_kernel(visits_ref, homed_ref, out_ref):
-    total = jnp.zeros((NQ, D), jnp.float32)
-    for parity in range(2):
-        chosen = as_bf16(picks(visits_ref[...], parity))
-        rows = homed_ref[:, parity * D : (parity + 1) * D]
-        total = total + lax.dot_general(
-            chosen, rows, (((0,), (0,)), ((), ())), preferred_element_type=jnp.float32
-        )
-    out_ref[...] = total
+def home_kernel(parity, visits_ref, homed_ref, *refs):
+    chosen = as_bf16(picks(visits_ref[...], parity))
+    total = lax.dot_general(
+        chosen, homed_ref[...], (((0,), (0,)), ((), ())), preferred_element_type=jnp.float32
+    )
+    for before_ref in refs[:-1]:
+        total = total + before_ref[...]
+    refs[-1][...] = total
 
 
 def tile_grads(rows, high, low, first, w_ref):
@@ -328,7 +327,6 @@
         out_shape=jax.ShapeDtypeStruct((CLUS, LAB, CAP, D), bf),
         name="all_box",
     )(*peers)
-    got_a, box_b = lax.optimization_barrier((got_a, box_b))
     got_b = swap(box_b.reshape(CLUS, LAB * CAP, D))
 
     half = ROWS // 2
@@ -348,13 +346,18 @@
     grad_far, *far_b_parts = second_grads(lab, got_b, blocks[3:], weights, near=False)
     grad_near, parts_near = second_grads(lab, got_b, blocks[:3], weights, near=True)
     home_b = ring_sum([parts_near[0], parts_near[1], parts_near[2]] + far_b_parts)
-    both = jnp.concatenate([home_a, home_b], axis=1).reshape(CLUS, CAP, 2 * D)
-    both = swap(both).reshape(ROWS, 2 * D)
+    home_a = swap(home_a.reshape(CLUS, CAP, D)).reshape(ROWS, D)
+    home_b = swap(home_b.reshape(CLUS, CAP, D)).reshape(ROWS, D)
     new = update(0, grads_a, blocks, weights, momentum)
     new = update(1, (grad_near, grad_far), got_b, weights, momentum, new)
-    query_grad = pl.pallas_call(
-        home_kernel, out_shape=jax.ShapeDtypeStruct((NQ, D), jnp.float32), name="home_sum"
-    )(vt, both)
+    total = ()
+    for parity, homed in enumerate((home_a, home_b)):
+        query_grad = pl.pallas_call(
+            lambda *refs, parity=parity: home_kernel(parity, *refs),
+            out_shape=jax.ShapeDtypeStruct((NQ, D), jnp.float32),
+            name="home_sum",
+        )(vt, homed, *total)
+        total = (query_grad,)
     return (query_grad, *new)
 
 

time: 181 us -> 186 us (1.028)
  starting transfers between devices: 50.1 us -> 53.9 us
  Pallas kernels: 61.1 us -> 63.1 us
    ppermute x2, waiting for transfers between devices: 7.69 us -> 0.01 us  [ring_sum(): down = lax.ppermute(down, 'lab', ring(-1))]
    all_to_all x3 -> x4, waiting for transfers between devices: 4.22 us -> 11.6 us  [swap(): return lax.all_to_all(x, 'clus', split_axis=0, concat_axis=0, tiled=True)]
    all_to_all x3 -> x4, starting transfers between devices: 27.5 us -> 31.3 us  [swap(): return lax.all_to_all(x, 'clus', split_axis=0, concat_axis=0, tiled=True)]
    pallas_call x1 -> x2, Pallas kernels: 2.71 us -> 4.79 us  [step(): pl.pallas_call(lambda *refs, parity=parity: home_kernel(parity, *refs), o...]
    convert_element_type x5, other arithmetic: 5.87 us -> 7.91 us  [add(): return total.astype(jnp.bfloat16)]
    unnamed x18 -> x20, local copies, waits for them, and re-layouts: 4.45 us -> 4.21 us
  transfers between devices with their start and end apart: 20 -> 21, of which waited for: 9 -> 7; matrix products, arithmetic and copies ran while one was open for 7% -> 8% of each run, Pallas kernels for 31% -> 31%
where the time goes in v7:
time: 186 us; the launch traced here: 185 us
  Pallas kernels  63.1 us (34%)
  starting transfers between devices  53.9 us (29%)
  waiting for transfers between devices  47.8 us (26%)
  other arithmetic  9.88 us (5%)
  local copies, waits for them, and re-layouts  9.69 us (5%)
    all_to_all x4, starting transfers between devices, swap(): return lax.all_to_all(x, 'clus', split_axis=0, concat_axis=0, tiled=True)  31.3 us
    pallas_call x2, Pallas kernels, update(): pl.pallas_call(lambda *refs: update_kernel(counts, *refs), grid=(bands,),...  18.4 us
    pallas_call x4, Pallas kernels, first_grads(): pl.pallas_call(lambda *refs: first_kernel(count, *refs), grid=(1,), in_sp...  18.1 us
    pallas_call x2, Pallas kernels, second_grads(): pl.pallas_call(lambda *refs: second_kernel(near, *refs), grid=(count, 2),...  14.9 us
    all_to_all x4, waiting for transfers between devices, swap(): return lax.all_to_all(x, 'clus', split_axis=0, concat_axis=0, tiled=True)  11.6 us
    ppermute x1, waiting for transfers between devices, step(): low_a = lax.ppermute(got_a[:half], 'lab', ring(1))  10.7 us
    ppermute x3, waiting for transfers between devices, step(): peers = [raw] + [lax.ppermute(raw, 'lab', ring(s)) for s in (1, -1, 2)]  9.37 us
    convert_element_type x5, other arithmetic, add(): return total.astype(jnp.bfloat16)  7.91 us
  transfers between devices with their start and end apart: 21, of which 7 were waited for; matrix products, arithmetic and copies ran while one was open for 8% of the time, Pallas kernels for 31%

profile of v7, /device:TPU:1, one launch (start us, length us, event | category | flops | bytes accessed | tf_op | source)
XLA Modules:
  0.0 185.2 jit_solution(6044188266279803408)
XLA Ops:
  0.6 2.6 %own_box.1 = (bf16[512,896]{1,0:T(8,128)(2,1)}, bf16[136,768]{1,0:T(8,128)(2,1)}) custom-call(s32[4,128]{1,0:T(4,128)} %bitcast.32, s32[4,128]{1,0:T(4,128)} %bitcast.35, bf16[128,768]{1,0:T(8,128)(2,1)} %queries_ref.1), custom_call_target="tpu_custom_call" | custom-call | tf_op jit(solution)/shard_map/own_box/pallas_call | solution.py:315
  3.2 8.7 %all-to-all-start.1 = ((bf16[32,16,896]{2,1,0:T(8,128)(2,1)}), bf16[32,16,896]{2,1,0:T(8,128)(2,1)S(1)}, u32[]{:S(2)}, u32[]{:S(2)}) async-start(bf16[32,16,896]{2,1,0:T(8,128)(2,1)} %bitcast.31), calls=%async_computation.1 | async-start | bytes 1835008 | tf_op jit(solution)/shard_map/all_to_all | solution.py:288
  13.7 2.2 %collective-permute-start.1 = (bf16[136,768]{1,0:T(8,128)(2,1)S(1)}, bf16[136,768]{1,0:T(8,128)(2,1)S(1)}, u32[]{:S(2)}, u32[]{:S(2)}) collective-permute-start(bf16[136,768]{1,0:T(8,128)(2,1)S(1)} %copy-done.6), channel_id=1, source_target_pairs={{0,3},{1,0},{2,1},{3,2},{4,7},{5,4},{6,5},{7,6},{8,11},{9,8},{10,9... | collective-permute-start | bytes 626696 | tf_op jit(solution)/shard_map/ppermute | solution.py:323
  17.1 4.0 %collective-permute-done.refs_1_ = bf16[136,768]{1,0:T(8,128)(2,1)S(1)} collective-permute-done((bf16[136,768]{1,0:T(8,128)(2,1)S(1)}, bf16[136,768]{1,0:T(8,128)(2,1)S(1)}, u32[]{:S(2)}, u32[]{:S(2)}) %collective-permute-start) | collective-permute-done | bytes 208928 | tf_op jit(solution)/shard_map/ppermute | solution.py:323
  21.1 5.4 %collective-permute-done.2.refs_3_ = bf16[136,768]{1,0:T(8,128)(2,1)S(1)} collective-permute-done((bf16[136,768]{1,0:T(8,128)(2,1)S(1)}, bf16[136,768]{1,0:T(8,128)(2,1)S(1)}, u32[]{:S(2)}, u32[]{:S(2)}) %collective-permute-start.2) | collective-permute-done | bytes 208928 | tf_op jit(solution)/shard_map/ppermute | solution.py:323
  27.2 4.2 %all_box.1 = bf16[32,4,16,768]{3,2,1,0:T(8,128)(2,1)} custom-call(bf16[136,768]{1,0:T(8,128)(2,1)} %get-tuple-element.23.refs_0_, bf16[136,768]{1,0:T(8,128)(2,1)} %copy-done.7, bf16[136,768]{1,0:T(8,128)(2,1)} %copy-done.8, bf16[136,768]{1,0:T(8,128)(2,1)} %copy-done.9), custom_call_target="tpu_custom_call" | custom-call | tf_op jit(solution)/shard_map/all_box/pallas_call | solution.py:325
  32.4 8.1 %all-to-all-start = ((bf16[32,64,768]{2,1,0:T(8,128)(2,1)}), bf16[32,64,768]{2,1,0:T(8,128)(2,1)S(1)}, u32[]{:S(2)}, u32[]{:S(2)}) async-start(bf16[32,64,768]{2,1,0:T(8,128)(2,1)} %bitcast.25), calls=%async_computation | async-start | bytes 6291456 | tf_op jit(solution)/shard_map/all_to_all | solution.py:288
  40.5 2.2 %fusion.4 = (bf16[16,16,896]{2,1,0:T(8,128)(2,1)}, bf16[16,16,896]{2,1,0:T(8,128)(2,1)}) fusion(bf16[32,16,896]{2,1,0:T(8,128)(2,1)} %copy-done.1), kind=kLoop, calls=%fused_computation.16 | loop fusion | bytes 1835008 | tf_op jit(solution)/shard_map/slice | solution.py:335
  45.3 10.7 %collective-permute-done.3.refs_3_.refs_1_.refs_5_ = bf16[256,896]{1,0:T(8,128)(2,1)} collective-permute-done((bf16[256,896]{1,0:T(8,128)(2,1)}, bf16[256,896]{1,0:T(8,128)(2,1)}, u32[]{:S(2)}, u32[]{:S(2)}) %collective-permute-start.3) | collective-permute-done | bytes 458784 | tf_op jit(solution)/shard_map/ppermute | solution.py:333
  56.0 2.7 %collective-permute-start.8 = (bf16[256,896]{1,0:T(8,128)(2,1)}, bf16[256,896]{1,0:T(8,128)(2,1)}, u32[]{:S(2)}, u32[]{:S(2)}) collective-permute-start(bf16[256,896]{1,0:T(8,128)(2,1)} %collective-permute-done.6.refs_6_.refs_2_.refs_8_), channel_id=1, source_target_pairs={{0,3},{1,0},{2,1},{3,2},{4,7},{5,4},{6,5},{7,6},{8,11},{9,8},{10,9... | collective-permute-start | bytes 1376264 | tf_op jit(solution)/shard_map/ppermute | solution.py:338
  58.7 2.7 %collective-permute-start.5 = (bf16[256,896]{1,0:T(8,128)(2,1)}, bf16[256,896]{1,0:T(8,128)(2,1)}, u32[]{:S(2)}, u32[]{:S(2)}) collective-permute-start(bf16[256,896]{1,0:T(8,128)(2,1)} %bitcast.6), channel_id=1, source_target_pairs={{0,3},{1,0},{2,1},{3,2},{4,7},{5,4},{6,5},{7,6},{8,11},{9,8},{10,9... | collective-permute-start | bytes 1376264 | tf_op jit(solution)/shard_map/ppermute | solution.py:336
  61.4 7.2 %collective-permute-done.7.refs_2_.refs_1_.refs_9_ = bf16[256,896]{1,0:T(8,128)(2,1)} collective-permute-done((bf16[256,896]{1,0:T(8,128)(2,1)}, bf16[256,896]{1,0:T(8,128)(2,1)}, u32[]{:S(2)}, u32[]{:S(2)}) %collective-permute-start.7) | collective-permute-done | bytes 458784 | tf_op jit(solution)/shard_map/ppermute | solution.py:337
  68.6 4.4 %first_grads.6 = (bf16[512,1024]{1,0:T(8,128)(2,1)}, bf16[256,768]{1,0:T(8,128)(2,1)}, bf16[256,768]{1,0:T(8,128)(2,1)}) custom-call(s32[1]{0:T(128)} %bitcast.1.refs_0_, bf16[256,896]{1,0:T(8,128)(2,1)} %collective-permute-done.7.refs_2_.refs_1_.refs_9_, bf16[256,896]{1,0:T(8,128)(2,1)} %collective-permute-done.8.refs_3_.refs_2_.refs_10_, ...), custom_call_target="tpu_custom_call" | custom-call | flops 1610612736 | bytes 3072000 | tf_op jit(solution)/shard_map/first_grads/pallas_call | solution.py:154
  73.0 2.4 %collective-permute-start.15 = (bf16[256,768]{1,0:T(8,128)(2,1)}, bf16[256,768]{1,0:T(8,128)(2,1)}, u32[]{:S(2)}, u32[]{:S(2)}) collective-permute-start(bf16[256,768]{1,0:T(8,128)(2,1)} %get-tuple-element.32), channel_id=1, source_target_pairs={{0,3},{1,0},{2,1},{3,2},{4,7},{5,4},{6,5},{7,6},{8,11},{9,8},{10,9... | collective-permute-start | bytes 1179656 | tf_op jit(solution)/shard_map/ppermute | solution.py:302
  75.4 3.0 %collective-permute-done.4.refs_4_.refs_2_.refs_6_ = bf16[256,896]{1,0:T(8,128)(2,1)} collective-permute-done((bf16[256,896]{1,0:T(8,128)(2,1)}, bf16[256,896]{1,0:T(8,128)(2,1)}, u32[]{:S(2)}, u32[]{:S(2)}) %collective-permute-start.4) | collective-permute-done | bytes 458784 | tf_op jit(solution)/shard_map/ppermute | solution.py:335
  78.4 4.6 %first_grads.7 = (bf16[512,1024]{1,0:T(8,128)(2,1)}, bf16[512,768]{1,0:T(8,128)(2,1)}) custom-call(s32[1]{0:T(128)} %bitcast.1.refs_0_, bf16[256,896]{1,0:T(8,128)(2,1)} %collective-permute-done.3.refs_3_.refs_1_.refs_5_, bf16[256,896]{1,0:T(8,128)(2,1)} %collective-permute-done.4.refs_4_.refs_2_.refs_6_, bf16[2,1024,768]{2,1,0:T(8,128)(2,1)} %refs_3_.7), custom_call_target="tpu_custom_call" | custom-call | flops 1610612736 | bytes 3072000 | tf_op jit(solution)/shard_map/first_grads/pallas_call | solution.py:154
  83.0 4.6 %first_grads.5 = (bf16[512,1024]{1,0:T(8,128)(2,1)}, bf16[512,768]{1,0:T(8,128)(2,1)}) custom-call(s32[1]{0:T(128)} %bitcast.1.refs_0_, bf16[256,896]{1,0:T(8,128)(2,1)} %collective-permute-done.5.refs_5_.refs_1_.refs_7_, bf16[256,896]{1,0:T(8,128)(2,1)} %collective-permute-done.6.refs_6_.refs_2_.refs_8_, bf16[2,1024,768]{2,1,0:T(8,128)(2,1)} %refs_3_.7), custom_call_target="tpu_custom_call" | custom-call | flops 1610612736 | bytes 3072000 | tf_op jit(solution)/shard_map/first_grads/pallas_call | solution.py:154
  91.8 2.7 %collective-permute-start.16 = (bf16[512,768]{1,0:T(8,128)(2,1)}, bf16[512,768]{1,0:T(8,128)(2,1)}, u32[]{:S(2)}, u32[]{:S(2)}) collective-permute-start(bf16[512,768]{1,0:T(8,128)(2,1)} %pad_maximum_fusion.3), channel_id=1, source_target_pairs={{0,3},{1,0},{2,1},{3,2},{4,7},{5,4},{6,5},{7,6},{8,11},{9,8},{10,9... | collective-permute-start | bytes 2359304 | tf_op jit(solution)/shard_map/ppermute | solution.py:306
  97.2 5.1 %second_grads.3 = (bf16[512,1024]{1,0:T(8,128)(2,1)}, bf16[256,768]{1,0:T(8,128)(2,1)}, bf16[256,768]{1,0:T(8,128)(2,1)}) custom-call(s32[1]{0:T(128)} %bitcast.1.refs_0_, bf16[32,64,768]{2,1,0:T(8,128)(2,1)} %copy-done, bf16[256,896]{1,0:T(8,128)(2,1)} %collective-permute-done.7.refs_2_.refs_1_.refs_9_, ...), custom_call_target="tpu_custom_call" | custom-call | flops 1610612736 | bytes 3072000 | tf_op jit(solution)/shard_map/second_grads/pallas_call | solution.py:210
  102.3 2.7 %collective-permute-start.11 = (bf16[256,768]{1,0:T(8,128)(2,1)}, bf16[256,768]{1,0:T(8,128)(2,1)S(1)}, u32[]{:S(2)}, u32[]{:S(2)}) collective-permute-start(bf16[256,768]{1,0:T(8,128)(2,1)} %get-tuple-element.27), channel_id=1, source_target_pairs={{0,3},{1,0},{2,1},{3,2},{4,7},{5,4},{6,5},{7,6},{8,11},{9,8},{10,9... | collective-permute-start | bytes 1179656 | tf_op jit(solution)/shard_map/ppermute | solution.py:302
  105.0 9.8 %second_grads.2 = (bf16[1536,1024]{1,0:T(8,128)(2,1)}, bf16[3,512,768]{2,1,0:T(8,128)(2,1)}) custom-call(s32[1]{0:T(128)} %bitcast.1.refs_0_, bf16[32,64,768]{2,1,0:T(8,128)(2,1)} %copy-done, bf16[512,896]{1,0:T(8,128)(2,1)} %bitcast.26, bf16[256,896]{1,0:T(8,128)(2,1)} %collective-permute-done.3.refs_3_.refs_1_.refs_5_, ...), custom_call_target="tpu_custom_call" | custom-call | flops 4831838208 | bytes 9216000 | tf_op jit(solution)/shard_map/second_grads/pallas_call | solution.py:210
  116.0 5.9 %collective-permute-done.9 = bf16[256,768]{1,0:T(8,128)(2,1)S(1)} collective-permute-done((bf16[256,768]{1,0:T(8,128)(2,1)}, bf16[256,768]{1,0:T(8,128)(2,1)S(1)}, u32[]{:S(2)}, u32[]{:S(2)}) %collective-permute-start.9) | collective-permute-done | bytes 393248 | tf_op jit(solution)/shard_map/ppermute | solution.py:301
  125.0 4.5 %first_grads.4 = (bf16[512,1024]{1,0:T(8,128)(2,1)}, bf16[512,768]{1,0:T(8,128)(2,1)}) custom-call(s32[1]{0:T(128)} %bitcast.1.refs_0_, bf16[512,896]{1,0:T(8,128)(2,1)} %bitcast.27, bf16[2,1024,768]{2,1,0:T(8,128)(2,1)} %refs_3_.7), custom_call_target="tpu_custom_call" | custom-call | flops 1610612736 | bytes 3072000 | tf_op jit(solution)/shard_map/first_grads/pallas_call | solution.py:154
  129.5 2.8 %add_convert_fusion = bf16[512,768]{1,0:T(8,128)(2,1)} fusion(bf16[512,768]{1,0:T(8,128)(2,1)} %collective-permute-done.16, bf16[512,768]{1,0:T(8,128)(2,1)} %collective-permute-done.14, bf16[512,768]{1,0:T(8,128)(2,1)} %get-tuple-element.28), kind=kLoop, calls=%fused_computation.3 | loop fusion | flops 2359296 | bytes 3145728 | tf_op jit(solution)/shard_map/convert_element_type | solution.py:295
  132.3 10.6 %all-to-all-start.3 = ((bf16[32,16,768]{2,1,0:T(8,128)(2,1)}), bf16[32,16,768]{2,1,0:T(8,128)(2,1)S(1)}, u32[]{:S(2)}, u32[]{:S(2)}) async-start(bf16[32,16,768]{2,1,0:T(8,128)(2,1)} %bitcast.15), calls=%async_computation.3 | async-start | bytes 1572864 | tf_op jit(solution)/shard_map/all_to_all | solution.py:288
  142.9 2.6 %fusion.1 = bf16[512,768]{1,0:T(8,128)(2,1)} fusion(bf16[512,768]{1,0:T(8,128)(2,1)S(1)} %collective-permute-done.12, bf16[512,768]{1,0:T(8,128)(2,1)} %collective-permute-done.10, bf16[3,512,768]{2,1,0:T(8,128)(2,1)} %get-tuple-element.25), kind=kLoop, calls=%fused_computation.2 | loop fusion | flops 2359296 | bytes 3145728 | tf_op jit(solution)/shard_map/convert_element_type | solution.py:295
  145.5 11.6 %all-to-all-done.3 = bf16[32,16,768]{2,1,0:T(8,128)(2,1)S(1)} async-done(((bf16[32,16,768]{2,1,0:T(8,128)(2,1)}), bf16[32,16,768]{2,1,0:T(8,128)(2,1)S(1)}, u32[]{:S(2)}, u32[]{:S(2)}) %all-to-all-start.3) | async-done | bytes 786464 | tf_op jit(solution)/shard_map/all_to_all | solution.py:288
  157.2 3.9 %all-to-all-start.2 = ((bf16[32,16,768]{2,1,0:T(8,128)(2,1)}), bf16[32,16,768]{2,1,0:T(8,128)(2,1)S(1)}, u32[]{:S(2)}, u32[]{:S(2)}) async-start(bf16[32,16,768]{2,1,0:T(8,128)(2,1)} %bitcast.13), calls=%async_computation.2 | async-start | bytes 1572864 | tf_op jit(solution)/shard_map/all_to_all | solution.py:288
  161.1 9.3 %update.2 = (bf16[2,1024,768]{2,1,0:T(8,128)(2,1)}, f32[2,1024,768]{2,1,0:T(8,128)}) custom-call(bf16[512,1024]{1,0:T(8,128)(2,1)} %get-tuple-element.35.refs_0_, bf16[512,1024]{1,0:T(8,128)(2,1)} %get-tuple-element.36.refs_1_, bf16[512,1024]{1,0:T(8,128)(2,1)} %get-tuple-element.37.refs_2_, bf16[512,1024]{1,0:T(8,128)(2,1)} %get-tuple-element.38.refs_3_, ...), custom_call_target="tpu_custom_call" | custom-call | flops 3221225472 | bytes 18874368 | tf_op jit(solution)/shard_map/update/pallas_call | solution.py:267
  170.4 9.1 %update.3 = (bf16[2,1024,768]{2,1,0:T(8,128)(2,1)}, f32[2,1024,768]{2,1,0:T(8,128)}) custom-call(bf16[1536,1024]{1,0:T(8,128)(2,1)} %get-tuple-element.33.refs_0_, bf16[512,1024]{1,0:T(8,128)(2,1)} %get-tuple-element.34.refs_1_, bf16[32,64,768]{2,1,0:T(8,128)(2,1)} %copy-done, ...), custom_call_target="tpu_custom_call", output_to_operand_aliasing={{0}: (5, {}), {1}: (6, {})} | custom-call | flops 3221225472 | bytes 18874368 | tf_op jit(solution)/shard_map/update/pallas_call | solution.py:267
  179.5 2.3 %home_sum.2.refs_2_ = f32[128,768]{1,0:T(8,128)} custom-call(s32[4,128]{1,0:T(4,128)} %bitcast.33, bf16[512,768]{1,0:T(8,128)(2,1)} %bitcast.29), custom_call_target="tpu_custom_call" | custom-call | tf_op jit(solution)/shard_map/home_sum/pallas_call | solution.py:355
  182.8 2.5 %home_sum.3 = f32[128,768]{1,0:T(8,128)} custom-call(s32[4,128]{1,0:T(4,128)} %bitcast.34, bf16[512,768]{1,0:T(8,128)(2,1)} %bitcast.30, f32[128,768]{1,0:T(8,128)} %home_sum.2.refs_2_), custom_call_target="tpu_custom_call" | custom-call | tf_op jit(solution)/shard_map/home_sum/pallas_call | solution.py:355
  (55 shorter events, 19.3 us)
Async XLA Ops:
  3.2 8.7 %copy-start.6 = (bf16[136,768]{1,0:T(8,128)(2,1)S(1)}, bf16[136,768]{1,0:T(8,128)(2,1)}, u32[]{:S(2)}) copy-start(bf16[136,768]{1,0:T(8,128)(2,1)} %get-tuple-element.23.refs_0_) | copy-start | bytes 626692
  3.2 28.2 %all-to-all-start.1 = ((bf16[32,16,896]{2,1,0:T(8,128)(2,1)}), bf16[32,16,896]{2,1,0:T(8,128)(2,1)S(1)}, u32[]{:S(2)}, u32[]{:S(2)}) async-start(bf16[32,16,896]{2,1,0:T(8,128)(2,1)} %bitcast.31), calls=%async_computation.1 | async-start | bytes 1835008 | tf_op jit(solution)/shard_map/all_to_all | solution.py:288
  12.0 9.1 %collective-permute-start = (bf16[136,768]{1,0:T(8,128)(2,1)S(1)}, bf16[136,768]{1,0:T(8,128)(2,1)S(1)}, u32[]{:S(2)}, u32[]{:S(2)}) collective-permute-start(bf16[136,768]{1,0:T(8,128)(2,1)S(1)} %copy-done.6), channel_id=1, source_target_pairs={{0,1},{1,2},{2,3},{3,0},{4,5},{5,6},{6,7},{7,4},{8,9},{9,10},{10,1... | collective-permute-start | bytes 626696 | tf_op jit(solution)/shard_map/ppermute | solution.py:323
  13.7 7.4 %collective-permute-start.1 = (bf16[136,768]{1,0:T(8,128)(2,1)S(1)}, bf16[136,768]{1,0:T(8,128)(2,1)S(1)}, u32[]{:S(2)}, u32[]{:S(2)}) collective-permute-start(bf16[136,768]{1,0:T(8,128)(2,1)S(1)} %copy-done.6), channel_id=1, source_target_pairs={{0,3},{1,0},{2,1},{3,2},{4,7},{5,4},{6,5},{7,6},{8,11},{9,8},{10,9... | collective-permute-start | bytes 626696 | tf_op jit(solution)/shard_map/ppermute | solution.py:323
  15.9 10.6 %collective-permute-start.2 = (bf16[136,768]{1,0:T(8,128)(2,1)S(1)}, bf16[136,768]{1,0:T(8,128)(2,1)S(1)}, u32[]{:S(2)}, u32[]{:S(2)}) collective-permute-start(bf16[136,768]{1,0:T(8,128)(2,1)S(1)} %copy-done.6), channel_id=1, source_target_pairs={{0,2},{1,3},{2,0},{3,1},{4,6},{5,7},{6,4},{7,5},{8,10},{9,11},{10,... | collective-permute-start | bytes 626696 | tf_op jit(solution)/shard_map/ppermute | solution.py:323
  21.1 5.4 %copy-start.7 = (bf16[136,768]{1,0:T(8,128)(2,1)}, bf16[136,768]{1,0:T(8,128)(2,1)S(1)}, u32[]{:S(2)}) copy-start(bf16[136,768]{1,0:T(8,128)(2,1)S(1)} %collective-permute-done.refs_1_) | copy-start | bytes 626692
  21.1 5.4 %copy-start.8 = (bf16[136,768]{1,0:T(8,128)(2,1)}, bf16[136,768]{1,0:T(8,128)(2,1)S(1)}, u32[]{:S(2)}) copy-start(bf16[136,768]{1,0:T(8,128)(2,1)S(1)} %collective-permute-done.1.refs_2_) | copy-start | bytes 626692
  26.5 0.7 copy-start.9
  31.4 1.0 copy-start.1
  32.4 63.1 %all-to-all-start = ((bf16[32,64,768]{2,1,0:T(8,128)(2,1)}), bf16[32,64,768]{2,1,0:T(8,128)(2,1)S(1)}, u32[]{:S(2)}, u32[]{:S(2)}) async-start(bf16[32,64,768]{2,1,0:T(8,128)(2,1)} %bitcast.25), calls=%async_computation | async-start | bytes 6291456 | tf_op jit(solution)/shard_map/all_to_all | solution.py:288
  42.7 13.4 %collective-permute-start.3 = (bf16[256,896]{1,0:T(8,128)(2,1)}, bf16[256,896]{1,0:T(8,128)(2,1)}, u32[]{:S(2)}, u32[]{:S(2)}) collective-permute-start(bf16[256,896]{1,0:T(8,128)(2,1)} %bitcast.6), channel_id=1, source_target_pairs={{0,1},{1,2},{2,3},{3,0},{4,5},{5,6},{6,7},{7,4},{8,9},{9,10},{10,1... | collective-permute-start | bytes 1376264 | tf_op jit(solution)/shard_map/ppermute | solution.py:333
  43.5 12.5 %collective-permute-start.6 = (bf16[256,896]{1,0:T(8,128)(2,1)}, bf16[256,896]{1,0:T(8,128)(2,1)}, u32[]{:S(2)}, u32[]{:S(2)}) collective-permute-start(bf16[256,896]{1,0:T(8,128)(2,1)} %bitcast.7), channel_id=1, source_target_pairs={{0,3},{1,0},{2,1},{3,2},{4,7},{5,4},{6,5},{7,6},{8,11},{9,8},{10,9... | collective-permute-start | bytes 1376264 | tf_op jit(solution)/shard_map/ppermute | solution.py:334
  56.0 12.5 %collective-permute-start.7 = (bf16[256,896]{1,0:T(8,128)(2,1)}, bf16[256,896]{1,0:T(8,128)(2,1)}, u32[]{:S(2)}, u32[]{:S(2)}) collective-permute-start(bf16[256,896]{1,0:T(8,128)(2,1)} %collective-permute-done.3.refs_3_.refs_1_.refs_5_), channel_id=1, source_target_pairs={{0,1},{1,2},{2,3},{3,0},{4,5},{5,6},{6,7},{7,4},{8,9},{9,10},{10,1... | collective-permute-start | bytes 1376264 | tf_op jit(solution)/shard_map/ppermute | solution.py:337
  56.0 12.5 %collective-permute-start.8 = (bf16[256,896]{1,0:T(8,128)(2,1)}, bf16[256,896]{1,0:T(8,128)(2,1)}, u32[]{:S(2)}, u32[]{:S(2)}) collective-permute-start(bf16[256,896]{1,0:T(8,128)(2,1)} %collective-permute-done.6.refs_6_.refs_2_.refs_8_), channel_id=1, source_target_pairs={{0,3},{1,0},{2,1},{3,2},{4,7},{5,4},{6,5},{7,6},{8,11},{9,8},{10,9... | collective-permute-start | bytes 1376264 | tf_op jit(solution)/shard_map/ppermute | solution.py:338
  58.7 19.7 %collective-permute-start.4 = (bf16[256,896]{1,0:T(8,128)(2,1)}, bf16[256,896]{1,0:T(8,128)(2,1)}, u32[]{:S(2)}, u32[]{:S(2)}) collective-permute-start(bf16[256,896]{1,0:T(8,128)(2,1)} %bitcast.7), channel_id=1, source_target_pairs={{0,1},{1,2},{2,3},{3,0},{4,5},{5,6},{6,7},{7,4},{8,9},{9,10},{10,1... | collective-permute-start | bytes 1376264 | tf_op jit(solution)/shard_map/ppermute | solution.py:335
  58.7 24.2 %collective-permute-start.5 = (bf16[256,896]{1,0:T(8,128)(2,1)}, bf16[256,896]{1,0:T(8,128)(2,1)}, u32[]{:S(2)}, u32[]{:S(2)}) collective-permute-start(bf16[256,896]{1,0:T(8,128)(2,1)} %bitcast.6), channel_id=1, source_target_pairs={{0,3},{1,0},{2,1},{3,2},{4,7},{5,4},{6,5},{7,6},{8,11},{9,8},{10,9... | collective-permute-start | bytes 1376264 | tf_op jit(solution)/shard_map/ppermute | solution.py:336
  73.0 16.7 %collective-permute-start.15 = (bf16[256,768]{1,0:T(8,128)(2,1)}, bf16[256,768]{1,0:T(8,128)(2,1)}, u32[]{:S(2)}, u32[]{:S(2)}) collective-permute-start(bf16[256,768]{1,0:T(8,128)(2,1)} %get-tuple-element.32), channel_id=1, source_target_pairs={{0,3},{1,0},{2,1},{3,2},{4,7},{5,4},{6,5},{7,6},{8,11},{9,8},{10,9... | collective-permute-start | bytes 1179656 | tf_op jit(solution)/shard_map/ppermute | solution.py:302
  82.9 11.5 %collective-permute-start.13 = (bf16[256,768]{1,0:T(8,128)(2,1)}, bf16[256,768]{1,0:T(8,128)(2,1)S(1)}, u32[]{:S(2)}, u32[]{:S(2)}) collective-permute-start(bf16[256,768]{1,0:T(8,128)(2,1)} %get-tuple-element.30), channel_id=1, source_target_pairs={{0,1},{1,2},{2,3},{3,0},{4,5},{5,6},{6,7},{7,4},{8,9},{9,10},{10,1... | collective-permute-start | bytes 1179656 | tf_op jit(solution)/shard_map/ppermute | solution.py:301
  87.5 2.1 %copy-start.5 = (bf16[512,768]{1,0:T(8,128)(2,1)S(1)}, bf16[512,768]{1,0:T(8,128)(2,1)}, u32[]{:S(2)}) copy-start(bf16[512,768]{1,0:T(8,128)(2,1)} %get-tuple-element.31) | copy-start | bytes 2359300
  89.7 4.8 %copy-start.4 = (bf16[512,768]{1,0:T(8,128)(2,1)S(1)}, bf16[512,768]{1,0:T(8,128)(2,1)}, u32[]{:S(2)}) copy-start(bf16[512,768]{1,0:T(8,128)(2,1)} %get-tuple-element.29) | copy-start | bytes 2359300
  91.8 37.7 %collective-permute-start.16 = (bf16[512,768]{1,0:T(8,128)(2,1)}, bf16[512,768]{1,0:T(8,128)(2,1)}, u32[]{:S(2)}, u32[]{:S(2)}) collective-permute-start(bf16[512,768]{1,0:T(8,128)(2,1)} %pad_maximum_fusion.3), channel_id=1, source_target_pairs={{0,3},{1,0},{2,1},{3,2},{4,7},{5,4},{6,5},{7,6},{8,11},{9,8},{10,9... | collective-permute-start | bytes 2359304 | tf_op jit(solution)/shard_map/ppermute | solution.py:306
  95.5 34.0 %collective-permute-start.14 = (bf16[512,768]{1,0:T(8,128)(2,1)}, bf16[512,768]{1,0:T(8,128)(2,1)}, u32[]{:S(2)}, u32[]{:S(2)}) collective-permute-start(bf16[512,768]{1,0:T(8,128)(2,1)} %pad_maximum_fusion.2), channel_id=1, source_target_pairs={{0,1},{1,2},{2,3},{3,0},{4,5},{5,6},{6,7},{7,4},{8,9},{9,10},{10,1... | collective-permute-start | bytes 2359304 | tf_op jit(solution)/shard_map/ppermute | solution.py:305
  95.5 1.6 copy-start
  102.3 19.7 %collective-permute-start.9 = (bf16[256,768]{1,0:T(8,128)(2,1)}, bf16[256,768]{1,0:T(8,128)(2,1)S(1)}, u32[]{:S(2)}, u32[]{:S(2)}) collective-permute-start(bf16[256,768]{1,0:T(8,128)(2,1)} %get-tuple-element.26), channel_id=1, source_target_pairs={{0,1},{1,2},{2,3},{3,0},{4,5},{5,6},{6,7},{7,4},{8,9},{9,10},{10,1... | collective-permute-start | bytes 1179656 | tf_op jit(solution)/shard_map/ppermute | solution.py:301
  102.3 19.7 %collective-permute-start.11 = (bf16[256,768]{1,0:T(8,128)(2,1)}, bf16[256,768]{1,0:T(8,128)(2,1)S(1)}, u32[]{:S(2)}, u32[]{:S(2)}) collective-permute-start(bf16[256,768]{1,0:T(8,128)(2,1)} %get-tuple-element.27), channel_id=1, source_target_pairs={{0,3},{1,0},{2,1},{3,2},{4,7},{5,4},{6,5},{7,6},{8,11},{9,8},{10,9... | collective-permute-start | bytes 1179656 | tf_op jit(solution)/shard_map/ppermute | solution.py:302
  123.3 19.6 %collective-permute-start.12 = (bf16[512,768]{1,0:T(8,128)(2,1)S(1)}, bf16[512,768]{1,0:T(8,128)(2,1)S(1)}, u32[]{:S(2)}, u32[]{:S(2)}) collective-permute-start(bf16[512,768]{1,0:T(8,128)(2,1)S(1)} %pad_maximum_fusion.1), channel_id=1, source_target_pairs={{0,3},{1,0},{2,1},{3,2},{4,7},{5,4},{6,5},{7,6},{8,11},{9,8},{10,9... | collective-permute-start | bytes 2359304 | tf_op jit(solution)/shard_map/ppermute | solution.py:306
  123.4 19.5 %collective-permute-start.10 = (bf16[512,768]{1,0:T(8,128)(2,1)S(1)}, bf16[512,768]{1,0:T(8,128)(2,1)}, u32[]{:S(2)}, u32[]{:S(2)}) collective-permute-start(bf16[512,768]{1,0:T(8,128)(2,1)S(1)} %pad_maximum_fusion), channel_id=1, source_target_pairs={{0,1},{1,2},{2,3},{3,0},{4,5},{5,6},{6,7},{7,4},{8,9},{9,10},{10,1... | collective-permute-start | bytes 2359304 | tf_op jit(solution)/shard_map/ppermute | solution.py:305
  132.3 24.9 %all-to-all-start.3 = ((bf16[32,16,768]{2,1,0:T(8,128)(2,1)}), bf16[32,16,768]{2,1,0:T(8,128)(2,1)S(1)}, u32[]{:S(2)}, u32[]{:S(2)}) async-start(bf16[32,16,768]{2,1,0:T(8,128)(2,1)} %bitcast.15), calls=%async_computation.3 | async-start | bytes 1572864 | tf_op jit(solution)/shard_map/all_to_all | solution.py:288
  157.2 13.3 %copy-start.2 = (bf16[32,16,768]{2,1,0:T(8,128)(2,1)}, bf16[32,16,768]{2,1,0:T(8,128)(2,1)S(1)}, u32[]{:S(2)}) copy-start(bf16[32,16,768]{2,1,0:T(8,128)(2,1)S(1)} %all-to-all-done.3) | copy-start | bytes 2359300
  157.2 24.7 %all-to-all-start.2 = ((bf16[32,16,768]{2,1,0:T(8,128)(2,1)}), bf16[32,16,768]{2,1,0:T(8,128)(2,1)S(1)}, u32[]{:S(2)}, u32[]{:S(2)}) async-start(bf16[32,16,768]{2,1,0:T(8,128)(2,1)} %bitcast.13), calls=%async_computation.2 | async-start | bytes 1572864 | tf_op jit(solution)/shard_map/all_to_all | solution.py:288
  181.9 0.9 copy-start.3

commit v8 on v7

--- a/solution.py
+++ b/solution.py
@@ -295,6 +295,19 @@
     return total.astype(jnp.bfloat16)
 
 
+def early_ring_sum(parts):
+    own, low, high, far_a, far_b = parts
+    half = ROWS // 2
+    up = lax.ppermute(far_a, "lab", ring(1))
+    down = lax.ppermute(far_b, "lab", ring(-1))
+    up_rest = lax.ppermute(high[half:], "lab", ring(1))
+    down_rest = lax.ppermute(low[:half], "lab", ring(-1))
+    up, down = add(high[:half], up), add(low[half:], down)
+    up = lax.ppermute(up, "lab", ring(1))
+    down = lax.ppermute(down, "lab", ring(-1))
+    return jnp.concatenate([add(own[:half], up, down_rest), add(own[half:], up_rest, down)])
+
+
 def ring_sum(parts):
     own, low, high, far_a, far_b = parts
     half = ROWS // 2
@@ -342,7 +355,7 @@
         grad, *parts = first_grads(lab, block, weights, apart=place == "far")
         grads_a.append(grad)
         parts_a += parts
-    home_a = ring_sum(parts_a)
+    home_a = early_ring_sum(parts_a)
     grad_far, *far_b_parts = second_grads(lab, got_b, blocks[3:], weights, near=False)
     grad_near, parts_near = second_grads(lab, got_b, blocks[:3], weights, near=True)
     home_b = ring_sum([parts_near[0], parts_near[1], parts_near[2]] + far_b_parts)

time: 186 us -> 193 us (1.038)
  starting transfers between devices: 53.9 us -> 59.9 us
    ppermute x0 -> x6, waiting for transfers between devices: none -> 6.42 us  [the longest x1 4.22 us: early_ring_sum(): down = lax.ppermute(far_b, 'lab', ring(-1))]
    all_to_all x4, starting transfers between devices: 31.3 us -> 37.7 us  [swap(): return lax.all_to_all(x, 'clus', split_axis=0, concat_axis=0, tiled=True)]
    ppermute x2 -> x1, waiting for transfers between devices: 5.94 us -> 0.01 us  [ring_sum(): up = lax.ppermute(far_a, 'lab', ring(1))]
    ppermute x0 -> x6, starting transfers between devices: none -> 4.78 us  [the longest x1 1.85 us: early_ring_sum(): down_rest = lax.ppermute(low[:half], 'lab', ring(-1))]
    ppermute x2 -> x1, starting transfers between devices: 5.15 us -> 2.44 us  [ring_sum(): down = lax.ppermute(far_b, 'lab', ring(-1))]
    ppermute x2 -> x1, starting transfers between devices: 2.74 us -> 0.15 us  [ring_sum(): down = lax.ppermute(down, 'lab', ring(-1))]
    slice x1 -> x2, local copies, waits for them, and re-layouts: 1.09 us -> 3.61 us  [the longest x1 1.86 us: early_ring_sum(): up_rest = lax.ppermute(high[half:], 'lab', ring(1))]
    ppermute x1, waiting for transfers between devices: 2.99 us -> 0.83 us  [step(): low_b = lax.ppermute(got_a[half:], 'lab', ring(1))]
  transfers between devices with their start and end apart: 21 -> 23, of which waited for: 7 -> 8; matrix products, arithmetic and copies ran while one was open for 8% -> 9% of each run, Pallas kernels for 31% -> 30%
where the time goes in v8:
time: 193 us; the launch traced here: 191 us
  Pallas kernels  63.1 us (33%)
  starting transfers between devices  59.9 us (31%)
  waiting for transfers between devices  46.1 us (24%)
  local copies, waits for them, and re-layouts  11.2 us (6%)
  other arithmetic  10.2 us (5%)
    all_to_all x4, starting transfers between devices, swap(): return lax.all_to_all(x, 'clus', split_axis=0, concat_axis=0, tiled=True)  37.7 us
    pallas_call x2, Pallas kernels, update(): pl.pallas_call(lambda *refs: update_kernel(counts, *refs), grid=(bands,),...  18.5 us
    pallas_call x4, Pallas kernels, first_grads(): pl.pallas_call(lambda *refs: first_kernel(count, *refs), grid=(1,), in_sp...  18.1 us
    pallas_call x2, Pallas kernels, second_grads(): pl.pallas_call(lambda *refs: second_kernel(near, *refs), grid=(count, 2),...  14.9 us
    all_to_all x4, waiting for transfers between devices, swap(): return lax.all_to_all(x, 'clus', split_axis=0, concat_axis=0, tiled=True)  11.7 us
    ppermute x1, waiting for transfers between devices, step(): low_a = lax.ppermute(got_a[:half], 'lab', ring(1))  10.7 us
    ppermute x3, waiting for transfers between devices, step(): peers = [raw] + [lax.ppermute(raw, 'lab', ring(s)) for s in (1, -1, 2)]  9.37 us
    convert_element_type x5, other arithmetic, add(): return total.astype(jnp.bfloat16)  9.14 us
  transfers between devices with their start and end apart: 23, of which 8 were waited for; matrix products, arithmetic and copies ran while one was open for 9% of the time, Pallas kernels for 30%

profile of v8, /device:TPU:1, one launch (start us, length us, event | category | flops | bytes accessed | tf_op | source)
XLA Modules:
  0.0 191.4 jit_solution(1062446630460796663)
XLA Ops:
  0.6 2.6 %own_box.1 = (bf16[512,896]{1,0:T(8,128)(2,1)}, bf16[136,768]{1,0:T(8,128)(2,1)}) custom-call(s32[4,128]{1,0:T(4,128)} %bitcast.32, s32[4,128]{1,0:T(4,128)} %bitcast.35, bf16[128,768]{1,0:T(8,128)(2,1)} %queries_ref.1), custom_call_target="tpu_custom_call" | custom-call | tf_op jit(solution)/shard_map/own_box/pallas_call | solution.py:328
  3.2 8.7 %all-to-all-start.1 = ((bf16[32,16,896]{2,1,0:T(8,128)(2,1)}), bf16[32,16,896]{2,1,0:T(8,128)(2,1)S(1)}, u32[]{:S(2)}, u32[]{:S(2)}) async-start(bf16[32,16,896]{2,1,0:T(8,128)(2,1)} %bitcast.31), calls=%async_computation.1 | async-start | bytes 1835008 | tf_op jit(solution)/shard_map/all_to_all | solution.py:288
  13.7 2.2 %collective-permute-start.1 = (bf16[136,768]{1,0:T(8,128)(2,1)S(1)}, bf16[136,768]{1,0:T(8,128)(2,1)S(1)}, u32[]{:S(2)}, u32[]{:S(2)}) collective-permute-start(bf16[136,768]{1,0:T(8,128)(2,1)S(1)} %copy-done.7), channel_id=1, source_target_pairs={{0,3},{1,0},{2,1},{3,2},{4,7},{5,4},{6,5},{7,6},{8,11},{9,8},{10,9... | collective-permute-start | bytes 626696 | tf_op jit(solution)/shard_map/ppermute | solution.py:336
  17.1 4.0 %collective-permute-done.refs_1_ = bf16[136,768]{1,0:T(8,128)(2,1)S(1)} collective-permute-done((bf16[136,768]{1,0:T(8,128)(2,1)S(1)}, bf16[136,768]{1,0:T(8,128)(2,1)S(1)}, u32[]{:S(2)}, u32[]{:S(2)}) %collective-permute-start) | collective-permute-done | bytes 208928 | tf_op jit(solution)/shard_map/ppermute | solution.py:336
  21.1 5.4 %collective-permute-done.2.refs_3_ = bf16[136,768]{1,0:T(8,128)(2,1)S(1)} collective-permute-done((bf16[136,768]{1,0:T(8,128)(2,1)S(1)}, bf16[136,768]{1,0:T(8,128)(2,1)S(1)}, u32[]{:S(2)}, u32[]{:S(2)}) %collective-permute-start.2) | collective-permute-done | bytes 208928 | tf_op jit(solution)/shard_map/ppermute | solution.py:336
  27.2 4.3 %all_box.1 = bf16[32,4,16,768]{3,2,1,0:T(8,128)(2,1)} custom-call(bf16[136,768]{1,0:T(8,128)(2,1)} %get-tuple-element.23.refs_0_, bf16[136,768]{1,0:T(8,128)(2,1)} %copy-done.8, bf16[136,768]{1,0:T(8,128)(2,1)} %copy-done.9, bf16[136,768]{1,0:T(8,128)(2,1)} %copy-done.10), custom_call_target="tpu_custom_call" | custom-call | tf_op jit(solution)/shard_map/all_box/pallas_call | solution.py:338
  32.4 8.1 %all-to-all-start = ((bf16[32,64,768]{2,1,0:T(8,128)(2,1)}), bf16[32,64,768]{2,1,0:T(8,128)(2,1)S(1)}, u32[]{:S(2)}, u32[]{:S(2)}) async-start(bf16[32,64,768]{2,1,0:T(8,128)(2,1)} %bitcast.25), calls=%async_computation | async-start | bytes 6291456 | tf_op jit(solution)/shard_map/all_to_all | solution.py:288
  40.5 2.2 %fusion.4 = (bf16[16,16,896]{2,1,0:T(8,128)(2,1)}, bf16[16,16,896]{2,1,0:T(8,128)(2,1)}) fusion(bf16[32,16,896]{2,1,0:T(8,128)(2,1)} %copy-done.1), kind=kLoop, calls=%fused_computation.16 | loop fusion | bytes 1835008 | tf_op jit(solution)/shard_map/slice | solution.py:348
  45.3 10.7 %collective-permute-done.3.refs_3_.refs_1_.refs_5_ = bf16[256,896]{1,0:T(8,128)(2,1)} collective-permute-done((bf16[256,896]{1,0:T(8,128)(2,1)}, bf16[256,896]{1,0:T(8,128)(2,1)}, u32[]{:S(2)}, u32[]{:S(2)}) %collective-permute-start.3) | collective-permute-done | bytes 458784 | tf_op jit(solution)/shard_map/ppermute | solution.py:346
  56.0 2.7 %collective-permute-start.8 = (bf16[256,896]{1,0:T(8,128)(2,1)}, bf16[256,896]{1,0:T(8,128)(2,1)}, u32[]{:S(2)}, u32[]{:S(2)}) collective-permute-start(bf16[256,896]{1,0:T(8,128)(2,1)} %collective-permute-done.6.refs_6_.refs_2_.refs_8_), channel_id=1, source_target_pairs={{0,3},{1,0},{2,1},{3,2},{4,7},{5,4},{6,5},{7,6},{8,11},{9,8},{10,9... | collective-permute-start | bytes 1376264 | tf_op jit(solution)/shard_map/ppermute | solution.py:351
  58.7 2.7 %collective-permute-start.5 = (bf16[256,896]{1,0:T(8,128)(2,1)}, bf16[256,896]{1,0:T(8,128)(2,1)}, u32[]{:S(2)}, u32[]{:S(2)}) collective-permute-start(bf16[256,896]{1,0:T(8,128)(2,1)} %bitcast.6), channel_id=1, source_target_pairs={{0,3},{1,0},{2,1},{3,2},{4,7},{5,4},{6,5},{7,6},{8,11},{9,8},{10,9... | collective-permute-start | bytes 1376264 | tf_op jit(solution)/shard_map/ppermute | solution.py:349
  61.4 7.2 %collective-permute-done.7.refs_2_.refs_1_.refs_9_ = bf16[256,896]{1,0:T(8,128)(2,1)} collective-permute-done((bf16[256,896]{1,0:T(8,128)(2,1)}, bf16[256,896]{1,0:T(8,128)(2,1)}, u32[]{:S(2)}, u32[]{:S(2)}) %collective-permute-start.7) | collective-permute-done | bytes 458784 | tf_op jit(solution)/shard_map/ppermute | solution.py:350
  68.5 4.4 %first_grads.6 = (bf16[512,1024]{1,0:T(8,128)(2,1)}, bf16[256,768]{1,0:T(8,128)(2,1)}, bf16[256,768]{1,0:T(8,128)(2,1)}) custom-call(s32[1]{0:T(128)} %bitcast.1.refs_0_, bf16[256,896]{1,0:T(8,128)(2,1)} %collective-permute-done.7.refs_2_.refs_1_.refs_9_, bf16[256,896]{1,0:T(8,128)(2,1)} %collective-permute-done.8.refs_3_.refs_2_.refs_10_, ...), custom_call_target="tpu_custom_call" | custom-call | flops 1610612736 | bytes 3072000 | tf_op jit(solution)/shard_map/first_grads/pallas_call | solution.py:154
  73.0 4.6 %first_grads.4 = (bf16[512,1024]{1,0:T(8,128)(2,1)}, bf16[512,768]{1,0:T(8,128)(2,1)}) custom-call(s32[1]{0:T(128)} %bitcast.1.refs_0_, bf16[512,896]{1,0:T(8,128)(2,1)} %bitcast.26, bf16[2,1024,768]{2,1,0:T(8,128)(2,1)} %refs_3_.7), custom_call_target="tpu_custom_call" | custom-call | flops 1610612736 | bytes 3072000 | tf_op jit(solution)/shard_map/first_grads/pallas_call | solution.py:154
  78.4 4.6 %first_grads.7 = (bf16[512,1024]{1,0:T(8,128)(2,1)}, bf16[512,768]{1,0:T(8,128)(2,1)}) custom-call(s32[1]{0:T(128)} %bitcast.1.refs_0_, bf16[256,896]{1,0:T(8,128)(2,1)} %collective-permute-done.3.refs_3_.refs_1_.refs_5_, bf16[256,896]{1,0:T(8,128)(2,1)} %collective-permute-done.4.refs_4_.refs_2_.refs_6_, bf16[2,1024,768]{2,1,0:T(8,128)(2,1)} %refs_3_.7), custom_call_target="tpu_custom_call" | custom-call | flops 1610612736 | bytes 3072000 | tf_op jit(solution)/shard_map/first_grads/pallas_call | solution.py:154
  87.7 4.5 %first_grads.5 = (bf16[512,1024]{1,0:T(8,128)(2,1)}, bf16[512,768]{1,0:T(8,128)(2,1)}) custom-call(s32[1]{0:T(128)} %bitcast.1.refs_0_, bf16[256,896]{1,0:T(8,128)(2,1)} %collective-permute-done.5.refs_5_.refs_1_.refs_7_, bf16[256,896]{1,0:T(8,128)(2,1)} %collective-permute-done.6.refs_6_.refs_2_.refs_8_, bf16[2,1024,768]{2,1,0:T(8,128)(2,1)} %refs_3_.7), custom_call_target="tpu_custom_call" | custom-call | flops 1610612736 | bytes 3072000 | tf_op jit(solution)/shard_map/first_grads/pallas_call | solution.py:154
  92.3 1.9 slice.76
  94.4 2.0 %add_convert_fusion.3 = bf16[256,768]{1,0:T(8,128)(2,1)} fusion(bf16[256,768]{1,0:T(8,128)(2,1)} %collective-permute-done.13, bf16[512,768]{1,0:T(8,128)(2,1)} %get-tuple-element.29), kind=kLoop, calls=%fused_computation.13 | loop fusion | flops 786432 | bytes 1179648 | tf_op jit(solution)/shard_map/convert_element_type | solution.py:295
  96.4 4.2 %collective-permute-done.17 = bf16[256,768]{1,0:T(8,128)(2,1)} collective-permute-done((bf16[256,768]{1,0:T(8,128)(2,1)}, bf16[256,768]{1,0:T(8,128)(2,1)}, u32[]{:S(2)}, u32[]{:S(2)}) %collective-permute-start.17) | collective-permute-done | bytes 393248 | tf_op jit(solution)/shard_map/ppermute | solution.py:302
  100.6 1.9 add_convert_fusion.1
  104.1 5.1 %second_grads.3 = (bf16[512,1024]{1,0:T(8,128)(2,1)}, bf16[256,768]{1,0:T(8,128)(2,1)}, bf16[256,768]{1,0:T(8,128)(2,1)}) custom-call(s32[1]{0:T(128)} %bitcast.1.refs_0_, bf16[32,64,768]{2,1,0:T(8,128)(2,1)} %copy-done, bf16[256,896]{1,0:T(8,128)(2,1)} %collective-permute-done.7.refs_2_.refs_1_.refs_9_, ...), custom_call_target="tpu_custom_call" | custom-call | flops 1610612736 | bytes 3072000 | tf_op jit(solution)/shard_map/second_grads/pallas_call | solution.py:210
  109.5 2.4 %collective-permute-start.11 = (bf16[256,768]{1,0:T(8,128)(2,1)}, bf16[256,768]{1,0:T(8,128)(2,1)S(1)}, u32[]{:S(2)}, u32[]{:S(2)}) collective-permute-start(bf16[256,768]{1,0:T(8,128)(2,1)} %get-tuple-element.27), channel_id=1, source_target_pairs={{0,3},{1,0},{2,1},{3,2},{4,7},{5,4},{6,5},{7,6},{8,11},{9,8},{10,9... | collective-permute-start | bytes 1179656 | tf_op jit(solution)/shard_map/ppermute | solution.py:315
  111.9 9.8 %second_grads.2 = (bf16[1536,1024]{1,0:T(8,128)(2,1)}, bf16[3,512,768]{2,1,0:T(8,128)(2,1)}) custom-call(s32[1]{0:T(128)} %bitcast.1.refs_0_, bf16[32,64,768]{2,1,0:T(8,128)(2,1)} %copy-done, bf16[512,896]{1,0:T(8,128)(2,1)} %bitcast.27, bf16[256,896]{1,0:T(8,128)(2,1)} %collective-permute-done.3.refs_3_.refs_1_.refs_5_, ...), custom_call_target="tpu_custom_call" | custom-call | flops 4831838208 | bytes 9216000 | tf_op jit(solution)/shard_map/second_grads/pallas_call | solution.py:210
  127.5 2.2 %collective-permute-done.18 = bf16[256,768]{1,0:T(8,128)(2,1)S(1)} collective-permute-done((bf16[256,768]{1,0:T(8,128)(2,1)S(1)}, bf16[256,768]{1,0:T(8,128)(2,1)S(1)}, u32[]{:S(2)}, u32[]{:S(2)}) %collective-permute-start.18) | collective-permute-done | bytes 393248 | tf_op jit(solution)/shard_map/ppermute | solution.py:307
  132.1 17.1 %all-to-all-start.3 = ((bf16[32,16,768]{2,1,0:T(8,128)(2,1)}), bf16[32,16,768]{2,1,0:T(8,128)(2,1)S(1)}, u32[]{:S(2)}, u32[]{:S(2)}) async-start(bf16[32,16,768]{2,1,0:T(8,128)(2,1)} %bitcast.15), calls=%async_computation.3 | async-start | bytes 1572864 | tf_op jit(solution)/shard_map/all_to_all | solution.py:288
  149.2 2.6 %fusion.1 = bf16[512,768]{1,0:T(8,128)(2,1)} fusion(bf16[512,768]{1,0:T(8,128)(2,1)S(1)} %collective-permute-done.12, bf16[512,768]{1,0:T(8,128)(2,1)} %collective-permute-done.10, bf16[3,512,768]{2,1,0:T(8,128)(2,1)} %get-tuple-element.25), kind=kLoop, calls=%fused_computation.2 | loop fusion | flops 2359296 | bytes 3145728 | tf_op jit(solution)/shard_map/convert_element_type | solution.py:295
  151.7 11.7 %all-to-all-done.3 = bf16[32,16,768]{2,1,0:T(8,128)(2,1)S(1)} async-done(((bf16[32,16,768]{2,1,0:T(8,128)(2,1)}), bf16[32,16,768]{2,1,0:T(8,128)(2,1)S(1)}, u32[]{:S(2)}, u32[]{:S(2)}) %all-to-all-start.3) | async-done | bytes 786464 | tf_op jit(solution)/shard_map/all_to_all | solution.py:288
  163.4 3.8 %all-to-all-start.2 = ((bf16[32,16,768]{2,1,0:T(8,128)(2,1)}), bf16[32,16,768]{2,1,0:T(8,128)(2,1)S(1)}, u32[]{:S(2)}, u32[]{:S(2)}) async-start(bf16[32,16,768]{2,1,0:T(8,128)(2,1)} %bitcast.13), calls=%async_computation.2 | async-start | bytes 1572864 | tf_op jit(solution)/shard_map/all_to_all | solution.py:288
  167.2 9.3 %update.2 = (bf16[2,1024,768]{2,1,0:T(8,128)(2,1)}, f32[2,1024,768]{2,1,0:T(8,128)}) custom-call(bf16[512,1024]{1,0:T(8,128)(2,1)} %get-tuple-element.35.refs_0_, bf16[512,1024]{1,0:T(8,128)(2,1)} %get-tuple-element.36.refs_1_, bf16[512,1024]{1,0:T(8,128)(2,1)} %get-tuple-element.37.refs_2_, bf16[512,1024]{1,0:T(8,128)(2,1)} %get-tuple-element.38.refs_3_, ...), custom_call_target="tpu_custom_call" | custom-call | flops 3221225472 | bytes 18874368 | tf_op jit(solution)/shard_map/update/pallas_call | solution.py:267
  176.6 9.1 %update.3 = (bf16[2,1024,768]{2,1,0:T(8,128)(2,1)}, f32[2,1024,768]{2,1,0:T(8,128)}) custom-call(bf16[1536,1024]{1,0:T(8,128)(2,1)} %get-tuple-element.33.refs_0_, bf16[512,1024]{1,0:T(8,128)(2,1)} %get-tuple-element.34.refs_1_, bf16[32,64,768]{2,1,0:T(8,128)(2,1)} %copy-done, ...), custom_call_target="tpu_custom_call", output_to_operand_aliasing={{0}: (5, {}), {1}: (6, {})} | custom-call | flops 3221225472 | bytes 18874368 | tf_op jit(solution)/shard_map/update/pallas_call | solution.py:267
  185.7 2.4 %home_sum.2.refs_2_ = f32[128,768]{1,0:T(8,128)} custom-call(s32[4,128]{1,0:T(4,128)} %bitcast.33, bf16[512,768]{1,0:T(8,128)(2,1)} %bitcast.29), custom_call_target="tpu_custom_call" | custom-call | tf_op jit(solution)/shard_map/home_sum/pallas_call | solution.py:368
  188.9 2.4 %home_sum.3 = f32[128,768]{1,0:T(8,128)} custom-call(s32[4,128]{1,0:T(4,128)} %bitcast.34, bf16[512,768]{1,0:T(8,128)(2,1)} %bitcast.30, f32[128,768]{1,0:T(8,128)} %home_sum.2.refs_2_), custom_call_target="tpu_custom_call" | custom-call | tf_op jit(solution)/shard_map/home_sum/pallas_call | solution.py:368
  (60 shorter events, 24.1 us)
Async XLA Ops:
  3.2 8.7 %copy-start.7 = (bf16[136,768]{1,0:T(8,128)(2,1)S(1)}, bf16[136,768]{1,0:T(8,128)(2,1)}, u32[]{:S(2)}) copy-start(bf16[136,768]{1,0:T(8,128)(2,1)} %get-tuple-element.23.refs_0_) | copy-start | bytes 626692
  3.2 28.2 %all-to-all-start.1 = ((bf16[32,16,896]{2,1,0:T(8,128)(2,1)}), bf16[32,16,896]{2,1,0:T(8,128)(2,1)S(1)}, u32[]{:S(2)}, u32[]{:S(2)}) async-start(bf16[32,16,896]{2,1,0:T(8,128)(2,1)} %bitcast.31), calls=%async_computation.1 | async-start | bytes 1835008 | tf_op jit(solution)/shard_map/all_to_all | solution.py:288
  12.0 9.1 %collective-permute-start = (bf16[136,768]{1,0:T(8,128)(2,1)S(1)}, bf16[136,768]{1,0:T(8,128)(2,1)S(1)}, u32[]{:S(2)}, u32[]{:S(2)}) collective-permute-start(bf16[136,768]{1,0:T(8,128)(2,1)S(1)} %copy-done.7), channel_id=1, source_target_pairs={{0,1},{1,2},{2,3},{3,0},{4,5},{5,6},{6,7},{7,4},{8,9},{9,10},{10,1... | collective-permute-start | bytes 626696 | tf_op jit(solution)/shard_map/ppermute | solution.py:336
  13.7 7.4 %collective-permute-start.1 = (bf16[136,768]{1,0:T(8,128)(2,1)S(1)}, bf16[136,768]{1,0:T(8,128)(2,1)S(1)}, u32[]{:S(2)}, u32[]{:S(2)}) collective-permute-start(bf16[136,768]{1,0:T(8,128)(2,1)S(1)} %copy-done.7), channel_id=1, source_target_pairs={{0,3},{1,0},{2,1},{3,2},{4,7},{5,4},{6,5},{7,6},{8,11},{9,8},{10,9... | collective-permute-start | bytes 626696 | tf_op jit(solution)/shard_map/ppermute | solution.py:336
  15.9 10.6 %collective-permute-start.2 = (bf16[136,768]{1,0:T(8,128)(2,1)S(1)}, bf16[136,768]{1,0:T(8,128)(2,1)S(1)}, u32[]{:S(2)}, u32[]{:S(2)}) collective-permute-start(bf16[136,768]{1,0:T(8,128)(2,1)S(1)} %copy-done.7), channel_id=1, source_target_pairs={{0,2},{1,3},{2,0},{3,1},{4,6},{5,7},{6,4},{7,5},{8,10},{9,11},{10,... | collective-permute-start | bytes 626696 | tf_op jit(solution)/shard_map/ppermute | solution.py:336
  21.1 5.4 %copy-start.8 = (bf16[136,768]{1,0:T(8,128)(2,1)}, bf16[136,768]{1,0:T(8,128)(2,1)S(1)}, u32[]{:S(2)}) copy-start(bf16[136,768]{1,0:T(8,128)(2,1)S(1)} %collective-permute-done.refs_1_) | copy-start | bytes 626692
  21.1 5.4 %copy-start.9 = (bf16[136,768]{1,0:T(8,128)(2,1)}, bf16[136,768]{1,0:T(8,128)(2,1)S(1)}, u32[]{:S(2)}) copy-start(bf16[136,768]{1,0:T(8,128)(2,1)S(1)} %collective-permute-done.1.refs_2_) | copy-start | bytes 626692
  31.4 1.0 copy-start.1
  32.4 70.1 %all-to-all-start = ((bf16[32,64,768]{2,1,0:T(8,128)(2,1)}), bf16[32,64,768]{2,1,0:T(8,128)(2,1)S(1)}, u32[]{:S(2)}, u32[]{:S(2)}) async-start(bf16[32,64,768]{2,1,0:T(8,128)(2,1)} %bitcast.25), calls=%async_computation | async-start | bytes 6291456 | tf_op jit(solution)/shard_map/all_to_all | solution.py:288
  42.6 13.4 %collective-permute-start.3 = (bf16[256,896]{1,0:T(8,128)(2,1)}, bf16[256,896]{1,0:T(8,128)(2,1)}, u32[]{:S(2)}, u32[]{:S(2)}) collective-permute-start(bf16[256,896]{1,0:T(8,128)(2,1)} %bitcast.6), channel_id=1, source_target_pairs={{0,1},{1,2},{2,3},{3,0},{4,5},{5,6},{6,7},{7,4},{8,9},{9,10},{10,1... | collective-permute-start | bytes 1376264 | tf_op jit(solution)/shard_map/ppermute | solution.py:346
  43.5 12.5 %collective-permute-start.6 = (bf16[256,896]{1,0:T(8,128)(2,1)}, bf16[256,896]{1,0:T(8,128)(2,1)}, u32[]{:S(2)}, u32[]{:S(2)}) collective-permute-start(bf16[256,896]{1,0:T(8,128)(2,1)} %bitcast.7), channel_id=1, source_target_pairs={{0,3},{1,0},{2,1},{3,2},{4,7},{5,4},{6,5},{7,6},{8,11},{9,8},{10,9... | collective-permute-start | bytes 1376264 | tf_op jit(solution)/shard_map/ppermute | solution.py:347
  56.0 12.5 %collective-permute-start.7 = (bf16[256,896]{1,0:T(8,128)(2,1)}, bf16[256,896]{1,0:T(8,128)(2,1)}, u32[]{:S(2)}, u32[]{:S(2)}) collective-permute-start(bf16[256,896]{1,0:T(8,128)(2,1)} %collective-permute-done.3.refs_3_.refs_1_.refs_5_), channel_id=1, source_target_pairs={{0,1},{1,2},{2,3},{3,0},{4,5},{5,6},{6,7},{7,4},{8,9},{9,10},{10,1... | collective-permute-start | bytes 1376264 | tf_op jit(solution)/shard_map/ppermute | solution.py:350
  56.0 12.5 %collective-permute-start.8 = (bf16[256,896]{1,0:T(8,128)(2,1)}, bf16[256,896]{1,0:T(8,128)(2,1)}, u32[]{:S(2)}, u32[]{:S(2)}) collective-permute-start(bf16[256,896]{1,0:T(8,128)(2,1)} %collective-permute-done.6.refs_6_.refs_2_.refs_8_), channel_id=1, source_target_pairs={{0,3},{1,0},{2,1},{3,2},{4,7},{5,4},{6,5},{7,6},{8,11},{9,8},{10,9... | collective-permute-start | bytes 1376264 | tf_op jit(solution)/shard_map/ppermute | solution.py:351
  58.7 19.7 %collective-permute-start.4 = (bf16[256,896]{1,0:T(8,128)(2,1)}, bf16[256,896]{1,0:T(8,128)(2,1)}, u32[]{:S(2)}, u32[]{:S(2)}) collective-permute-start(bf16[256,896]{1,0:T(8,128)(2,1)} %bitcast.7), channel_id=1, source_target_pairs={{0,1},{1,2},{2,3},{3,0},{4,5},{5,6},{6,7},{7,4},{8,9},{9,10},{10,1... | collective-permute-start | bytes 1376264 | tf_op jit(solution)/shard_map/ppermute | solution.py:348
  58.7 29.0 %collective-permute-start.5 = (bf16[256,896]{1,0:T(8,128)(2,1)}, bf16[256,896]{1,0:T(8,128)(2,1)}, u32[]{:S(2)}, u32[]{:S(2)}) collective-permute-start(bf16[256,896]{1,0:T(8,128)(2,1)} %bitcast.6), channel_id=1, source_target_pairs={{0,3},{1,0},{2,1},{3,2},{4,7},{5,4},{6,5},{7,6},{8,11},{9,8},{10,9... | collective-permute-start | bytes 1376264 | tf_op jit(solution)/shard_map/ppermute | solution.py:349
  72.9 21.4 %collective-permute-start.13 = (bf16[256,768]{1,0:T(8,128)(2,1)}, bf16[256,768]{1,0:T(8,128)(2,1)}, u32[]{:S(2)}, u32[]{:S(2)}) collective-permute-start(bf16[256,768]{1,0:T(8,128)(2,1)} %get-tuple-element.30), channel_id=1, source_target_pairs={{0,1},{1,2},{2,3},{3,0},{4,5},{5,6},{6,7},{7,4},{8,9},{9,10},{10,1... | collective-permute-start | bytes 1179656 | tf_op jit(solution)/shard_map/ppermute | solution.py:301
  84.7 41.4 %collective-permute-start.15 = (bf16[256,768]{1,0:T(8,128)(2,1)}, bf16[256,768]{1,0:T(8,128)(2,1)S(1)}, u32[]{:S(2)}, u32[]{:S(2)}) collective-permute-start(bf16[256,768]{1,0:T(8,128)(2,1)} %slice.74), channel_id=1, source_target_pairs={{0,3},{1,0},{2,1},{3,2},{4,7},{5,4},{6,5},{7,6},{8,11},{9,8},{10,9... | collective-permute-start | bytes 1179656 | tf_op jit(solution)/shard_map/ppermute | solution.py:304
  86.5 14.1 %collective-permute-start.17 = (bf16[256,768]{1,0:T(8,128)(2,1)}, bf16[256,768]{1,0:T(8,128)(2,1)}, u32[]{:S(2)}, u32[]{:S(2)}) collective-permute-start(bf16[256,768]{1,0:T(8,128)(2,1)} %get-tuple-element.32), channel_id=1, source_target_pairs={{0,3},{1,0},{2,1},{3,2},{4,7},{5,4},{6,5},{7,6},{8,11},{9,8},{10,9... | collective-permute-start | bytes 1179656 | tf_op jit(solution)/shard_map/ppermute | solution.py:302
  92.3 8.3 %copy-start.4 = (bf16[512,768]{1,0:T(8,128)(2,1)S(1)}, bf16[512,768]{1,0:T(8,128)(2,1)}, u32[]{:S(2)}) copy-start(bf16[512,768]{1,0:T(8,128)(2,1)} %get-tuple-element.31) | copy-start | bytes 2359300
  94.1 33.4 %collective-permute-start.16 = (bf16[256,768]{1,0:T(8,128)(2,1)}, bf16[256,768]{1,0:T(8,128)(2,1)}, u32[]{:S(2)}, u32[]{:S(2)}) collective-permute-start(bf16[256,768]{1,0:T(8,128)(2,1)} %slice.76), channel_id=1, source_target_pairs={{0,1},{1,2},{2,3},{3,0},{4,5},{5,6},{6,7},{7,4},{8,9},{9,10},{10,1... | collective-permute-start | bytes 1179656 | tf_op jit(solution)/shard_map/ppermute | solution.py:303
  96.4 31.2 %collective-permute-start.14 = (bf16[256,768]{1,0:T(8,128)(2,1)}, bf16[256,768]{1,0:T(8,128)(2,1)}, u32[]{:S(2)}, u32[]{:S(2)}) collective-permute-start(bf16[256,768]{1,0:T(8,128)(2,1)} %add_convert_fusion.3), channel_id=1, source_target_pairs={{0,1},{1,2},{2,3},{3,0},{4,5},{5,6},{6,7},{7,4},{8,9},{9,10},{10,1... | collective-permute-start | bytes 1179656 | tf_op jit(solution)/shard_map/ppermute | solution.py:306
  102.5 1.6 copy-start
  109.2 13.8 %collective-permute-start.9 = (bf16[256,768]{1,0:T(8,128)(2,1)}, bf16[256,768]{1,0:T(8,128)(2,1)S(1)}, u32[]{:S(2)}, u32[]{:S(2)}) collective-permute-start(bf16[256,768]{1,0:T(8,128)(2,1)} %get-tuple-element.26), channel_id=1, source_target_pairs={{0,1},{1,2},{2,3},{3,0},{4,5},{5,6},{6,7},{7,4},{8,9},{9,10},{10,1... | collective-permute-start | bytes 1179656 | tf_op jit(solution)/shard_map/ppermute | solution.py:314
  109.5 15.0 %collective-permute-start.11 = (bf16[256,768]{1,0:T(8,128)(2,1)}, bf16[256,768]{1,0:T(8,128)(2,1)S(1)}, u32[]{:S(2)}, u32[]{:S(2)}) collective-permute-start(bf16[256,768]{1,0:T(8,128)(2,1)} %get-tuple-element.27), channel_id=1, source_target_pairs={{0,3},{1,0},{2,1},{3,2},{4,7},{5,4},{6,5},{7,6},{8,11},{9,8},{10,9... | collective-permute-start | bytes 1179656 | tf_op jit(solution)/shard_map/ppermute | solution.py:315
  121.8 1.2 copy-start.6
  123.0 6.7 %collective-permute-start.18 = (bf16[256,768]{1,0:T(8,128)(2,1)S(1)}, bf16[256,768]{1,0:T(8,128)(2,1)S(1)}, u32[]{:S(2)}, u32[]{:S(2)}) collective-permute-start(bf16[256,768]{1,0:T(8,128)(2,1)S(1)} %copy-done.6), channel_id=1, source_target_pairs={{0,3},{1,0},{2,1},{3,2},{4,7},{5,4},{6,5},{7,6},{8,11},{9,8},{10,9... | collective-permute-start | bytes 1179656 | tf_op jit(solution)/shard_map/ppermute | solution.py:307
  125.8 3.9 %copy-start.5 = (bf16[512,768]{1,0:T(8,128)(2,1)S(1)}, bf16[512,768]{1,0:T(8,128)(2,1)}, u32[]{:S(2)}) copy-start(bf16[512,768]{1,0:T(8,128)(2,1)} %get-tuple-element.28) | copy-start | bytes 2359300
  125.8 23.3 %collective-permute-start.12 = (bf16[512,768]{1,0:T(8,128)(2,1)S(1)}, bf16[512,768]{1,0:T(8,128)(2,1)S(1)}, u32[]{:S(2)}, u32[]{:S(2)}) collective-permute-start(bf16[512,768]{1,0:T(8,128)(2,1)S(1)} %pad_maximum_fusion.1), channel_id=1, source_target_pairs={{0,3},{1,0},{2,1},{3,2},{4,7},{5,4},{6,5},{7,6},{8,11},{9,8},{10,9... | collective-permute-start | bytes 2359304 | tf_op jit(solution)/shard_map/ppermute | solution.py:319
  126.1 23.1 %collective-permute-start.10 = (bf16[512,768]{1,0:T(8,128)(2,1)S(1)}, bf16[512,768]{1,0:T(8,128)(2,1)}, u32[]{:S(2)}, u32[]{:S(2)}) collective-permute-start(bf16[512,768]{1,0:T(8,128)(2,1)S(1)} %pad_maximum_fusion), channel_id=1, source_target_pairs={{0,1},{1,2},{2,3},{3,0},{4,5},{5,6},{6,7},{7,4},{8,9},{9,10},{10,1... | collective-permute-start | bytes 2359304 | tf_op jit(solution)/shard_map/ppermute | solution.py:318
  132.1 31.3 %all-to-all-start.3 = ((bf16[32,16,768]{2,1,0:T(8,128)(2,1)}), bf16[32,16,768]{2,1,0:T(8,128)(2,1)S(1)}, u32[]{:S(2)}, u32[]{:S(2)}) async-start(bf16[32,16,768]{2,1,0:T(8,128)(2,1)} %bitcast.15), calls=%async_computation.3 | async-start | bytes 1572864 | tf_op jit(solution)/shard_map/all_to_all | solution.py:288
  163.4 13.2 %copy-start.2 = (bf16[32,16,768]{2,1,0:T(8,128)(2,1)}, bf16[32,16,768]{2,1,0:T(8,128)(2,1)S(1)}, u32[]{:S(2)}) copy-start(bf16[32,16,768]{2,1,0:T(8,128)(2,1)S(1)} %all-to-all-done.3) | copy-start | bytes 2359300
  163.4 24.6 %all-to-all-start.2 = ((bf16[32,16,768]{2,1,0:T(8,128)(2,1)}), bf16[32,16,768]{2,1,0:T(8,128)(2,1)S(1)}, u32[]{:S(2)}, u32[]{:S(2)}) async-start(bf16[32,16,768]{2,1,0:T(8,128)(2,1)} %bitcast.13), calls=%async_computation.2 | async-start | bytes 1572864 | tf_op jit(solution)/shard_map/all_to_all | solution.py:288
  (2 other events, 1.6 us)
